TPU v7x, 128 devices: a whole 4x4x4 slice. The times are simulated.
128 devices in a mesh: trow: 16 (over y, x), tcol: 8 (over z, core).
Axes of the slice: x: 4, y: 4, z: 4, core: 2. Of those that a mesh axis runs over, the one named last changes fastest.
Arguments:
- left_factors: bfloat16 [2, 2, 32768, 3072], P(None, None, 'trow', 'tcol'), may hold values from -0.109375 to 0.109375
- right_factors: bfloat16 [2, 2, 12288, 8192], P(None, None, 'tcol', 'trow'), may hold values from -0.375 to 0.375
- ranks: int32 [2, 128, 48], P(None, 'trow', 'tcol'), may hold values from 4 to 64, as said below
- v_current: float32 [2, 2, 12288, 128], P(None, None, ('tcol', 'trow')), may hold values from -32 to 32
- u_prev: float32 [2, 2, 32768, 128], P(None, None, ('trow', 'tcol')), may hold values from -32 to 32
- alpha_prev: float32 [1], replicated, may hold values from 0.5 to 2
Outputs:
- u_next: float32 [2, 2, 32768, 128], P(None, None, ('trow', 'tcol'))
- v_next: float32 [2, 2, 12288, 128], P(None, None, ('tcol', 'trow'))
- scales: float32 [2], replicated
Inputs may be any that keep to these rules, and one draw needn't show every extreme that they name: `ranks`: for frequency f, tile (i, j) has rank 64 // 2 + 1 to 64 where |i * 48 - j * 128| < 768, and rank 4 to 32 elsewhere.
All inputs are finite; a program needn't handle non-finite values.
Results may differ from a plain program's by a relative error of at most 0.0028.
Values may be sent and summed in bfloat16 or wider, within the bound.
No kernel may reach another device: no remote copies, remote signals or barrier semaphores. Data moves between devices by JAX's collectives and lax.ppermute only.
A program may use at most 128 MiB of HBM per device.

v0:
```python
import jax
import jax.numpy as jnp
from jax import lax
from jax.sharding import Mesh
from jax.sharding import PartitionSpec as P

TROW = ("trow_0", "trow_1")
TCOL = ("tcol_0", "tcol_1")
TROW_TCOL = ("trow_0", "trow_1", "tcol_0", "tcol_1")
TCOL_TROW = ("tcol_0", "tcol_1", "trow_0", "trow_1")


epsilon = 1e-06


def padded_to(lines, peers):
    spare = -len(lines) % peers
    return jnp.pad(lines, [(0, spare)] + [(0, 0)] * (lines.ndim - 1))


def total_of(value, axis):
    lines = value.reshape(-1, *value.shape[1:][-1:])
    padded = padded_to(lines, lax.axis_size(axis))
    own = lax.psum_scatter(padded, axis, scatter_dimension=0, tiled=True)
    whole = lax.all_gather(own, axis, axis=0, tiled=True)
    return whole[: len(lines)].reshape(value.shape)


def from_everyone(value, axis):
    copies = jnp.broadcast_to(value, (lax.axis_size(axis), *value.shape))
    return lax.all_to_all(copies, axis, split_axis=0, concat_axis=0, tiled=True)


def taken_together(value, axis):
    everything = from_everyone(value, axis)
    return jnp.sum(everything, axis=0)


def split_up(value, dim, peers):
    before, after = (value.shape[:dim], value.shape[dim + 1 :])
    return jnp.moveaxis(value.reshape(*before, peers, -1, *after), dim, 0)


def summed_on_arrival(value, axis, dim):
    pieces = split_up(value, dim, lax.axis_size(axis))
    arrived = lax.all_to_all(pieces, axis, split_axis=0, concat_axis=0, tiled=True)
    return arrived.sum(axis=0)


def over_axes(value, axes):
    for axis in axes:
        value = lax.psum(value, axis)
    return value


def complex_product(form, a_real, a_imag, b_real, b_imag, conjugate):
    real_real = jnp.einsum(form, a_real, b_real, preferred_element_type=jnp.float32)
    imag_imag = jnp.einsum(form, a_imag, b_imag, preferred_element_type=jnp.float32)
    real_imag = jnp.einsum(form, a_real, b_imag, preferred_element_type=jnp.float32)
    imag_real = jnp.einsum(form, a_imag, b_real, preferred_element_type=jnp.float32)
    if conjugate:
        return (real_real + imag_imag, real_imag - imag_real)
    return (real_real - imag_imag, real_imag + imag_real)


def tile_views(left_factors, right_factors, rank_mask):
    frequencies = left_factors.shape[0]
    columns = rank_mask.shape[1]
    row_tiles = rank_mask.shape[2]
    tile_rows = right_factors.shape[2] // columns
    right_tiles = right_factors.reshape(frequencies, 2, columns, tile_rows, row_tiles, -1)
    left_tiles = left_factors.reshape(frequencies, 2, row_tiles, tile_rows, columns, -1)
    weight = rank_mask[..., None]
    return (left_tiles, right_tiles, weight, tile_rows)


def forward_tiles(gathered, left_factors, right_factors, rank_mask):
    left_tiles, right_tiles, weight, tile_rows = tile_views(left_factors, right_factors, rank_mask)
    frequencies = gathered.shape[0]
    sources = gathered.reshape(frequencies, 2, rank_mask.shape[1], tile_rows, -1)
    proj_real, proj_imag = complex_product(
        "fcmir,fcmn->fcirn",
        right_tiles[:, 0],
        right_tiles[:, 1],
        sources[:, 0],
        sources[:, 1],
        True,
    )
    proj_real = (proj_real * weight).astype(jnp.bfloat16)
    proj_imag = (proj_imag * weight).astype(jnp.bfloat16)
    out_real, out_imag = complex_product(
        "fimcr,fcirn->fimn", left_tiles[:, 0], left_tiles[:, 1], proj_real, proj_imag, False
    )
    return jnp.stack([out_real, out_imag], 1).reshape(
        frequencies, 2, rank_mask.shape[2] * tile_rows, -1
    )


def adjoint_tiles(targets, left_factors, right_factors, rank_mask):
    left_tiles, right_tiles, weight, tile_rows = tile_views(left_factors, right_factors, rank_mask)
    frequencies = targets.shape[0]
    blocks = targets.reshape(frequencies, 2, rank_mask.shape[2], tile_rows, -1)
    back_real, back_imag = complex_product(
        "fimcr,fimn->fcirn", left_tiles[:, 0], left_tiles[:, 1], blocks[:, 0], blocks[:, 1], True
    )
    back_real = (back_real * weight).astype(jnp.bfloat16)
    back_imag = (back_imag * weight).astype(jnp.bfloat16)
    out_real, out_imag = complex_product(
        "fcmir,fcirn->fcmn", right_tiles[:, 0], right_tiles[:, 1], back_real, back_imag, False
    )
    return jnp.stack([out_real, out_imag], 1).reshape(
        frequencies, 2, rank_mask.shape[1] * tile_rows, -1
    )


def body(left_factors, right_factors, ranks, v_current, u_prev, alpha_prev):
    rank_full = left_factors.shape[3] // ranks.shape[2]
    rank_mask = (
        jnp.arange(rank_full)[None, None, None, :] < jnp.transpose(ranks, (0, 2, 1))[..., None]
    ).astype(jnp.float32)
    devices = lax.axis_size(TROW) * lax.axis_size(TCOL)
    gathered = lax.all_gather(v_current.astype(jnp.bfloat16), TROW, axis=2, tiled=True)
    partial_value = forward_tiles(gathered, left_factors, right_factors, rank_mask)
    share_rows = u_prev.shape[2]
    col_start = lax.axis_index(TCOL) * share_rows
    own_part = (
        lax.dynamic_slice_in_dim(partial_value, col_start, share_rows, 2) - alpha_prev[0] * u_prev
    )
    partial_value = lax.dynamic_update_slice_in_dim(partial_value, own_part, col_start, 2)
    count_u = u_prev.size * devices
    block_total = total_of(partial_value, TCOL)
    squares = taken_together(jnp.sum(block_total * block_total), TROW)
    beta_scale = jnp.sqrt(squares / count_u + epsilon)
    block_scaled = block_total / beta_scale
    u_next = lax.dynamic_slice_in_dim(block_scaled, col_start, share_rows, 2)
    targets = block_scaled.astype(jnp.bfloat16)
    partial_back = adjoint_tiles(targets, left_factors, right_factors, rank_mask)
    source_share = v_current.shape[2]
    row_start = lax.axis_index(TROW) * source_share
    own_back = (
        lax.dynamic_slice_in_dim(partial_back, row_start, source_share, 2) - beta_scale * v_current
    )
    partial_back = lax.dynamic_update_slice_in_dim(partial_back, own_back, row_start, 2)
    residual_v = summed_on_arrival(partial_back, TROW, 2)
    squares_v = over_axes(jnp.sum(residual_v * residual_v), TROW_TCOL)
    alpha_next = jnp.sqrt(squares_v / (v_current.size * devices) + epsilon)
    v_next = residual_v / alpha_next
    return (u_next, v_next, jnp.stack([beta_scale, alpha_next]))


def solution(mesh):
    finer = Mesh(mesh.devices.reshape(4, 4, 4, 2), ("trow_0", "trow_1", "tcol_0", "tcol_1"))
    placed = (
        P(None, None, TROW, TCOL),
        P(None, None, TCOL, TROW),
        P(None, TROW, TCOL),
        P(None, None, TCOL_TROW, None),
        P(None, None, TROW_TCOL, None),
        P(),
    )
    return jax.shard_map(
        body,
        mesh=finer,
        in_specs=placed,
        out_specs=(P(None, None, TROW_TCOL, None), P(None, None, TCOL_TROW, None), P()),
        check_vma=False,
    )
```

profile of v0, /device:TPU:1, one launch (start us, length us, event | category | flops | bytes accessed | tf_op | source)
XLA Modules:
  0.0 310.7 jit_solution(11976299568009127680)
XLA Ops:
  7.2 1.6 convert_element_type.29
  8.9 16.2 %reshape.72 = bf16[2,2,6,256,8,64]{5,4,3,2,1,0:T(8,128)(2,1)} reshape(bf16[2,2,1536,512]{3,2,1,0:T(8,128)(2,1)} %param.7) | data formatting | bytes 12582912 | tf_op jit(solution)/shard_map/reshape | solution.py:71
  25.1 11.0 %fusion.62 = (bf16[2,1,6,256,8,64]{5,4,3,2,1,0:T(8,128)(2,1)}, bf16[2,1,6,256,8,64]{5,4,3,2,1,0:T(8,128)(2,1)}) fusion(bf16[2,2,6,256,8,64]{5,4,3,2,1,0:T(8,128)(2,1)} %reshape.72), kind=kLoop, calls=%fused_computation.80 | loop fusion | bytes 12582912 | tf_op jit(solution)/shard_map/slice | solution.py:83
  36.1 5.8 %copy.168 = bf16[2,1,6,256,8,64]{3,5,4,2,0,1:T(8,128)(2,1)S(1)} copy(bf16[2,1,6,256,8,64]{5,4,3,2,1,0:T(8,128)(2,1)} %get-tuple-element.15) | data formatting | bytes 6291456
  42.0 7.1 %copy.167 = bf16[2,1,6,256,8,64]{3,5,4,2,0,1:T(8,128)(2,1)} copy(bf16[2,1,6,256,8,64]{5,4,3,2,1,0:T(8,128)(2,1)} %get-tuple-element.14) | data formatting | bytes 6291456
  49.1 8.7 %copy.129 = bf16[2,2,2048,384]{2,3,1,0:T(8,128)(2,1)} copy(bf16[2,2,2048,384]{3,2,1,0:T(8,128)(2,1)} %param.6) | data formatting | bytes 12582912 | tf_op args[0]
  57.8 8.2 %copy.173 = bf16[192,8,8,256]{3,2,1,0:T(8,128)(2,1)} copy(bf16[192,8,8,256]{3,1,2,0:T(8,128)(2,1)} %bitcast.163) | data formatting | bytes 12582912
  66.7 6.2 %fusion.63 = (bf16[2,1,8,256,6,64]{3,2,5,4,1,0:T(8,128)(2,1)}, bf16[2,1,8,256,6,64]{3,2,5,4,1,0:T(8,128)(2,1)}) fusion(bf16[2,2,8,256,6,64]{3,2,5,4,1,0:T(8,128)(2,1)} %bitcast.162), kind=kLoop, calls=%fused_computation.81 | loop fusion | bytes 12582912 | tf_op jit(solution)/shard_map/slice | solution.py:92
  72.8 1.5 copy.126
  74.3 1.0 fusion.16
  75.3 1.0 fusion.14
  77.2 1.2 multiply_convert_fusion.1
  78.5 1.4 multiply_convert_fusion
  79.9 1.0 copy-done.5
  80.9 1.2 fusion.2
  82.1 2.5 fusion.4
  84.6 2.6 fusion.26
  87.2 2.9 copy.137
  90.1 5.6 %fusion.27 = f32[2,8,256,128]{2,3,1,0:T(8,128)} fusion(f32[2,8,128,256,1]{3,2,4,1,0:T(8,128)} %fusion.4, bf16[2,6,8,64,128]{4,3,2,1,0:T(8,128)(2,1)} %copy-done.12, bf16[2,1,8,256,6,64]{3,2,5,4,1,0:T(8,128)(2,1)} %get-tuple-element.16), kind=kOutput, calls=%fused_computation.43 | convolution fusion | flops 403177472 | bytes 8912896 | tf_op jit(solution)/shard_map/fimcr,fcirn->fimn/dot_general | solution.py:57
  95.7 2.9 copy.134
  98.6 2.7 pad_maximum_fusion
  102.3 2.2 copy.139
  104.5 38.6 %reduce-scatter.2.cloned.1.call-done = f32[1024,128]{1,0:T(8,128)} async-done(((f32[8192,128]{1,0:T(8,128)}), f32[1024,128]{1,0:T(8,128)}) %reduce-scatter.2.cloned.1.call-update) | async-done | bytes 524304 | tf_op jit(solution)/shard_map/reduce_scatter | solution.py:24
  143.2 4.4 %copy.170 = bf16[2,1,8,256,6,64]{3,5,4,2,0,1:T(8,128)(2,1)} copy(bf16[2,1,8,256,6,64]{3,2,5,4,1,0:T(8,128)(2,1)} %get-tuple-element.17) | data formatting | bytes 6291456
  147.6 2.5 copy.169
  150.1 29.0 %all-gather.5.cloned.1.call-done = f32[8192,128]{1,0:T(8,128)} async-done(((f32[1024,128]{1,0:T(8,128)}), f32[8192,128]{1,0:T(8,128)}) %all-gather.5.cloned.1.call-update) | async-done | bytes 4194320 | tf_op jit(solution)/shard_map/all_gather | solution.py:25
  179.1 3.9 %multiply_reduce_fusion = f32[]{:T(128)} fusion(f32[8192,128]{1,0:T(8,128)} %all-gather.5.cloned.1.call-done), kind=kLoop, calls=%fused_computation.3 | loop fusion | flops 2097151 | bytes 4194308 | tf_op jit(solution)/shard_map/reduce_sum | solution.py:132
  183.0 1.2 broadcast_in_dim.2
  184.3 6.5 %all-to-all-start = ((f32[16,1,1]{2,1,0:T(1,128)}), f32[16,1,1]{2,1,0:T(1,128)S(1)}, u32[]{:S(2)}, u32[]{:S(2)}) async-start(f32[16,1,1]{2,1,0:T(1,128)} %broadcast_in_dim.2), calls=%async_computation.1 | async-start | bytes 16384 | tf_op jit(solution)/shard_map/all_to_all | solution.py:31
  190.8 6.4 %all-to-all-done = f32[16,1,1]{2,1,0:T(1,128)S(1)} async-done(((f32[16,1,1]{2,1,0:T(1,128)}), f32[16,1,1]{2,1,0:T(1,128)S(1)}, u32[]{:S(2)}, u32[]{:S(2)}) %all-to-all-start) | async-done | bytes 96 | tf_op jit(solution)/shard_map/all_to_all | solution.py:31
  198.5 4.8 %fusion.61 = (bf16[8192,128]{1,0:T(8,128)(2,1)S(1)}, f32[8192,128]{1,0:T(8,128)}) fusion(f32[8192,128]{1,0:T(8,128)} %all-gather.5.cloned.1.call-done, f32[]{:T(128)} %sqrt.6), kind=kLoop, calls=%fused_computation.79 | loop fusion | flops 2097152 | bytes 10485764 | tf_op jit(solution)/shard_map/convert_element_type | solution.py:136
  203.3 1.0 fusion.47
  204.3 1.0 fusion.48
  205.3 0.9 copy-done.6
  206.2 1.0 fusion.49
  207.2 1.0 fusion.46
  208.2 1.7 fusion
  211.1 1.9 fusion.12
  213.5 1.9 fusion.36
  215.4 3.2 %copy.148 = f32[2,6,256,128]{3,2,1,0:T(8,128)} copy(f32[2,6,256,128]{2,3,1,0:T(8,128)} %fusion.36) | data formatting | bytes 3145728 | tf_op jit(solution)/shard_map/add | solution.py:63
  218.6 3.8 %fusion.37 = f32[2,6,256,128]{2,3,1,0:T(8,128)} fusion(f32[2,6,128,256,1]{3,2,4,1,0:T(8,128)} %fusion.12, bf16[2,6,8,64,128]{4,3,2,1,0:T(8,128)(2,1)} %copy-done.11, bf16[2,1,6,256,8,64]{3,5,4,2,0,1:T(8,128)(2,1)S(1)} %copy-done.2), kind=kOutput, calls=%fused_computation.48 | convolution fusion | flops 403046400 | bytes 7864320 | tf_op jit(solution)/shard_map/fcmir,fcirn->fcmn/dot_general | solution.py:57
  222.5 2.0 copy.147
  225.7 40.8 %all_to_all.11 = f32[16,2,2,96,128]{4,3,1,2,0:T(8,128)S(1)} all-to-all(f32[16,2,2,96,128]{4,3,1,2,0:T(8,128)S(1)} %bitcast.186), channel_id=1, replica_groups=mesh['trow_0'=4,'trow_1'=4,'tcol_0'=4,'tcol_1'=2] {'trow_0','trow_1'}, dimensions={0} | all-to-all | bytes 6291456 | tf_op jit(solution)/shard_map/all_to_all | solution.py:46
  267.3 7.6 %psum.28 = f32[]{:T(128)} all-reduce(f32[]{:T(128)} %multiply_reduce_fusion.1), channel_id=1, replica_groups=mesh['trow_0'=4,'trow_1'=4,'tcol_0'=4,'tcol_1'=2] {'trow_0'}, use_global_device_ids=true, to_apply=%region_5.6 | all-reduce | flops 1 | bytes 8 | tf_op jit(solution)/shard_map/psum | solution.py:52
  274.9 7.1 %psum.29 = f32[]{:T(128)} all-reduce(f32[]{:T(128)} %psum.28), channel_id=1, replica_groups=mesh['trow_0'=4,'trow_1'=4,'tcol_0'=4,'tcol_1'=2] {'trow_1'}, use_global_device_ids=true, to_apply=%region_6.7 | all-reduce | flops 1 | bytes 8 | tf_op jit(solution)/shard_map/psum | solution.py:52
  281.9 7.1 %psum.30 = f32[]{:T(128)} all-reduce(f32[]{:T(128)} %psum.29), channel_id=1, replica_groups=mesh['trow_0'=4,'trow_1'=4,'tcol_0'=4,'tcol_1'=2] {'tcol_0'}, use_global_device_ids=true, to_apply=%region_7.8 | all-reduce | flops 1 | bytes 8 | tf_op jit(solution)/shard_map/psum | solution.py:52
  289.0 1.9 constant_dynamic-slice_fusion
  290.9 11.3 %psum.31 = f32[]{:T(128)} all-reduce(f32[]{:T(128)} %psum.30), channel_id=1, replica_groups=mesh['trow_0'=4,'trow_1'=4,'tcol_0'=4,'tcol_1'=2] {'tcol_1'}, use_global_device_ids=true, to_apply=%region_8.9 | all-reduce | flops 1 | bytes 8 | tf_op jit(solution)/shard_map/psum | solution.py:52
  (50 shorter events, 7.7 us)
Async XLA Ops:
  7.2 65.7 %all-gather.3.cloned.1.call-start = ((), (), s32[]{:S(2)}) async-start(), calls=%async_computation.3 | async-start | bytes 1671168 | tf_op jit(solution)/shard_map/all_gather | solution.py:122
  8.8 134.3 %reduce-scatter.2.cloned.1.call-start = ((), (), s32[]{:S(2)}) async-start(), calls=%async_computation.4 | async-start | bytes 4718592 | tf_op jit(solution)/shard_map/reduce_scatter | solution.py:24
  41.9 7.1 %copy-start.15 = (s32[2,8,6]{1,0,2:T(2,128)S(1)}, s32[2,8,6]{1,0,2:T(2,128)}, u32[]{:S(2)}) copy-start(s32[2,8,6]{1,0,2:T(2,128)} %param.8) | copy-start | bytes 1156
  75.3 1.9 copy-start
  78.5 1.4 copy-start.12
  78.5 2.5 copy-start.5
  82.1 2.5 copy-start.3
  98.6 2.9 copy-start.8
  98.6 3.5 %copy-start.9 = (f32[2,8,256,128]{3,2,1,0:T(8,128)S(1)}, f32[2,8,256,128]{3,2,1,0:T(8,128)}, u32[]{:S(2)}) copy-start(f32[2,8,256,128]{3,2,1,0:T(8,128)} %copy.134) | copy-start | bytes 6291460
  98.6 3.6 %copy-start.14 = (f32[2,2,256,128]{3,2,1,0:T(8,128)S(1)}, f32[2,2,256,128]{3,2,1,0:T(8,128)}, u32[]{:S(2)}) copy-start(f32[2,2,256,128]{3,2,1,0:T(8,128)} %param.10) | copy-start | bytes 1572868
  104.5 74.6 %all-gather.5.cloned.1.call-start = ((), (), s32[]{:S(2)}) async-start(), calls=%async_computation.5 | async-start | bytes 4718592 | tf_op jit(solution)/shard_map/all_gather | solution.py:25
  143.2 4.4 %copy-start.4 = (bf16[2,1,8,256,6,64]{3,2,5,4,1,0:T(8,128)(2,1)S(1)}, bf16[2,1,8,256,6,64]{3,2,5,4,1,0:T(8,128)(2,1)}, u32[]{:S(2)}) copy-start(bf16[2,1,8,256,6,64]{3,2,5,4,1,0:T(8,128)(2,1)} %get-tuple-element.16) | copy-start | bytes 9437188
  184.3 12.9 %all-to-all-start = ((f32[16,1,1]{2,1,0:T(1,128)}), f32[16,1,1]{2,1,0:T(1,128)S(1)}, u32[]{:S(2)}, u32[]{:S(2)}) async-start(f32[16,1,1]{2,1,0:T(1,128)} %broadcast_in_dim.2), calls=%async_computation.1 | async-start | bytes 16384 | tf_op jit(solution)/shard_map/all_to_all | solution.py:31
  198.5 4.8 %copy-start.7 = (bf16[2,1,8,256,6,64]{3,5,4,2,0,1:T(8,128)(2,1)S(1)}, bf16[2,1,8,256,6,64]{3,5,4,2,0,1:T(8,128)(2,1)}, u32[]{:S(2)}) copy-start(bf16[2,1,8,256,6,64]{3,5,4,2,0,1:T(8,128)(2,1)} %copy.170) | copy-start | bytes 9437188
  204.3 1.9 copy-start.6
  209.9 1.2 copy-start.11
  211.1 2.5 copy-start.1
  215.4 3.2 %copy-start.2 = (bf16[2,1,6,256,8,64]{3,5,4,2,0,1:T(8,128)(2,1)S(1)}, bf16[2,1,6,256,8,64]{3,5,4,2,0,1:T(8,128)(2,1)}, u32[]{:S(2)}) copy-start(bf16[2,1,6,256,8,64]{3,5,4,2,0,1:T(8,128)(2,1)} %copy.167) | copy-start | bytes 9437188
  222.5 2.0 copy-start.10
  224.5 0.9 copy-start.13
Sparse Core Ops, SparseCore 0:
  10.7 45.4 all-gather.2
  104.6 38.4 reduce-scatter.1
  144.9 34.2 all-gather.4
where the time goes:
time: 312 us; the launch traced here: 311 us
  local copies, waits for them, and re-layouts  94.3 us (30%)
  waiting for transfers between devices  74 us (24%)
  blocking collectives  73.8 us (24%)
  matrix products  28.8 us (9%)
  other arithmetic  17.1 us (5%)
  between operations  16 us (5%)
  starting transfers between devices  6.66 us (2%)
    unnamed x39, local copies, waits for them, and re-layouts  42.8 us
    all_to_all x1, blocking collectives, summed_on_arrival(): lax.all_to_all(pieces, axis, split_axis=0, concat_axis=0, tiled=True)  40.8 us
    reduce_scatter x1, waiting for transfers between devices, total_of(): own = lax.psum_scatter(padded, axis, scatter_dimension=0, tiled=True)  38.6 us
    psum x4, blocking collectives, over_axes(): value = lax.psum(value, axis)  33 us
    all_gather x1, waiting for transfers between devices, total_of(): whole = lax.all_gather(own, axis, axis=0, tiled=True)  29 us
    reshape x1, local copies, waits for them, and re-layouts, tile_views(): right_factors.reshape(frequencies, 2, columns, tile_rows, row_tiles, -1)  16.2 us
    slice x1, local copies, waits for them, and re-layouts, forward_tiles(): right_tiles[:, 0]  11 us
    dot_general x3, matrix products, complex_product(): jnp.einsum(form, a_real, b_real, preferred_element_type=jnp.float32)  10.7 us
  transfers between devices with their start and end apart: 4, of which 3 were waited for; matrix products, arithmetic and copies ran while one was open for 23% of the time, Pallas kernels for 0%

commit v1 on v0

v1 whole, which is shorter than its diff:
```python
import functools

import jax
import jax.numpy as jnp
from jax import lax
from jax.experimental import pallas as pl
from jax.experimental.pallas import tpu as pltpu
from jax.sharding import Mesh
from jax.sharding import PartitionSpec as P

TROW = ("trow_0", "trow_1")
TCOL = ("tcol_0", "tcol_1")
TROW_TCOL = ("trow_0", "trow_1", "tcol_0", "tcol_1")
TCOL_TROW = ("tcol_0", "tcol_1", "trow_0", "trow_1")

epsilon = 1e-06
BF = jnp.bfloat16
F32 = jnp.float32
VMEM = pltpu.MemorySpace.VMEM
SMEM = pltpu.MemorySpace.SMEM
HBM = pltpu.MemorySpace.HBM


def spec(space):
    return pl.BlockSpec(memory_space=space)


def params():
    return pltpu.CompilerParams(vmem_limit_bytes=56 * 1024 * 1024)


def rank_lanes(ranks_of, count, width, rank_full):
    lane = lax.broadcasted_iota(jnp.int32, (8, width), 1)
    limit = jnp.full((8, width), ranks_of(0), jnp.int32)
    for tile in range(1, count):
        limit = jnp.where(lane >= tile * rank_full, ranks_of(tile) + tile * rank_full, limit)
    return (lane < limit)[:1]


def conjugated(stacked, real, imag, half):
    a = jnp.dot(stacked, real, preferred_element_type=F32)
    b = jnp.dot(stacked, imag, preferred_element_type=F32)
    return a[:half] + b[half:], a[half:] - b[:half]


def regroup(first, second, rank_full):
    even = jnp.concatenate([first[:, :rank_full], second[:, :rank_full]], axis=1)
    odd = jnp.concatenate([first[:, rank_full:], second[:, rank_full:]], axis=1)
    return even, odd


def turned(block, half):
    return jnp.concatenate([-block[half:], block[:half]], axis=0)


def forward_kernel(
    f, dims, where_ref, ranks_ref, source_ref, right_ref, left_ref,
    send_ref, keep_ref, right_buf, left_buf, source_t, proj, grouped, right_sem, left_sem,
):
    tile, rank_full, rows, cols, nv, share, peers = dims
    right_copies = [
        pltpu.make_async_copy(
            right_ref.at[f, :, pl.ds(j * tile, tile), :], right_buf.at[j], right_sem.at[j]
        )
        for j in range(cols)
    ]
    for copy in right_copies:
        copy.start()
    z, c = where_ref[0], where_ref[1]
    half = rows // 2
    order = [2 * lax.rem(z + d, half) + (1 - c) for d in range(half)]
    order += [2 * lax.rem(z + d, half) + c for d in range(half)]
    left_copies = [
        pltpu.make_async_copy(
            left_ref.at[f, :, pl.ds(pl.multiple_of(i * tile, tile), tile), :],
            left_buf.at[n],
            left_sem.at[n],
        )
        for n, i in enumerate(order)
    ]
    for copy in left_copies:
        copy.start()
    for r in range(peers):
        for part in range(2):
            source_t[part * nv : (part + 1) * nv, r * share : (r + 1) * share] = source_ref[r, part].T
    for j in range(cols):
        right_copies[j].wait()
        stacked = source_t[:, j * tile : (j + 1) * tile]
        real, imag = conjugated(stacked, right_buf[j, 0], right_buf[j, 1], nv)
        kept = rank_lanes(lambda i: ranks_ref[f, i, j], rows, rows * rank_full, rank_full)
        proj[j, :nv] = jnp.where(kept, real, 0.0).astype(BF)
        proj[j, nv:] = jnp.where(kept, imag, 0.0).astype(BF)
    wide = cols * rank_full
    pair = 2 * rank_full
    for j in range(0, cols, 2):
        for i in range(0, rows, 2):
            lanes = slice(i * rank_full, i * rank_full + pair)
            even, odd = regroup(proj[j, :, lanes], proj[j + 1, :, lanes], rank_full)
            at = j * rank_full
            grouped[i, :, at : at + pair] = even
            grouped[i + 1, :, at : at + pair] = odd
            grouped[i, :, wide + at : wide + at + pair] = turned(even, nv)
            grouped[i + 1, :, wide + at : wide + at + pair] = turned(odd, nv)
    for n, i in enumerate(order):
        left_copies[n].wait()
        both = jnp.concatenate([left_buf[n, 0], left_buf[n, 1]], axis=1)
        out = lax.dot_general(
            both, grouped[i], (((1,), (1,)), ((), ())), preferred_element_type=F32
        )
        if n < half:
            send_ref[n, 0] = out[:, :nv].astype(BF)
            send_ref[n, 1] = out[:, nv:].astype(BF)
        else:
            keep_ref[n - half, 0] = out[:, :nv]
            keep_ref[n - half, 1] = out[:, nv:]


def forward(f, where, ranks, source, right, left, dims):
    tile, rank_full, rows, cols, nv, share, peers = dims
    half = rows // 2
    flops = 16 * rows * cols * tile * rank_full * nv
    return pl.pallas_call(
        functools.partial(forward_kernel, f, dims),
        out_shape=(
            jax.ShapeDtypeStruct((half, 2, tile, nv), BF),
            jax.ShapeDtypeStruct((half, 2, tile, nv), F32),
        ),
        in_specs=[spec(SMEM), spec(SMEM), spec(VMEM), spec(HBM), spec(HBM)],
        out_specs=(spec(VMEM), spec(VMEM)),
        scratch_shapes=[
            pltpu.VMEM((cols, 2, tile, rows * rank_full), BF),
            pltpu.VMEM((rows, 2, tile, cols * rank_full), BF),
            pltpu.VMEM((2 * nv, cols * tile), BF),
            pltpu.VMEM((cols, 2 * nv, rows * rank_full), BF),
            pltpu.VMEM((rows, 2 * nv, 2 * cols * rank_full), BF),
            pltpu.SemaphoreType.DMA((cols,)),
            pltpu.SemaphoreType.DMA((rows,)),
        ],
        compiler_params=params(),
        cost_estimate=pl.CostEstimate(flops=flops, bytes_accessed=8_000_000, transcendentals=0),
        name=f"forward_{f}",
    )(where, ranks, source, right, left)


def adjoint_kernel(
    f, dims, where_ref, ranks_ref, right_ref, left_ref, *refs,
):
    tile, rank_full, rows, cols, nv, share, peers = dims
    targets = refs[:rows]
    out_ref, right_buf, left_buf, back, grouped, right_sem, left_sem = refs[rows:]
    z, c = where_ref[0], where_ref[1]
    half = rows // 2
    order = [2 * lax.rem(z + d, half) + c for d in range(half)]
    order += [2 * lax.rem(z + d, half) + (1 - c) for d in range(half)]
    left_copies = [
        pltpu.make_async_copy(
            left_ref.at[f, :, pl.ds(pl.multiple_of(i * tile, tile), tile), :],
            left_buf.at[n],
            left_sem.at[n],
        )
        for n, i in enumerate(order)
    ]
    for copy in left_copies:
        copy.start()
    right_copies = [
        pltpu.make_async_copy(
            right_ref.at[f, :, pl.ds(j * tile, tile), :], right_buf.at[j], right_sem.at[j]
        )
        for j in range(cols)
    ]
    for copy in right_copies:
        copy.start()
    for n, i in enumerate(order):
        left_copies[n].wait()
        real, imag = conjugated(targets[n][...], left_buf[n, 0], left_buf[n, 1], nv)
        kept = rank_lanes(lambda j: ranks_ref[f, i, j], cols, cols * rank_full, rank_full)
        back[i, :nv] = jnp.where(kept, real, 0.0).astype(BF)
        back[i, nv:] = jnp.where(kept, imag, 0.0).astype(BF)
    wide = rows * rank_full
    pair = 2 * rank_full
    for i in range(0, rows, 2):
        for j in range(0, cols, 2):
            lanes = slice(j * rank_full, j * rank_full + pair)
            even, odd = regroup(back[i, :, lanes], back[i + 1, :, lanes], rank_full)
            at = i * rank_full
            grouped[j, :, at : at + pair] = even
            grouped[j + 1, :, at : at + pair] = odd
            grouped[j, :, wide + at : wide + at + pair] = turned(even, nv)
            grouped[j + 1, :, wide + at : wide + at + pair] = turned(odd, nv)
    for j in range(cols):
        right_copies[j].wait()
        both = jnp.concatenate([right_buf[j, 0], right_buf[j, 1]], axis=1)
        out = lax.dot_general(
            both, grouped[j], (((1,), (1,)), ((), ())), preferred_element_type=F32
        ).astype(BF)
        row = 0
        while row < tile:
            whole = j * tile + row
            r, start = divmod(whole, share)
            count = min(share - start, tile - row)
            out_ref[r, 0, start : start + count] = out[row : row + count, :nv]
            out_ref[r, 1, start : start + count] = out[row : row + count, nv:]
            row += count


def adjoint(f, where, ranks, right, left, targets, dims):
    tile, rank_full, rows, cols, nv, share, peers = dims
    flops = 16 * rows * cols * tile * rank_full * nv
    return pl.pallas_call(
        functools.partial(adjoint_kernel, f, dims),
        out_shape=jax.ShapeDtypeStruct((peers, 2, share, nv), BF),
        in_specs=[spec(SMEM), spec(SMEM), spec(HBM), spec(HBM)] + [spec(VMEM)] * rows,
        out_specs=spec(VMEM),
        scratch_shapes=[
            pltpu.VMEM((cols, 2, tile, rows * rank_full), BF),
            pltpu.VMEM((rows, 2, tile, cols * rank_full), BF),
            pltpu.VMEM((rows, 2 * nv, cols * rank_full), BF),
            pltpu.VMEM((cols, 2 * nv, 2 * rows * rank_full), BF),
            pltpu.SemaphoreType.DMA((cols,)),
            pltpu.SemaphoreType.DMA((rows,)),
        ],
        compiler_params=params(),
        cost_estimate=pl.CostEstimate(flops=flops, bytes_accessed=8_000_000, transcendentals=0),
        name=f"adjoint_{f}",
    )(where, ranks, right, left, *targets)


def combine_kernel(keep_ref, other_ref, own_ref, *piece_refs):
    own_ref[...] = keep_ref[0] + other_ref[0].astype(F32)
    for d, ref in enumerate(piece_refs):
        ref[...] = (keep_ref[d + 1] + other_ref[d + 1].astype(F32)).astype(BF)


def combine(f, keep, other):
    half, _, tile, nv = keep.shape
    piece = (2, tile, nv)
    return pl.pallas_call(
        combine_kernel,
        out_shape=(jax.ShapeDtypeStruct(piece, F32),)
        + (jax.ShapeDtypeStruct(piece, BF),) * (half - 1),
        in_specs=[spec(VMEM)] * 2,
        out_specs=(spec(VMEM),) * half,
        compiler_params=params(),
        cost_estimate=pl.CostEstimate(flops=keep.size * 2, bytes_accessed=keep.size * 8, transcendentals=0),
        name=f"combine_{f}",
    )(keep, other)


def folded(value):
    return jnp.sum(value.reshape(-1, 8, value.shape[-1]), axis=0)


def residual_kernel(f, alpha_ref, u_prev_ref, own_ref, *refs):
    pieces, (res_ref, target_ref, square_ref) = refs[:-3], refs[-3:]
    total = own_ref[...] - alpha_ref[0] * u_prev_ref[f]
    for ref in pieces:
        total = total + ref[...].astype(F32)
    res_ref[...] = total
    nv = total.shape[-1]
    for part in range(2):
        target_ref[part * nv : (part + 1) * nv] = total[part].T.astype(BF)
    square_ref[...] = folded(total * total)


def residual(f, alpha_prev, u_prev, own, pieces):
    _, tile, nv = own.shape
    return pl.pallas_call(
        functools.partial(residual_kernel, f),
        out_shape=(
            jax.ShapeDtypeStruct(own.shape, F32),
            jax.ShapeDtypeStruct((2 * nv, tile), BF),
            jax.ShapeDtypeStruct((8, nv), F32),
        ),
        in_specs=[spec(SMEM)] + [spec(VMEM)] * (2 + len(pieces)),
        out_specs=(spec(VMEM),) * 3,
        compiler_params=params(),
        cost_estimate=pl.CostEstimate(flops=own.size * 8, bytes_accessed=own.size * 16, transcendentals=0),
        name=f"residual_{f}",
    )(alpha_prev, u_prev, own, *pieces)


def sums_kernel(v_ref, first_ref, second_ref, square0_ref, square1_ref, w_ref, stats_ref):
    stats = [jnp.zeros((8, v_ref.shape[-1]), F32) for _ in range(3)]
    for f, ref in enumerate((first_ref, second_ref)):
        total = ref[0].astype(F32)
        for r in range(1, ref.shape[0]):
            total = total + ref[r].astype(F32)
        w_ref[f] = total
        v = v_ref[f]
        for n, product in enumerate((total * total, total * v, v * v)):
            stats[n] = stats[n] + folded(product)
    stats.append(square0_ref[...] + square1_ref[...])
    rows = [jnp.sum(s, axis=0, keepdims=True) for s in stats]
    stats_ref[...] = jnp.concatenate(rows, axis=1)


def sums(v, first, second, square0, square1):
    nv = v.shape[-1]
    return pl.pallas_call(
        sums_kernel,
        out_shape=(jax.ShapeDtypeStruct(v.shape, F32), jax.ShapeDtypeStruct((1, 4 * nv), F32)),
        in_specs=[spec(VMEM)] * 5,
        out_specs=(spec(VMEM),) * 2,
        compiler_params=params(),
        cost_estimate=pl.CostEstimate(flops=first.size * 4, bytes_accessed=first.size * 4, transcendentals=0),
        name="sums",
    )(v, first, second, square0, square1)


def finish_kernel(count_u, count_v, all_ref, v_ref, w_ref, res0_ref, res1_ref, u_ref, next_ref, scale_ref):
    nv = v_ref.shape[-1]
    everyone = jnp.sum(all_ref[...], axis=0)
    ww, wv, vv, uu = [jnp.sum(everyone[:, n * nv : (n + 1) * nv]) for n in range(4)]
    one = jnp.ones((8, nv), F32)
    beta = jnp.sqrt(one * (uu / count_u) + epsilon)
    inverse = 1.0 / beta
    square = ww * inverse * inverse - 2.0 * wv * one + vv * beta * beta
    alpha = jnp.sqrt(jnp.maximum(square, 0.0) / count_v + epsilon)
    b, ib, ia = beta[:1], inverse[:1], (1.0 / alpha)[:1]
    for f, ref in enumerate((res0_ref, res1_ref)):
        u_ref[f] = ref[...] * ib
    next_ref[...] = (w_ref[...] * ib - v_ref[...] * b) * ia
    lane = lax.broadcasted_iota(jnp.int32, (8, nv), 1)
    scale_ref[...] = jnp.where(lane == 0, beta, alpha)


def finish(everyone, v, w, res0, res1, devices):
    nv = v.shape[-1]
    count_u = float(2 * res0.size * devices)
    count_v = float(v.size * devices)
    return pl.pallas_call(
        functools.partial(finish_kernel, count_u, count_v),
        out_shape=(
            jax.ShapeDtypeStruct((2, *res0.shape), F32),
            jax.ShapeDtypeStruct(v.shape, F32),
            jax.ShapeDtypeStruct((8, nv), F32),
        ),
        in_specs=[spec(VMEM)] * 5,
        out_specs=(spec(VMEM),) * 3,
        compiler_params=params(),
        cost_estimate=pl.CostEstimate(flops=v.size * 16, bytes_accessed=v.size * 16, transcendentals=0),
        name="finish",
    )(everyone, v, w, res0, res1)


def body(left, right, ranks, v, u_prev, alpha_prev):
    frequencies, rows, cols = ranks.shape
    tile = left.shape[2] // rows
    rank_full = left.shape[3] // cols
    nv = v.shape[3]
    peers = lax.axis_size(TROW)
    chips = lax.axis_size("tcol_0")
    devices = peers * lax.axis_size(TCOL)
    dims = (tile, rank_full, rows, cols, nv, v.shape[2], peers)
    where = jnp.stack([lax.axis_index("tcol_0"), lax.axis_index("tcol_1")]).astype(jnp.int32)
    swap = [(0, 1), (1, 0)]

    def along_z(value, step):
        return lax.ppermute(value, "tcol_0", [(i, (i + step) % chips) for i in range(chips)])

    def exchange(value, axes):
        return lax.all_to_all(value, axes, split_axis=0, concat_axis=0, tiled=True)

    source = v.astype(BF)
    results = []
    for f in range(frequencies):
        gathered = exchange(jnp.broadcast_to(source[f], (peers, *source.shape[1:])), TROW)
        send, keep = forward(f, where, ranks, gathered, right, left, dims)
        other = lax.ppermute(send, "tcol_1", swap)
        own, *pieces = combine(f, keep, other)
        arrived = [along_z(piece, d + 1) for d, piece in enumerate(pieces)]
        res, target, square = residual(f, alpha_prev, u_prev, own, arrived)
        near = [target] + [along_z(target, chips - d) for d in range(1, chips)]
        far = [lax.ppermute(value, "tcol_1", swap) for value in near]
        partial = adjoint(f, where, ranks, right, left, near + far, dims)
        results.append((res, square, exchange(partial, TROW)))
    (res0, square0, first), (res1, square1, second) = results
    w, stats = sums(v, first, second, square0, square1)
    everyone = exchange(jnp.broadcast_to(stats, (devices, *stats.shape)), TROW_TCOL)
    u_next, v_next, scales = finish(everyone, v, w, res0, res1, devices)
    return (u_next, v_next, scales[0, :2])


def solution(mesh):
    finer = Mesh(mesh.devices.reshape(4, 4, 4, 2), ("trow_0", "trow_1", "tcol_0", "tcol_1"))
    placed = (
        P(None, None, TROW, TCOL),
        P(None, None, TCOL, TROW),
        P(None, TROW, TCOL),
        P(None, None, TCOL_TROW, None),
        P(None, None, TROW_TCOL, None),
        P(),
    )
    return jax.shard_map(
        body,
        mesh=finer,
        in_specs=placed,
        out_specs=(P(None, None, TROW_TCOL, None), P(None, None, TCOL_TROW, None), P()),
        check_vma=False,
    )
```

time: 312 us -> 177 us (0.57)
  local copies, waits for them, and re-layouts: 94.3 us -> 11.5 us
  Pallas kernels: 0 us -> 49.9 us
  waiting for transfers between devices: 74 us -> 29.6 us
  starting transfers between devices: 6.66 us -> 45.4 us
  blocking collectives: 73.8 us -> 36.3 us
  matrix products: 28.8 us -> 0 us
  other arithmetic: 17.1 us -> 1.55 us
  between operations: 16 us -> 1.48 us
    pallas_call x0 -> x10, Pallas kernels: none -> 49.9 us  [the longest x2 18.5 us: forward(): pl.pallas_call(functools.partial(forward_kernel, f, dims), out_shape=(jax...]
    reduce_scatter x1 -> x0, waiting for transfers between devices: 38.6 us -> none  [total_of(): own = lax.psum_scatter(padded, axis, scatter_dimension=0, tiled=True)]
    unnamed x39 -> x53, local copies, waits for them, and re-layouts: 42.8 us -> 7.25 us
    psum x4 -> x0, blocking collectives: 33 us -> none  [over_axes(): value = lax.psum(value, axis)]
    all_gather x2 -> x0, waiting for transfers between devices: 29 us -> none  [the longest x1 29 us: total_of(): whole = lax.all_gather(own, axis, axis=0, tiled=True)]
    ppermute x0 -> x22, starting transfers between devices: none -> 27.3 us  [the longest x12 17.2 us: along_z(): lax.ppermute(value, 'tcol_0', [(i, (i + step) % chips) for i in range(chi...]
    dot_general x12 -> x0, matrix products: 24.9 us -> none  [the longest x3 10.7 us: complex_product(): jnp.einsum(form, a_real, b_real, preferred_element_type=jnp.float32)]
    ppermute x0 -> x22, waiting for transfers between devices: none -> 18.3 us  [the longest x12 13.9 us: along_z(): lax.ppermute(value, 'tcol_0', [(i, (i + step) % chips) for i in range(chi...]
  transfers between devices with their start and end apart: 4 -> 25, of which waited for: 3 -> 14; matrix products, arithmetic and copies ran while one was open for 23% -> 1% of each run, Pallas kernels for 0% -> 26%
where the time goes in v1:
time: 177 us; the launch traced here: 176 us
  Pallas kernels  49.9 us (28%)
  starting transfers between devices  45.4 us (26%)
  blocking collectives  36.3 us (21%)
  waiting for transfers between devices  29.6 us (17%)
  local copies, waits for them, and re-layouts  11.5 us (6%)
    all_to_all x2, blocking collectives, exchange(): return lax.all_to_all(value, axes, split_axis=0, concat_axis=0, tiled=True)  36.3 us
    pallas_call x2, Pallas kernels, forward(): pl.pallas_call(functools.partial(forward_kernel, f, dims), out_shape=(jax...  18.5 us
    all_to_all x3, starting transfers between devices, exchange(): return lax.all_to_all(value, axes, split_axis=0, concat_axis=0, tiled=True)  18.2 us
    pallas_call x2, Pallas kernels, adjoint(): pl.pallas_call(functools.partial(adjoint_kernel, f, dims), out_shape=jax....  18 us
    ppermute x12, starting transfers between devices, along_z(): lax.ppermute(value, 'tcol_0', [(i, (i + step) % chips) for i in range(chi...  17.2 us
    ppermute x12, waiting for transfers between devices, along_z(): lax.ppermute(value, 'tcol_0', [(i, (i + step) % chips) for i in range(chi...  13.9 us
    all_to_all x3, waiting for transfers between devices, exchange(): return lax.all_to_all(value, axes, split_axis=0, concat_axis=0, tiled=True)  11.3 us
    unnamed x53, local copies, waits for them, and re-layouts  7.25 us
  transfers between devices with their start and end apart: 25, of which 14 were waited for; matrix products, arithmetic and copies ran while one was open for 1% of the time, Pallas kernels for 26%

profile of v1, /device:TPU:1, one launch (start us, length us, event | category | flops | bytes accessed | tf_op | source)
XLA Modules:
  0.0 175.8 jit_solution(10791849302469232117)
XLA Ops:
  0.6 0.9 convert_element_type.3
  1.6 1.1 broadcast_in_dim.9
  2.7 7.6 %all-to-all-start = ((bf16[16,2,96,128]{3,2,1,0:T(8,128)(2,1)}), bf16[16,2,96,128]{3,2,1,0:T(8,128)(2,1)S(1)}, u32[]{:S(2)}, u32[]{:S(2)}) async-start(bf16[16,2,96,128]{3,2,1,0:T(8,128)(2,1)} %broadcast_in_dim.9), calls=%async_computation | async-start | bytes 1572864 | tf_op jit(solution)/shard_map/all_to_all | solution.py:362
  10.3 1.4 copy.10.ranks_ref
  12.2 11.2 %all-to-all-done.source_ref = bf16[16,2,96,128]{3,2,1,0:T(8,128)(2,1)S(1)} async-done(((bf16[16,2,96,128]{3,2,1,0:T(8,128)(2,1)}), bf16[16,2,96,128]{3,2,1,0:T(8,128)(2,1)S(1)}, u32[]{:S(2)}, u32[]{:S(2)}) %all-to-all-start) | async-done | bytes 786464 | tf_op jit(solution)/shard_map/all_to_all | solution.py:362
  23.5 1.1 broadcast_in_dim.10
  24.6 3.7 %all-to-all-start.2 = ((bf16[16,2,96,128]{3,2,1,0:T(8,128)(2,1)}), bf16[16,2,96,128]{3,2,1,0:T(8,128)(2,1)S(1)}, u32[]{:S(2)}, u32[]{:S(2)}) async-start(bf16[16,2,96,128]{3,2,1,0:T(8,128)(2,1)} %broadcast_in_dim.10), calls=%async_computation.2 | async-start | bytes 1572864 | tf_op jit(solution)/shard_map/all_to_all | solution.py:362
  28.4 9.1 %forward_0.1 = (bf16[4,2,256,128]{3,2,1,0:T(8,128)(2,1)}, f32[4,2,256,128]{3,2,1,0:T(8,128)}) custom-call(s32[2]{0:T(128)} %pad_add_fusion.where_ref, s32[2,8,6]{2,1,0:T(8,128)} %copy.10.ranks_ref, bf16[16,2,96,128]{3,2,1,0:T(8,128)(2,1)} %copy-done.2, bf16[2,2,1536,512]{3,2,1,0:T(8,128)(2,1)} %right_ref.7, bf16[2,2,2048,384]{3,2,1,0:T(8,128)(2,1)} %left_ref.7), custom_call_target="tpu_custom_call" | custom-call | flops 1610612736 | bytes 8000000 | tf_op jit(solution)/shard_map/forward_0/pallas_call | solution.py:122
  37.4 2.2 %collective-permute-start = (bf16[4,2,256,128]{3,2,1,0:T(8,128)(2,1)}, bf16[4,2,256,128]{3,2,1,0:T(8,128)(2,1)S(1)}, u32[]{:S(2)}, u32[]{:S(2)}) collective-permute-start(bf16[4,2,256,128]{3,2,1,0:T(8,128)(2,1)} %get-tuple-element.27), channel_id=1, source_target_pairs={{0,1},{1,0},{2,3},{3,2},{4,5},{5,4},{6,7},{7,6},{8,9},{9,8},{10,11... | collective-permute-start | bytes 1572872 | tf_op jit(solution)/shard_map/ppermute | solution.py:369
  39.7 1.7 collective-permute-done.other_ref
  41.4 0.8 copy-done.4
  42.2 2.2 %combine_0.1 = (f32[2,256,128]{2,1,0:T(8,128)}, bf16[2,256,128]{2,1,0:T(8,128)(2,1)}, bf16[2,256,128]{2,1,0:T(8,128)(2,1)}, bf16[2,256,128]{2,1,0:T(8,128)(2,1)}) custom-call(f32[4,2,256,128]{3,2,1,0:T(8,128)} %get-tuple-element.26.keep_ref, bf16[4,2,256,128]{3,2,1,0:T(8,128)(2,1)} %copy-done.4), custom_call_target="tpu_custom_call" | custom-call | flops 524288 | bytes 2097152 | tf_op jit(solution)/shard_map/combine_0/pallas_call | solution.py:237
  44.4 1.6 collective-permute-start.1
  46.0 3.3 %collective-permute-start.2 = (bf16[2,256,128]{2,1,0:T(8,128)(2,1)}, bf16[2,256,128]{2,1,0:T(8,128)(2,1)S(1)}, u32[]{:S(2)}, u32[]{:S(2)}) collective-permute-start(bf16[2,256,128]{2,1,0:T(8,128)(2,1)} %get-tuple-element.30), channel_id=1, source_target_pairs={{0,4},{2,6},{4,0},{6,2},{1,5},{3,7},{5,1},{7,3},{8,12},{10,14},{12... | collective-permute-start | bytes 393224 | tf_op jit(solution)/shard_map/ppermute | solution.py:359
  49.3 0.7 collective-permute-start.3
  50.7 1.1 collective-permute-done.1.refs_0_
  51.9 3.7 %collective-permute-done.2.refs_1_ = bf16[2,256,128]{2,1,0:T(8,128)(2,1)S(1)} collective-permute-done((bf16[2,256,128]{2,1,0:T(8,128)(2,1)}, bf16[2,256,128]{2,1,0:T(8,128)(2,1)S(1)}, u32[]{:S(2)}, u32[]{:S(2)}) %collective-permute-start.2) | collective-permute-done | bytes 131104 | tf_op jit(solution)/shard_map/ppermute | solution.py:359
  55.6 0.6 copy-done.22
  56.3 2.1 %residual_0.1 = (f32[2,256,128]{2,1,0:T(8,128)}, bf16[256,256]{1,0:T(8,128)(2,1)}, f32[8,128]{1,0:T(8,128)}) custom-call(f32[1]{0:T(128)S(6)} %copy.13.alpha_ref, f32[2,2,256,128]{3,2,1,0:T(8,128)} %u_prev_ref.3, f32[2,256,128]{2,1,0:T(8,128)} %get-tuple-element.28.own_ref, bf16[2,256,128]{2,1,0:T(8,128)(2,1)} %copy-done.20, ...), custom_call_target="tpu_custom_call" | custom-call | flops 524288 | bytes 1048576 | tf_op jit(solution)/shard_map/residual_0/pallas_call | solution.py:267
  58.4 1.1 collective-permute-start.6
  59.5 2.2 %collective-permute-start.5 = (bf16[256,256]{1,0:T(8,128)(2,1)}, bf16[256,256]{1,0:T(8,128)(2,1)S(1)}, u32[]{:S(2)}, u32[]{:S(2)}) collective-permute-start(bf16[256,256]{1,0:T(8,128)(2,1)} %get-tuple-element.32.refs_0_), channel_id=1, source_target_pairs={{0,4},{2,6},{4,0},{6,2},{1,5},{3,7},{5,1},{7,3},{8,12},{10,14},{12... | collective-permute-start | bytes 393224 | tf_op jit(solution)/shard_map/ppermute | solution.py:359
  62.1 0.9 copy-done.1
  63.0 9.4 %forward_1.1 = (bf16[4,2,256,128]{3,2,1,0:T(8,128)(2,1)}, f32[4,2,256,128]{3,2,1,0:T(8,128)}) custom-call(s32[2]{0:T(128)} %pad_add_fusion.where_ref, s32[2,8,6]{2,1,0:T(8,128)} %copy.10.ranks_ref, bf16[16,2,96,128]{3,2,1,0:T(8,128)(2,1)} %copy-done.1, bf16[2,2,1536,512]{3,2,1,0:T(8,128)(2,1)} %right_ref.7, bf16[2,2,2048,384]{3,2,1,0:T(8,128)(2,1)} %left_ref.7), custom_call_target="tpu_custom_call" | custom-call | flops 1610612736 | bytes 8000000 | tf_op jit(solution)/shard_map/forward_1/pallas_call | solution.py:122
  72.5 2.4 %collective-permute-start.11 = (bf16[4,2,256,128]{3,2,1,0:T(8,128)(2,1)}, bf16[4,2,256,128]{3,2,1,0:T(8,128)(2,1)S(1)}, u32[]{:S(2)}, u32[]{:S(2)}) collective-permute-start(bf16[4,2,256,128]{3,2,1,0:T(8,128)(2,1)} %get-tuple-element.34), channel_id=1, source_target_pairs={{0,1},{1,0},{2,3},{3,2},{4,5},{5,4},{6,7},{7,6},{8,9},{9,8},{10,11... | collective-permute-start | bytes 1572872 | tf_op jit(solution)/shard_map/ppermute | solution.py:369
  75.9 0.9 collective-permute-done.7.refs_4_
  78.4 9.0 %adjoint_0.1 = bf16[16,2,96,128]{3,2,1,0:T(8,128)(2,1)} custom-call(s32[2]{0:T(128)} %pad_add_fusion.where_ref, s32[2,8,6]{2,1,0:T(8,128)} %copy.10.ranks_ref, bf16[2,2,1536,512]{3,2,1,0:T(8,128)(2,1)} %right_ref.7, bf16[2,2,2048,384]{3,2,1,0:T(8,128)(2,1)} %left_ref.7, bf16[256,256]{1,0:T(8,128)(2,1)} %get-tuple-element.32.refs_0_, ...), custom_call_target="tpu_custom_call" | custom-call | flops 1610612736 | bytes 8000000 | tf_op jit(solution)/shard_map/adjoint_0/pallas_call | solution.py:209
  87.4 6.9 %all-to-all-start.1 = ((bf16[16,2,96,128]{3,2,1,0:T(8,128)(2,1)}), bf16[16,2,96,128]{3,2,1,0:T(8,128)(2,1)S(1)}, u32[]{:S(2)}, u32[]{:S(2)}) async-start(bf16[16,2,96,128]{3,2,1,0:T(8,128)(2,1)} %adjoint_0.1), calls=%async_computation.1 | async-start | bytes 1572864 | tf_op jit(solution)/shard_map/all_to_all | solution.py:362
  94.3 0.8 copy-done.3
  95.1 2.2 %combine_1.1 = (f32[2,256,128]{2,1,0:T(8,128)}, bf16[2,256,128]{2,1,0:T(8,128)(2,1)}, bf16[2,256,128]{2,1,0:T(8,128)(2,1)}, bf16[2,256,128]{2,1,0:T(8,128)(2,1)}) custom-call(f32[4,2,256,128]{3,2,1,0:T(8,128)} %get-tuple-element.33.keep_ref, bf16[4,2,256,128]{3,2,1,0:T(8,128)(2,1)} %copy-done.3), custom_call_target="tpu_custom_call" | custom-call | flops 524288 | bytes 2097152 | tf_op jit(solution)/shard_map/combine_1/pallas_call | solution.py:237
  97.7 0.9 collective-permute-start.13
  98.6 1.9 %collective-permute-start.14 = (bf16[2,256,128]{2,1,0:T(8,128)(2,1)}, bf16[2,256,128]{2,1,0:T(8,128)(2,1)S(1)}, u32[]{:S(2)}, u32[]{:S(2)}) collective-permute-start(bf16[2,256,128]{2,1,0:T(8,128)(2,1)} %get-tuple-element.38), channel_id=1, source_target_pairs={{0,6},{2,0},{4,2},{6,4},{1,7},{3,1},{5,3},{7,5},{8,14},{10,8},{12,... | collective-permute-start | bytes 393224 | tf_op jit(solution)/shard_map/ppermute | solution.py:359
  100.5 5.7 %collective-permute-done.12.refs_0_ = bf16[2,256,128]{2,1,0:T(8,128)(2,1)S(1)} collective-permute-done((bf16[2,256,128]{2,1,0:T(8,128)(2,1)}, bf16[2,256,128]{2,1,0:T(8,128)(2,1)S(1)}, u32[]{:S(2)}, u32[]{:S(2)}) %collective-permute-start.12) | collective-permute-done | bytes 131104 | tf_op jit(solution)/shard_map/ppermute | solution.py:359
  107.1 2.1 %residual_1.1 = (f32[2,256,128]{2,1,0:T(8,128)}, bf16[256,256]{1,0:T(8,128)(2,1)}, f32[8,128]{1,0:T(8,128)}) custom-call(f32[1]{0:T(128)S(6)} %copy.13.alpha_ref, f32[2,2,256,128]{3,2,1,0:T(8,128)} %u_prev_ref.3, f32[2,256,128]{2,1,0:T(8,128)} %get-tuple-element.35.own_ref, bf16[2,256,128]{2,1,0:T(8,128)(2,1)} %copy-done.21, ...), custom_call_target="tpu_custom_call" | custom-call | flops 524288 | bytes 1048576 | tf_op jit(solution)/shard_map/residual_1/pallas_call | solution.py:267
  109.1 1.1 collective-permute-start.17
  110.2 3.6 %collective-permute-start.16 = (bf16[256,256]{1,0:T(8,128)(2,1)}, bf16[256,256]{1,0:T(8,128)(2,1)S(1)}, u32[]{:S(2)}, u32[]{:S(2)}) collective-permute-start(bf16[256,256]{1,0:T(8,128)(2,1)} %get-tuple-element.39.refs_0_), channel_id=1, source_target_pairs={{0,4},{2,6},{4,0},{6,2},{1,5},{3,7},{5,1},{7,3},{8,12},{10,14},{12... | collective-permute-start | bytes 393224 | tf_op jit(solution)/shard_map/ppermute | solution.py:359
  113.8 1.2 collective-permute-start.18
  115.5 1.7 collective-permute-start.21
  117.2 2.5 %collective-permute-done.16.refs_2_ = bf16[256,256]{1,0:T(8,128)(2,1)S(1)} collective-permute-done((bf16[256,256]{1,0:T(8,128)(2,1)}, bf16[256,256]{1,0:T(8,128)(2,1)S(1)}, u32[]{:S(2)}, u32[]{:S(2)}) %collective-permute-start.16) | collective-permute-done | bytes 131104 | tf_op jit(solution)/shard_map/ppermute | solution.py:359
  119.8 1.5 collective-permute-start.20
  121.4 0.9 collective-permute-done.20.refs_6_
  122.9 0.7 copy-done.18
  123.5 9.0 %adjoint_1.1 = bf16[16,2,96,128]{3,2,1,0:T(8,128)(2,1)} custom-call(s32[2]{0:T(128)} %pad_add_fusion.where_ref, s32[2,8,6]{2,1,0:T(8,128)} %copy.10.ranks_ref, bf16[2,2,1536,512]{3,2,1,0:T(8,128)(2,1)} %right_ref.7, bf16[2,2,2048,384]{3,2,1,0:T(8,128)(2,1)} %left_ref.7, bf16[256,256]{1,0:T(8,128)(2,1)} %get-tuple-element.39.refs_0_, ...), custom_call_target="tpu_custom_call" | custom-call | flops 1610612736 | bytes 8000000 | tf_op jit(solution)/shard_map/adjoint_1/pallas_call | solution.py:209
  132.6 20.3 %all_to_all.25.second_ref = bf16[16,2,96,128]{3,2,1,0:T(8,128)(2,1)} all-to-all(bf16[16,2,96,128]{3,2,1,0:T(8,128)(2,1)} %adjoint_1.1), channel_id=1, replica_groups=mesh['trow_0'=4,'trow_1'=4,'tcol_0'=4,'tcol_1'=2] {'trow_0','trow_1'}, dimensions={0} | all-to-all | bytes 1572864 | tf_op jit(solution)/shard_map/all_to_all | solution.py:362
  152.9 2.4 %sums.1 = (f32[2,2,96,128]{3,2,1,0:T(8,128)}, f32[1,512]{1,0:T(1,128)}) custom-call(f32[2,2,96,128]{3,2,1,0:T(8,128)} %v_ref.3, bf16[16,2,96,128]{3,2,1,0:T(8,128)(2,1)} %copy-done, bf16[16,2,96,128]{3,2,1,0:T(8,128)(2,1)} %all_to_all.25.second_ref, f32[8,128]{1,0:T(8,128)} %get-tuple-element.40.square0_ref, f32[8,128]{1,0:T(8,128)} %get-tuple-element.41.square1_ref), custom_call_target="tpu_custom_call" | custom-call | flops 1572864 | bytes 1572864 | tf_op jit(solution)/shard_map/sums/pallas_call | solution.py:299
  155.3 0.8 broadcast_in_dim.11
  156.1 16.0 %all_to_all.26.all_ref = f32[128,1,512]{2,1,0:T(1,128)} all-to-all(f32[128,1,512]{2,1,0:T(1,128)S(1)} %broadcast_in_dim.11), channel_id=1, replica_groups=mesh['trow_0'=4,'trow_1'=4,'tcol_0'=4,'tcol_1'=2] {'trow_0','trow_1','tc..., dimensions={0} | all-to-all | bytes 524288 | tf_op jit(solution)/shard_map/all_to_all | solution.py:362
  172.1 2.5 %finish.1 = (f32[2,2,256,128]{3,2,1,0:T(8,128)}, f32[2,2,96,128]{3,2,1,0:T(8,128)}, f32[8,128]{1,0:T(8,128)}) custom-call(f32[128,1,512]{2,1,0:T(1,128)} %all_to_all.26.all_ref, f32[2,2,96,128]{3,2,1,0:T(8,128)} %v_ref.3, f32[2,2,96,128]{3,2,1,0:T(8,128)} %get-tuple-element.43.w_ref, f32[2,256,128]{2,1,0:T(8,128)} %get-tuple-element.44.res0_ref, ...), custom_call_target="tpu_custom_call" | custom-call | flops 786432 | bytes 786432 | tf_op jit(solution)/shard_map/finish/pallas_call | solution.py:331
  174.6 1.2 slice_bitcast_fusion.2
  (74 shorter events, 6.4 us)
Async XLA Ops:
  2.7 20.8 %all-to-all-start = ((bf16[16,2,96,128]{3,2,1,0:T(8,128)(2,1)}), bf16[16,2,96,128]{3,2,1,0:T(8,128)(2,1)S(1)}, u32[]{:S(2)}, u32[]{:S(2)}) async-start(bf16[16,2,96,128]{3,2,1,0:T(8,128)(2,1)} %broadcast_in_dim.9), calls=%async_computation | async-start | bytes 1572864 | tf_op jit(solution)/shard_map/all_to_all | solution.py:362
  23.5 4.9 %copy-start.2 = (bf16[16,2,96,128]{3,2,1,0:T(8,128)(2,1)}, bf16[16,2,96,128]{3,2,1,0:T(8,128)(2,1)S(1)}, u32[]{:S(2)}) copy-start(bf16[16,2,96,128]{3,2,1,0:T(8,128)(2,1)S(1)} %all-to-all-done.source_ref) | copy-start | bytes 2359300
  24.6 37.5 %all-to-all-start.2 = ((bf16[16,2,96,128]{3,2,1,0:T(8,128)(2,1)}), bf16[16,2,96,128]{3,2,1,0:T(8,128)(2,1)S(1)}, u32[]{:S(2)}, u32[]{:S(2)}) async-start(bf16[16,2,96,128]{3,2,1,0:T(8,128)(2,1)} %broadcast_in_dim.10), calls=%async_computation.2 | async-start | bytes 1572864 | tf_op jit(solution)/shard_map/all_to_all | solution.py:362
  37.4 4.0 %collective-permute-start = (bf16[4,2,256,128]{3,2,1,0:T(8,128)(2,1)}, bf16[4,2,256,128]{3,2,1,0:T(8,128)(2,1)S(1)}, u32[]{:S(2)}, u32[]{:S(2)}) collective-permute-start(bf16[4,2,256,128]{3,2,1,0:T(8,128)(2,1)} %get-tuple-element.27), channel_id=1, source_target_pairs={{0,1},{1,0},{2,3},{3,2},{4,5},{5,4},{6,7},{7,6},{8,9},{9,8},{10,11... | collective-permute-start | bytes 1572872 | tf_op jit(solution)/shard_map/ppermute | solution.py:369
  41.4 0.8 copy-start.4
  44.4 7.5 %collective-permute-start.1 = (bf16[2,256,128]{2,1,0:T(8,128)(2,1)}, bf16[2,256,128]{2,1,0:T(8,128)(2,1)S(1)}, u32[]{:S(2)}, u32[]{:S(2)}) collective-permute-start(bf16[2,256,128]{2,1,0:T(8,128)(2,1)} %get-tuple-element.29), channel_id=1, source_target_pairs={{0,2},{2,4},{4,6},{6,0},{1,3},{3,5},{5,7},{7,1},{8,10},{10,12},{12... | collective-permute-start | bytes 393224 | tf_op jit(solution)/shard_map/ppermute | solution.py:359
  46.0 9.5 %collective-permute-start.2 = (bf16[2,256,128]{2,1,0:T(8,128)(2,1)}, bf16[2,256,128]{2,1,0:T(8,128)(2,1)S(1)}, u32[]{:S(2)}, u32[]{:S(2)}) collective-permute-start(bf16[2,256,128]{2,1,0:T(8,128)(2,1)} %get-tuple-element.30), channel_id=1, source_target_pairs={{0,4},{2,6},{4,0},{6,2},{1,5},{3,7},{5,1},{7,3},{8,12},{10,14},{12... | collective-permute-start | bytes 393224 | tf_op jit(solution)/shard_map/ppermute | solution.py:359
  49.3 6.2 %collective-permute-start.3 = (bf16[2,256,128]{2,1,0:T(8,128)(2,1)}, bf16[2,256,128]{2,1,0:T(8,128)(2,1)S(1)}, u32[]{:S(2)}, u32[]{:S(2)}) collective-permute-start(bf16[2,256,128]{2,1,0:T(8,128)(2,1)} %get-tuple-element.31), channel_id=1, source_target_pairs={{0,6},{2,0},{4,2},{6,4},{1,7},{3,1},{5,3},{7,5},{8,14},{10,8},{12,... | collective-permute-start | bytes 393224 | tf_op jit(solution)/shard_map/ppermute | solution.py:359
  51.9 3.7 %copy-start.20 = (bf16[2,256,128]{2,1,0:T(8,128)(2,1)}, bf16[2,256,128]{2,1,0:T(8,128)(2,1)S(1)}, u32[]{:S(2)}) copy-start(bf16[2,256,128]{2,1,0:T(8,128)(2,1)S(1)} %collective-permute-done.1.refs_0_) | copy-start | bytes 393220
  55.6 0.7 copy-start.22
  55.6 0.7 copy-start.24
  58.4 16.5 %copy-start.5 = (bf16[256,256]{1,0:T(8,128)(2,1)S(1)}, bf16[256,256]{1,0:T(8,128)(2,1)}, u32[]{:S(2)}) copy-start(bf16[256,256]{1,0:T(8,128)(2,1)} %get-tuple-element.32.refs_0_) | copy-start | bytes 393220
  58.4 16.6 %collective-permute-start.6 = (bf16[256,256]{1,0:T(8,128)(2,1)}, bf16[256,256]{1,0:T(8,128)(2,1)S(1)}, u32[]{:S(2)}, u32[]{:S(2)}) collective-permute-start(bf16[256,256]{1,0:T(8,128)(2,1)} %get-tuple-element.32.refs_0_), channel_id=1, source_target_pairs={{0,2},{2,4},{4,6},{6,0},{1,3},{3,5},{5,7},{7,1},{8,10},{10,12},{12... | collective-permute-start | bytes 393224 | tf_op jit(solution)/shard_map/ppermute | solution.py:359
  59.5 15.9 %collective-permute-start.5 = (bf16[256,256]{1,0:T(8,128)(2,1)}, bf16[256,256]{1,0:T(8,128)(2,1)S(1)}, u32[]{:S(2)}, u32[]{:S(2)}) collective-permute-start(bf16[256,256]{1,0:T(8,128)(2,1)} %get-tuple-element.32.refs_0_), channel_id=1, source_target_pairs={{0,4},{2,6},{4,0},{6,2},{1,5},{3,7},{5,1},{7,3},{8,12},{10,14},{12... | collective-permute-start | bytes 393224 | tf_op jit(solution)/shard_map/ppermute | solution.py:359
  61.6 13.8 %collective-permute-start.4 = (bf16[256,256]{1,0:T(8,128)(2,1)}, bf16[256,256]{1,0:T(8,128)(2,1)S(1)}, u32[]{:S(2)}, u32[]{:S(2)}) collective-permute-start(bf16[256,256]{1,0:T(8,128)(2,1)} %get-tuple-element.32.refs_0_), channel_id=1, source_target_pairs={{0,6},{2,0},{4,2},{6,4},{1,7},{3,1},{5,3},{7,5},{8,14},{10,8},{12,... | collective-permute-start | bytes 393224 | tf_op jit(solution)/shard_map/ppermute | solution.py:359
  62.1 0.9 copy-start.1
  72.5 21.9 %collective-permute-start.11 = (bf16[4,2,256,128]{3,2,1,0:T(8,128)(2,1)}, bf16[4,2,256,128]{3,2,1,0:T(8,128)(2,1)S(1)}, u32[]{:S(2)}, u32[]{:S(2)}) collective-permute-start(bf16[4,2,256,128]{3,2,1,0:T(8,128)(2,1)} %get-tuple-element.34), channel_id=1, source_target_pairs={{0,1},{1,0},{2,3},{3,2},{4,5},{5,4},{6,7},{7,6},{8,9},{9,8},{10,11... | collective-permute-start | bytes 1572872 | tf_op jit(solution)/shard_map/ppermute | solution.py:369
  74.8 1.9 %collective-permute-start.7 = (bf16[256,256]{1,0:T(8,128)(2,1)S(1)}, bf16[256,256]{1,0:T(8,128)(2,1)S(1)}, u32[]{:S(2)}, u32[]{:S(2)}) collective-permute-start(bf16[256,256]{1,0:T(8,128)(2,1)S(1)} %copy-done.5), channel_id=1, source_target_pairs={{0,1},{1,0},{2,3},{3,2},{4,5},{5,4},{6,7},{7,6},{8,9},{9,8},{10,11... | collective-permute-start | bytes 393224 | tf_op jit(solution)/shard_map/ppermute | solution.py:374
  74.9 2.4 %copy-start.6 = (bf16[256,256]{1,0:T(8,128)(2,1)}, bf16[256,256]{1,0:T(8,128)(2,1)S(1)}, u32[]{:S(2)}) copy-start(bf16[256,256]{1,0:T(8,128)(2,1)S(1)} %collective-permute-done.6.refs_3_) | copy-start | bytes 393220
  74.9 2.0 %collective-permute-start.10 = (bf16[256,256]{1,0:T(8,128)(2,1)S(1)}, bf16[256,256]{1,0:T(8,128)(2,1)S(1)}, u32[]{:S(2)}, u32[]{:S(2)}) collective-permute-start(bf16[256,256]{1,0:T(8,128)(2,1)S(1)} %collective-permute-done.6.refs_3_), channel_id=1, source_target_pairs={{0,1},{1,0},{2,3},{3,2},{4,5},{5,4},{6,7},{7,6},{8,9},{9,8},{10,11... | collective-permute-start | bytes 393224 | tf_op jit(solution)/shard_map/ppermute | solution.py:374
  75.4 2.0 %copy-start.7 = (bf16[256,256]{1,0:T(8,128)(2,1)}, bf16[256,256]{1,0:T(8,128)(2,1)S(1)}, u32[]{:S(2)}) copy-start(bf16[256,256]{1,0:T(8,128)(2,1)S(1)} %collective-permute-done.5.refs_2_) | copy-start | bytes 393220
  75.4 1.8 %collective-permute-start.9 = (bf16[256,256]{1,0:T(8,128)(2,1)S(1)}, bf16[256,256]{1,0:T(8,128)(2,1)S(1)}, u32[]{:S(2)}, u32[]{:S(2)}) collective-permute-start(bf16[256,256]{1,0:T(8,128)(2,1)S(1)} %collective-permute-done.5.refs_2_), channel_id=1, source_target_pairs={{0,1},{1,0},{2,3},{3,2},{4,5},{5,4},{6,7},{7,6},{8,9},{9,8},{10,11... | collective-permute-start | bytes 393224 | tf_op jit(solution)/shard_map/ppermute | solution.py:374
  75.5 1.9 %copy-start.8 = (bf16[256,256]{1,0:T(8,128)(2,1)}, bf16[256,256]{1,0:T(8,128)(2,1)S(1)}, u32[]{:S(2)}) copy-start(bf16[256,256]{1,0:T(8,128)(2,1)S(1)} %collective-permute-done.4.refs_1_) | copy-start | bytes 393220
  75.5 1.9 %collective-permute-start.8 = (bf16[256,256]{1,0:T(8,128)(2,1)S(1)}, bf16[256,256]{1,0:T(8,128)(2,1)S(1)}, u32[]{:S(2)}, u32[]{:S(2)}) collective-permute-start(bf16[256,256]{1,0:T(8,128)(2,1)S(1)} %collective-permute-done.4.refs_1_), channel_id=1, source_target_pairs={{0,1},{1,0},{2,3},{3,2},{4,5},{5,4},{6,7},{7,6},{8,9},{9,8},{10,11... | collective-permute-start | bytes 393224 | tf_op jit(solution)/shard_map/ppermute | solution.py:374
  76.8 0.7 copy-start.13
  87.4 45.1 %all-to-all-start.1 = ((bf16[16,2,96,128]{3,2,1,0:T(8,128)(2,1)}), bf16[16,2,96,128]{3,2,1,0:T(8,128)(2,1)S(1)}, u32[]{:S(2)}, u32[]{:S(2)}) async-start(bf16[16,2,96,128]{3,2,1,0:T(8,128)(2,1)} %adjoint_0.1), calls=%async_computation.1 | async-start | bytes 1572864 | tf_op jit(solution)/shard_map/all_to_all | solution.py:362
  94.3 0.8 copy-start.3
  97.3 8.8 %collective-permute-start.12 = (bf16[2,256,128]{2,1,0:T(8,128)(2,1)}, bf16[2,256,128]{2,1,0:T(8,128)(2,1)S(1)}, u32[]{:S(2)}, u32[]{:S(2)}) collective-permute-start(bf16[2,256,128]{2,1,0:T(8,128)(2,1)} %get-tuple-element.36), channel_id=1, source_target_pairs={{0,2},{2,4},{4,6},{6,0},{1,3},{3,5},{5,7},{7,1},{8,10},{10,12},{12... | collective-permute-start | bytes 393224 | tf_op jit(solution)/shard_map/ppermute | solution.py:359
  97.7 8.4 %collective-permute-start.13 = (bf16[2,256,128]{2,1,0:T(8,128)(2,1)}, bf16[2,256,128]{2,1,0:T(8,128)(2,1)S(1)}, u32[]{:S(2)}, u32[]{:S(2)}) collective-permute-start(bf16[2,256,128]{2,1,0:T(8,128)(2,1)} %get-tuple-element.37), channel_id=1, source_target_pairs={{0,4},{2,6},{4,0},{6,2},{1,5},{3,7},{5,1},{7,3},{8,12},{10,14},{12... | collective-permute-start | bytes 393224 | tf_op jit(solution)/shard_map/ppermute | solution.py:359
  98.6 7.8 %collective-permute-start.14 = (bf16[2,256,128]{2,1,0:T(8,128)(2,1)}, bf16[2,256,128]{2,1,0:T(8,128)(2,1)S(1)}, u32[]{:S(2)}, u32[]{:S(2)}) collective-permute-start(bf16[2,256,128]{2,1,0:T(8,128)(2,1)} %get-tuple-element.38), channel_id=1, source_target_pairs={{0,6},{2,0},{4,2},{6,4},{1,7},{3,1},{5,3},{7,5},{8,14},{10,8},{12,... | collective-permute-start | bytes 393224 | tf_op jit(solution)/shard_map/ppermute | solution.py:359
  106.2 0.7 copy-start.21
  106.2 0.7 copy-start.23
  106.4 0.7 copy-start.25
  109.1 6.4 %collective-permute-start.17 = (bf16[256,256]{1,0:T(8,128)(2,1)}, bf16[256,256]{1,0:T(8,128)(2,1)S(1)}, u32[]{:S(2)}, u32[]{:S(2)}) collective-permute-start(bf16[256,256]{1,0:T(8,128)(2,1)} %get-tuple-element.39.refs_0_), channel_id=1, source_target_pairs={{0,2},{2,4},{4,6},{6,0},{1,3},{3,5},{5,7},{7,1},{8,10},{10,12},{12... | collective-permute-start | bytes 393224 | tf_op jit(solution)/shard_map/ppermute | solution.py:359
  110.2 9.6 %collective-permute-start.16 = (bf16[256,256]{1,0:T(8,128)(2,1)}, bf16[256,256]{1,0:T(8,128)(2,1)S(1)}, u32[]{:S(2)}, u32[]{:S(2)}) collective-permute-start(bf16[256,256]{1,0:T(8,128)(2,1)} %get-tuple-element.39.refs_0_), channel_id=1, source_target_pairs={{0,4},{2,6},{4,0},{6,2},{1,5},{3,7},{5,1},{7,3},{8,12},{10,14},{12... | collective-permute-start | bytes 393224 | tf_op jit(solution)/shard_map/ppermute | solution.py:359
  113.8 7.5 %collective-permute-start.15 = (bf16[256,256]{1,0:T(8,128)(2,1)}, bf16[256,256]{1,0:T(8,128)(2,1)S(1)}, u32[]{:S(2)}, u32[]{:S(2)}) collective-permute-start(bf16[256,256]{1,0:T(8,128)(2,1)} %get-tuple-element.39.refs_0_), channel_id=1, source_target_pairs={{0,6},{2,0},{4,2},{6,4},{1,7},{3,1},{5,3},{7,5},{8,14},{10,8},{12,... | collective-permute-start | bytes 393224 | tf_op jit(solution)/shard_map/ppermute | solution.py:359
  113.8 7.6 %collective-permute-start.18 = (bf16[256,256]{1,0:T(8,128)(2,1)}, bf16[256,256]{1,0:T(8,128)(2,1)S(1)}, u32[]{:S(2)}, u32[]{:S(2)}) collective-permute-start(bf16[256,256]{1,0:T(8,128)(2,1)} %get-tuple-element.39.refs_0_), channel_id=1, source_target_pairs={{0,1},{1,0},{2,3},{3,2},{4,5},{5,4},{6,7},{7,6},{8,9},{9,8},{10,11... | collective-permute-start | bytes 393224 | tf_op jit(solution)/shard_map/ppermute | solution.py:374
  115.5 7.1 %copy-start.9 = (bf16[256,256]{1,0:T(8,128)(2,1)}, bf16[256,256]{1,0:T(8,128)(2,1)S(1)}, u32[]{:S(2)}) copy-start(bf16[256,256]{1,0:T(8,128)(2,1)S(1)} %collective-permute-done.17.refs_3_) | copy-start | bytes 393220
  115.5 5.8 %collective-permute-start.21 = (bf16[256,256]{1,0:T(8,128)(2,1)S(1)}, bf16[256,256]{1,0:T(8,128)(2,1)S(1)}, u32[]{:S(2)}, u32[]{:S(2)}) collective-permute-start(bf16[256,256]{1,0:T(8,128)(2,1)S(1)} %collective-permute-done.17.refs_3_), channel_id=1, source_target_pairs={{0,1},{1,0},{2,3},{3,2},{4,5},{5,4},{6,7},{7,6},{8,9},{9,8},{10,11... | collective-permute-start | bytes 393224 | tf_op jit(solution)/shard_map/ppermute | solution.py:374
  119.8 2.8 %copy-start.10 = (bf16[256,256]{1,0:T(8,128)(2,1)}, bf16[256,256]{1,0:T(8,128)(2,1)S(1)}, u32[]{:S(2)}) copy-start(bf16[256,256]{1,0:T(8,128)(2,1)S(1)} %collective-permute-done.16.refs_2_) | copy-start | bytes 393220
  119.8 2.4 %collective-permute-start.20 = (bf16[256,256]{1,0:T(8,128)(2,1)S(1)}, bf16[256,256]{1,0:T(8,128)(2,1)S(1)}, u32[]{:S(2)}, u32[]{:S(2)}) collective-permute-start(bf16[256,256]{1,0:T(8,128)(2,1)S(1)} %collective-permute-done.16.refs_2_), channel_id=1, source_target_pairs={{0,1},{1,0},{2,3},{3,2},{4,5},{5,4},{6,7},{7,6},{8,9},{9,8},{10,11... | collective-permute-start | bytes 393224 | tf_op jit(solution)/shard_map/ppermute | solution.py:374
  121.2 1.4 copy-start.11
  121.2 1.3 collective-permute-start.19
  121.3 1.3 copy-start.12
  121.3 1.3 copy-start.14
  122.2 0.7 copy-start.16
  122.9 0.7 copy-start.18
  132.6 20.3 %copy-start = (bf16[16,2,96,128]{3,2,1,0:T(8,128)(2,1)}, bf16[16,2,96,128]{3,2,1,0:T(8,128)(2,1)S(1)}, u32[]{:S(2)}) copy-start(bf16[16,2,96,128]{3,2,1,0:T(8,128)(2,1)S(1)} %all-to-all-done.1.first_ref) | copy-start | bytes 2359300
  (3 other events, 1.9 us)

commit v2 on v1

v2 whole, which is shorter than its diff:
```python
import functools

import jax
import jax.numpy as jnp
from jax import lax
from jax.experimental import pallas as pl
from jax.experimental.pallas import tpu as pltpu
from jax.sharding import Mesh
from jax.sharding import PartitionSpec as P


TROW = ("trow_0", "trow_1")
TCOL = ("tcol_0", "tcol_1")
TROW_TCOL = ("trow_0", "trow_1", "tcol_0", "tcol_1")
TCOL_TROW = ("tcol_0", "tcol_1", "trow_0", "trow_1")

epsilon = 1e-06
BF = jnp.bfloat16
F32 = jnp.float32
VMEM = pltpu.MemorySpace.VMEM
SMEM = pltpu.MemorySpace.SMEM
HBM = pltpu.MemorySpace.HBM


def spec(space):
    return pl.BlockSpec(memory_space=space)


def in_hbm(value):
    return pltpu.with_memory_space_constraint(value, HBM)


def params(mib=16):
    return pltpu.CompilerParams(vmem_limit_bytes=mib * 1024 * 1024)


def rank_lanes(ranks_of, count, width, rank_full):
    lane = lax.broadcasted_iota(jnp.int32, (8, width), 1)
    limit = jnp.full((8, width), ranks_of(0), jnp.int32)
    for tile in range(1, count):
        limit = jnp.where(lane >= tile * rank_full, ranks_of(tile) + tile * rank_full, limit)
    return (lane < limit)[:1]


def conjugated(stacked, real, imag, half):
    a = jnp.dot(stacked, real, preferred_element_type=F32)
    b = jnp.dot(stacked, imag, preferred_element_type=F32)
    return a[:half] + b[half:], a[half:] - b[:half]


def regroup(first, second, rank_full):
    even = jnp.concatenate([first[:, :rank_full], second[:, :rank_full]], axis=1)
    odd = jnp.concatenate([first[:, rank_full:], second[:, rank_full:]], axis=1)
    return even, odd


def turned(block, half):
    return jnp.concatenate([-block[half:], block[:half]], axis=0)


def run_all(copies):
    for copy in copies:
        copy.start()
    return copies


def prepare_kernel(v_ref, *refs):
    out, value, sem = refs
    value[...] = v_ref[...].astype(BF)
    peers = out.shape[0]
    for copy in run_all([pltpu.make_async_copy(value, out.at[r], sem.at[r]) for r in range(peers)]):
        copy.wait()


def prepare(v, peers):
    return pl.pallas_call(
        prepare_kernel,
        out_shape=jax.ShapeDtypeStruct((peers, *v.shape), BF),
        in_specs=[spec(VMEM)],
        out_specs=spec(HBM),
        scratch_shapes=[pltpu.VMEM(v.shape, BF), pltpu.SemaphoreType.DMA((peers,))],
        compiler_params=params(8),
        cost_estimate=pl.CostEstimate(flops=v.size, bytes_accessed=v.size * 36, transcendentals=0),
        name="prepare",
    )(v)


def tile_rows(index, tile):
    return pl.ds(pl.multiple_of(index * tile, tile), tile)


def tile_copies(factor_ref, f, indices, tile, out, sem):
    return [
        pltpu.make_async_copy(factor_ref.at[f, :, tile_rows(index, tile), :], out.at[n], sem.at[n])
        for n, index in enumerate(indices)
    ]


def order_of(where_ref, half):
    z, c = where_ref[0], where_ref[1]
    chips = [2 * lax.rem(z + d, half) for d in range(half)]
    return [chip + c for chip in chips], [chip + (1 - c) for chip in chips]


def expanded(factor, grouped):
    both = jnp.concatenate([factor[0], factor[1]], axis=1)
    return lax.dot_general(both, grouped, (((1,), (1,)), ((), ())), preferred_element_type=F32)


def project_kernel(
    f, dims, where_ref, ranks_ref, source_ref, right_ref, left_ref,
    send_ref, kept_ref, kept_left_ref,
    right_buf, left_buf, source_t, proj, grouped, right_sem, left_sem, kept_sem,
):
    tile, rank_full, rows, cols, nv, share, peers = dims
    half = rows // 2
    near, far = order_of(where_ref, half)
    rights = run_all(tile_copies(right_ref, f, range(cols), tile, right_buf, right_sem))
    lefts = run_all(tile_copies(left_ref, f, far, tile, left_buf, left_sem))
    kept_lefts = run_all(tile_copies(left_ref, f, near, tile, kept_left_ref, kept_sem))
    for r in range(peers):
        for part in range(2):
            source_t[part * nv : (part + 1) * nv, r * share : (r + 1) * share] = source_ref[r, f, part].T
    for j in range(cols):
        rights[j].wait()
        stacked = source_t[:, j * tile : (j + 1) * tile]
        real, imag = conjugated(stacked, right_buf[j, 0], right_buf[j, 1], nv)
        kept = rank_lanes(lambda i: ranks_ref[f, i, j], rows, rows * rank_full, rank_full)
        proj[j, :nv] = jnp.where(kept, real, 0.0).astype(BF)
        proj[j, nv:] = jnp.where(kept, imag, 0.0).astype(BF)
    wide = cols * rank_full
    pair = 2 * rank_full
    for j in range(0, cols, 2):
        for i in range(0, rows, 2):
            lanes = slice(i * rank_full, i * rank_full + pair)
            even, odd = regroup(proj[j, :, lanes], proj[j + 1, :, lanes], rank_full)
            at = j * rank_full
            grouped[i, :, at : at + pair] = even
            grouped[i + 1, :, at : at + pair] = odd
            grouped[i, :, wide + at : wide + at + pair] = turned(even, nv)
            grouped[i + 1, :, wide + at : wide + at + pair] = turned(odd, nv)
    for d in range(half):
        lefts[d].wait()
        out = expanded(left_buf[d], grouped[far[d]])
        send_ref[d, 0] = out[:, :nv].astype(BF)
        send_ref[d, 1] = out[:, nv:].astype(BF)
        kept_ref[d] = grouped[near[d]]
    for copy in kept_lefts:
        copy.wait()


def project(f, where, ranks, source, right, left, dims):
    tile, rank_full, rows, cols, nv, _, _ = dims
    half = rows // 2
    flops = 12 * rows * cols * tile * rank_full * nv
    left_tiles = (half, 2, tile, cols * rank_full)
    return pl.pallas_call(
        functools.partial(project_kernel, f, dims),
        out_shape=(
            jax.ShapeDtypeStruct((half, 2, tile, nv), BF),
            jax.ShapeDtypeStruct((half, 2 * nv, 2 * cols * rank_full), BF),
            jax.ShapeDtypeStruct(left_tiles, BF),
        ),
        in_specs=[spec(SMEM), spec(SMEM), spec(VMEM), spec(HBM), spec(HBM)],
        out_specs=(spec(VMEM),) * 3,
        scratch_shapes=[
            pltpu.VMEM((cols, 2, tile, rows * rank_full), BF),
            pltpu.VMEM(left_tiles, BF),
            pltpu.VMEM((2 * nv, cols * tile), BF),
            pltpu.VMEM((cols, 2 * nv, rows * rank_full), BF),
            pltpu.VMEM((rows, 2 * nv, 2 * cols * rank_full), BF),
            pltpu.SemaphoreType.DMA((cols,)),
            pltpu.SemaphoreType.DMA((half,)),
            pltpu.SemaphoreType.DMA((half,)),
        ],
        compiler_params=params(24),
        cost_estimate=pl.CostEstimate(flops=flops, bytes_accessed=8_000_000, transcendentals=0),
    )(where, ranks, source, in_hbm(right), in_hbm(left))


def expand_kernel(dims, kept_ref, other_ref, left_ref, own_ref, *piece_refs):
    nv, half = dims[4], dims[2] // 2
    for d in list(range(1, half)) + [0]:
        out = expanded(left_ref[d], kept_ref[d])
        for part in range(2):
            total = out[:, part * nv : (part + 1) * nv] + other_ref[d, part].astype(F32)
            if d == 0:
                own_ref[part] = total
            else:
                piece_refs[d - 1][part] = total.astype(BF)


def expand(kept, other, left, dims):
    tile, rank_full, rows, cols, nv, _, _ = dims
    half = rows // 2
    piece = (2, tile, nv)
    return pl.pallas_call(
        functools.partial(expand_kernel, dims),
        out_shape=(jax.ShapeDtypeStruct(piece, F32),)
        + (jax.ShapeDtypeStruct(piece, BF),) * (half - 1),
        in_specs=[spec(VMEM)] * 3,
        out_specs=(spec(VMEM),) * half,
        compiler_params=params(),
        cost_estimate=pl.CostEstimate(
            flops=4 * rows * cols * tile * rank_full * nv, bytes_accessed=4_000_000, transcendentals=0
        ),
    )(kept, other, left)


def back_of(f, index, target, left, ranks_ref, dims):
    _, rank_full, _, cols, nv, _, _ = dims
    real, imag = conjugated(target, left[0], left[1], nv)
    kept = rank_lanes(lambda j: ranks_ref[f, index, j], cols, cols * rank_full, rank_full)
    return jnp.where(kept, real, 0.0).astype(BF), jnp.where(kept, imag, 0.0).astype(BF)


def near_kernel(f, dims, where_ref, ranks_ref, right_ref, left_ref, *refs):
    tile, _, rows, cols, nv, _, _ = dims
    half = rows // 2
    targets = refs[:half]
    back_ref, right_out, left_out, left_buf, left_sem, far_sem, right_sem = refs[half:]
    near, far = order_of(where_ref, half)
    lefts = run_all(tile_copies(left_ref, f, near, tile, left_buf, left_sem))
    later = run_all(tile_copies(left_ref, f, far, tile, left_out, far_sem))
    later += run_all(tile_copies(right_ref, f, range(cols), tile, right_out, right_sem))
    for d, target in enumerate(targets):
        lefts[d].wait()
        real, imag = back_of(f, near[d], target[...], left_buf[d], ranks_ref, dims)
        back_ref[d, :nv] = real
        back_ref[d, nv:] = imag
    for copy in later:
        copy.wait()


def near_back(f, where, ranks, right, left, targets, dims):
    tile, rank_full, rows, cols, nv, _, _ = dims
    half = rows // 2
    left_tiles = (half, 2, tile, cols * rank_full)
    return pl.pallas_call(
        functools.partial(near_kernel, f, dims),
        out_shape=(
            jax.ShapeDtypeStruct((half, 2 * nv, cols * rank_full), BF),
            jax.ShapeDtypeStruct((cols, 2, tile, rows * rank_full), BF),
            jax.ShapeDtypeStruct(left_tiles, BF),
        ),
        in_specs=[spec(SMEM), spec(SMEM), spec(HBM), spec(HBM)] + [spec(VMEM)] * half,
        out_specs=(spec(VMEM),) * 3,
        scratch_shapes=[
            pltpu.VMEM(left_tiles, BF),
            pltpu.SemaphoreType.DMA((half,)),
            pltpu.SemaphoreType.DMA((half,)),
            pltpu.SemaphoreType.DMA((cols,)),
        ],
        compiler_params=params(24),
        cost_estimate=pl.CostEstimate(
            flops=4 * rows * cols * tile * rank_full * nv, bytes_accessed=4_000_000, transcendentals=0
        ),
    )(where, ranks, in_hbm(right), in_hbm(left), *targets)


def adjoint_kernel(f, dims, where_ref, ranks_ref, near_ref, right_ref, left_ref, *refs):
    tile, rank_full, rows, cols, nv, share, _ = dims
    half = rows // 2
    targets = refs[:half]
    out_hbm, back, grouped, out_ref, out_sem = refs[half:]
    near, far = order_of(where_ref, half)
    for d in range(half):
        back[near[d]] = near_ref[d]
        real, imag = back_of(f, far[d], targets[d][...], left_ref[d], ranks_ref, dims)
        back[far[d], :nv] = real
        back[far[d], nv:] = imag
    wide = rows * rank_full
    pair = 2 * rank_full
    for i in range(0, rows, 2):
        for j in range(0, cols, 2):
            lanes = slice(j * rank_full, j * rank_full + pair)
            even, odd = regroup(back[i, :, lanes], back[i + 1, :, lanes], rank_full)
            at = i * rank_full
            grouped[j, :, at : at + pair] = even
            grouped[j + 1, :, at : at + pair] = odd
            grouped[j, :, wide + at : wide + at + pair] = turned(even, nv)
            grouped[j + 1, :, wide + at : wide + at + pair] = turned(odd, nv)
    copies = []
    for j in range(cols):
        out = expanded(right_ref[j], grouped[j]).astype(BF)
        row = 0
        while row < tile:
            r, start = divmod(j * tile + row, share)
            count = min(share - start, tile - row)
            out_ref[r, 0, start : start + count] = out[row : row + count, :nv]
            out_ref[r, 1, start : start + count] = out[row : row + count, nv:]
            row += count
            if start + count == share:
                copies += run_all([pltpu.make_async_copy(out_ref.at[r], out_hbm.at[r], out_sem.at[r])])
    for copy in copies:
        copy.wait()


def adjoint(f, where, ranks, near, right, left, targets, dims):
    tile, rank_full, rows, cols, nv, share, peers = dims
    flops = 12 * rows * cols * tile * rank_full * nv
    return pl.pallas_call(
        functools.partial(adjoint_kernel, f, dims),
        out_shape=jax.ShapeDtypeStruct((peers, 2, share, nv), BF),
        in_specs=[spec(SMEM), spec(SMEM)] + [spec(VMEM)] * (3 + len(targets)),
        out_specs=spec(HBM),
        scratch_shapes=[
            pltpu.VMEM((rows, 2 * nv, cols * rank_full), BF),
            pltpu.VMEM((cols, 2 * nv, 2 * rows * rank_full), BF),
            pltpu.VMEM((peers, 2, share, nv), BF),
            pltpu.SemaphoreType.DMA((peers,)),
        ],
        compiler_params=params(),
        cost_estimate=pl.CostEstimate(flops=flops, bytes_accessed=8_000_000, transcendentals=0),
    )(where, ranks, near, right, left, *targets)


def folded(value):
    return jnp.sum(value.reshape(-1, 8, value.shape[-1]), axis=0)


def residual_kernel(f, alpha_ref, u_prev_ref, own_ref, *refs):
    pieces, (res_ref, target_ref, square_ref) = refs[:-3], refs[-3:]
    total = own_ref[...] - alpha_ref[0] * u_prev_ref[f]
    for ref in pieces:
        total = total + ref[...].astype(F32)
    res_ref[...] = total
    nv = total.shape[-1]
    for part in range(2):
        target_ref[part * nv : (part + 1) * nv] = total[part].T.astype(BF)
    square_ref[...] = folded(total * total)


def residual(f, alpha_prev, u_prev, own, pieces):
    _, tile, nv = own.shape
    return pl.pallas_call(
        functools.partial(residual_kernel, f),
        out_shape=(
            jax.ShapeDtypeStruct(own.shape, F32),
            jax.ShapeDtypeStruct((2 * nv, tile), BF),
            jax.ShapeDtypeStruct((8, nv), F32),
        ),
        in_specs=[spec(SMEM)] + [spec(VMEM)] * (2 + len(pieces)),
        out_specs=(spec(VMEM),) * 3,
        compiler_params=params(),
        cost_estimate=pl.CostEstimate(flops=own.size * 8, bytes_accessed=own.size * 16, transcendentals=0),
    )(alpha_prev, u_prev, own, *pieces)


def lane_sums(stats):
    nv = stats[0].shape[-1]
    lane = lax.broadcasted_iota(jnp.int32, (1, nv), 1)
    row = jnp.zeros((1, nv), F32)
    for n, value in enumerate(stats):
        total = jnp.sum(jnp.sum(value, axis=0, keepdims=True), axis=1, keepdims=True)
        row = jnp.where(lane == n, total, row)
    return row


def sums_kernel(f, v_ref, partial_ref, square_ref, *refs):
    w_ref, stats_ref = refs[-2:]
    total = partial_ref[0].astype(F32)
    for r in range(1, partial_ref.shape[0]):
        total = total + partial_ref[r].astype(F32)
    w_ref[...] = total
    v = v_ref[f]
    row = lane_sums([folded(total * total), folded(total * v), folded(v * v), square_ref[...]])
    stats_ref[...] = row + refs[0][...] if len(refs) == 3 else row


def sums(f, v, partial, square, before):
    nv = v.shape[-1]
    return pl.pallas_call(
        functools.partial(sums_kernel, f),
        out_shape=(jax.ShapeDtypeStruct(v.shape[1:], F32), jax.ShapeDtypeStruct((1, nv), F32)),
        in_specs=[spec(VMEM)] * (3 + len(before)),
        out_specs=(spec(VMEM),) * 2,
        compiler_params=params(),
        cost_estimate=pl.CostEstimate(flops=partial.size * 2, bytes_accessed=partial.size * 2, transcendentals=0),
    )(v, partial, square, *before)


def finish_kernel(count_u, count_v, all_ref, v_ref, w0_ref, w1_ref, res0_ref, res1_ref, u_ref, next_ref, scale_ref):
    nv = v_ref.shape[-1]
    everyone = jnp.sum(all_ref[...], axis=0)
    ww, wv, vv, uu = [everyone[:, n : n + 1] for n in range(4)]
    beta = jnp.sqrt(uu / count_u + epsilon)
    inverse = 1.0 / beta
    square = ww * inverse * inverse - 2.0 * wv + vv * beta * beta
    alpha = jnp.sqrt(jnp.maximum(square, 0.0) / count_v + epsilon)
    spread = [jnp.broadcast_to(x, (1, nv)) for x in (beta, inverse, 1.0 / alpha)]
    b, ib, ia = spread
    for f, (res_ref, w_ref) in enumerate(((res0_ref, w0_ref), (res1_ref, w1_ref))):
        u_ref[f] = res_ref[...] * ib
        next_ref[f] = (w_ref[...] * ib - v_ref[f] * b) * ia
    scale_ref[0] = beta[0, 0]
    scale_ref[1] = alpha[0, 0]


def finish(everyone, v, w0, w1, res0, res1, devices):
    count_u = float(2 * res0.size * devices)
    count_v = float(v.size * devices)
    return pl.pallas_call(
        functools.partial(finish_kernel, count_u, count_v),
        out_shape=(
            jax.ShapeDtypeStruct((2, *res0.shape), F32),
            jax.ShapeDtypeStruct(v.shape, F32),
            jax.ShapeDtypeStruct((2,), F32),
        ),
        in_specs=[spec(VMEM)] * 6,
        out_specs=(spec(VMEM), spec(VMEM), spec(SMEM)),
        compiler_params=params(),
        cost_estimate=pl.CostEstimate(flops=v.size * 16, bytes_accessed=v.size * 16, transcendentals=0),
        name="finish",
    )(everyone, v, w0, w1, res0, res1)


def body(left, right, ranks, v, u_prev, alpha_prev):
    frequencies, rows, cols = ranks.shape
    tile = left.shape[2] // rows
    rank_full = left.shape[3] // cols
    nv = v.shape[3]
    peers = lax.axis_size(TROW)
    chips = lax.axis_size("tcol_0")
    devices = peers * lax.axis_size(TCOL)
    dims = (tile, rank_full, rows, cols, nv, v.shape[2], peers)
    where = jnp.stack([lax.axis_index("tcol_0"), lax.axis_index("tcol_1")]).astype(jnp.int32)
    swap = [(0, 1), (1, 0)]

    def along_z(value, step):
        return lax.ppermute(value, "tcol_0", [(i, (i + step) % chips) for i in range(chips)])

    def exchange(value, axes):
        return lax.all_to_all(value, axes, split_axis=0, concat_axis=0, tiled=True)

    source = prepare(v, peers)
    gathered = exchange(source, TROW)
    results = []
    for f in range(frequencies):
        send, kept, kept_left = project(f, where, ranks, gathered, right, left, dims)
        other = lax.ppermute(send, "tcol_1", swap)
        own, *pieces = expand(kept, other, kept_left, dims)
        arrived = []
        for d, piece in enumerate(pieces):
            arrived.append(along_z(piece, d + 1))
        res, target, square = residual(f, alpha_prev, u_prev, own, arrived)
        near = [target]
        for d in range(1, chips):
            near.append(along_z(target, chips - d))
        far = []
        for d in range(chips):
            far.append(lax.ppermute(near[d], "tcol_1", swap))
        back, far_right, far_left = near_back(f, where, ranks, right, left, near, dims)
        partial = adjoint(f, where, ranks, back, far_right, far_left, far, dims)
        results.append((res, square, exchange(partial, TROW)))
    (res0, square0, first), (res1, square1, second) = results
    w0, stats0 = sums(0, v, first, square0, ())
    w1, stats = sums(1, v, second, square1, (stats0,))
    everyone = exchange(jnp.broadcast_to(stats, (devices, *stats.shape)), TROW_TCOL)
    return finish(everyone, v, w0, w1, res0, res1, devices)


def solution(mesh):
    finer = Mesh(mesh.devices.reshape(4, 4, 4, 2), ("trow_0", "trow_1", "tcol_0", "tcol_1"))
    placed = (
        P(None, None, TROW, TCOL),
        P(None, None, TCOL, TROW),
        P(None, TROW, TCOL),
        P(None, None, TCOL_TROW, None),
        P(None, None, TROW_TCOL, None),
        P(),
    )
    return jax.shard_map(
        body,
        mesh=finer,
        in_specs=placed,
        out_specs=(P(None, None, TROW_TCOL, None), P(None, None, TCOL_TROW, None), P()),
        check_vma=False,
    )
```

time: 177 us -> 152 us (0.86)
  waiting for transfers between devices: 29.6 us -> 51.5 us
  blocking collectives: 36.3 us -> 15.5 us
  Pallas kernels: 49.9 us -> 31.2 us
  local copies, waits for them, and re-layouts: 11.5 us -> 6.21 us
    all_to_all x3, waiting for transfers between devices: 11.3 us -> 36.1 us  [exchange(): return lax.all_to_all(value, axes, split_axis=0, concat_axis=0, tiled=True)]
    all_to_all x2 -> x1, blocking collectives: 36.3 us -> 15.5 us  [exchange(): return lax.all_to_all(value, axes, split_axis=0, concat_axis=0, tiled=True)]
    pallas_call x2, Pallas kernels: 18 us -> 7.2 us  [adjoint(): pl.pallas_call(functools.partial(adjoint_kernel, f, dims), out_shape=jax....]
    pallas_call x2, Pallas kernels: 4.16 us -> 0.3 us  [residual(): pl.pallas_call(functools.partial(residual_kernel, f), out_shape=(jax.Shap...]
    pallas_call x5 -> x9, Pallas kernels: 25.3 us -> 22.5 us  [the longest x2 12.4 us: project(): pl.pallas_call(functools.partial(project_kernel, f, dims), out_shape=(jax...]
    ppermute x8, waiting for transfers between devices: 2.68 us -> 0.02 us  [body(): far.append(lax.ppermute(near[d], 'tcol_1', swap))]
    broadcast_in_dim x2 -> x0, local copies, waits for them, and re-layouts: 2.23 us -> none  [body(): jnp.broadcast_to(source[f], (peers, *source.shape[1:]))]
    unnamed x53 -> x17, local copies, waits for them, and re-layouts: 7.25 us -> 6.17 us
  transfers between devices with their start and end apart: 25 -> 25, of which waited for: 14 -> 9; matrix products, arithmetic and copies ran while one was open for 1% -> 0% of each run, Pallas kernels for 26% -> 14%
where the time goes in v2:
time: 152 us; the launch traced here: 151 us
  waiting for transfers between devices  51.5 us (34%)
  starting transfers between devices  45.1 us (30%)
  Pallas kernels  31.2 us (21%)
  blocking collectives  15.5 us (10%)
  local copies, waits for them, and re-layouts  6.21 us (4%)
  between operations  1.71 us (1%)
    all_to_all x3, waiting for transfers between devices, exchange(): return lax.all_to_all(value, axes, split_axis=0, concat_axis=0, tiled=True)  36.1 us
    all_to_all x3, starting transfers between devices, exchange(): return lax.all_to_all(value, axes, split_axis=0, concat_axis=0, tiled=True)  17.9 us
    ppermute x12, starting transfers between devices, along_z(): lax.ppermute(value, 'tcol_0', [(i, (i + step) % chips) for i in range(chi...  17.3 us
    all_to_all x1, blocking collectives, exchange(): return lax.all_to_all(value, axes, split_axis=0, concat_axis=0, tiled=True)  15.5 us
    ppermute x12, waiting for transfers between devices, along_z(): lax.ppermute(value, 'tcol_0', [(i, (i + step) % chips) for i in range(chi...  13.9 us
    pallas_call x2, Pallas kernels, project(): pl.pallas_call(functools.partial(project_kernel, f, dims), out_shape=(jax...  12.4 us
    pallas_call x2, Pallas kernels, near_back(): pl.pallas_call(functools.partial(near_kernel, f, dims), out_shape=(jax.Sh...  7.23 us
    pallas_call x2, Pallas kernels, adjoint(): pl.pallas_call(functools.partial(adjoint_kernel, f, dims), out_shape=jax....  7.2 us
  transfers between devices with their start and end apart: 25, of which 9 were waited for; matrix products, arithmetic and copies ran while one was open for 0% of the time, Pallas kernels for 14%

profile of v2, /device:TPU:1, one launch (start us, length us, event | category | flops | bytes accessed | tf_op | source)
XLA Modules:
  0.0 151.3 jit_solution(11589727493856668653)
XLA Ops:
  0.6 0.9 copy-done
  1.6 1.3 prepare.1
  2.9 7.6 %all-to-all-start = ((bf16[16,2,2,96,128]{4,3,2,1,0:T(8,128)(2,1)}), bf16[16,2,2,96,128]{4,3,2,1,0:T(8,128)(2,1)S(1)}, u32[]{:S(2)}, u32[]{:S(2)}) async-start(bf16[16,2,2,96,128]{4,3,2,1,0:T(8,128)(2,1)} %prepare.1), calls=%async_computation | async-start | bytes 3145728 | tf_op jit(solution)/shard_map/all_to_all | solution.py:434
  10.7 22.9 %all-to-all-done.source_ref = bf16[16,2,2,96,128]{4,3,2,1,0:T(8,128)(2,1)S(1)} async-done(((bf16[16,2,2,96,128]{4,3,2,1,0:T(8,128)(2,1)}), bf16[16,2,2,96,128]{4,3,2,1,0:T(8,128)(2,1)S(1)}, u32[]{:S(2)}, u32[]{:S(2)}) %all-to-all-start) | async-done | bytes 1572896 | tf_op jit(solution)/shard_map/all_to_all | solution.py:434
  33.6 6.1 %shard_map.90 = (bf16[4,2,256,128]{3,2,1,0:T(8,128)(2,1)S(1)}, bf16[4,256,768]{2,1,0:T(8,128)(2,1)S(1)}, bf16[4,2,256,384]{3,2,1,0:T(8,128)(2,1)S(1)}) custom-call(s32[2]{0:T(128)S(1)} %pad_add_fusion.where_ref, s32[2,8,6]{2,1,0:T(8,128)S(1)} %copy.11.ranks_ref, bf16[16,2,2,96,128]{4,3,2,1,0:T(8,128)(2,1)S(1)} %all-to-all-done.source_ref, ...), custom_call_target="tpu_custom_call" | custom-call | flops 1207959552 | bytes 8000000 | tf_op jit(solution)/shard_map/pallas_call | solution.py:157
  39.7 2.5 %collective-permute-start.11 = (bf16[4,2,256,128]{3,2,1,0:T(8,128)(2,1)S(1)}, bf16[4,2,256,128]{3,2,1,0:T(8,128)(2,1)S(1)}, u32[]{:S(2)}, u32[]{:S(2)}) collective-permute-start(bf16[4,2,256,128]{3,2,1,0:T(8,128)(2,1)S(1)} %get-tuple-element.46), channel_id=1, source_target_pairs={{0,1},{1,0},{2,3},{3,2},{4,5},{5,4},{6,7},{7,6},{8,9},{9,8},{10,11... | collective-permute-start | bytes 1572872 | tf_op jit(solution)/shard_map/ppermute | solution.py:441
  42.2 1.5 %collective-permute-done.11.other_ref = bf16[4,2,256,128]{3,2,1,0:T(8,128)(2,1)S(1)} collective-permute-done((bf16[4,2,256,128]{3,2,1,0:T(8,128)(2,1)S(1)}, bf16[4,2,256,128]{3,2,1,0:T(8,128)(2,1)S(1)}, u32[]{:S(2)}, u32[]{:S(2)}) %collective-permute-start.11) | collective-permute-done | bytes 524320 | tf_op jit(solution)/shard_map/ppermute | solution.py:441
  43.7 0.6 shard_map.91
  44.3 1.7 %collective-permute-start.12 = (bf16[2,256,128]{2,1,0:T(8,128)(2,1)S(1)}, bf16[2,256,128]{2,1,0:T(8,128)(2,1)S(1)}, u32[]{:S(2)}, u32[]{:S(2)}) collective-permute-start(bf16[2,256,128]{2,1,0:T(8,128)(2,1)S(1)} %get-tuple-element.49), channel_id=1, source_target_pairs={{0,2},{2,4},{4,6},{6,0},{1,3},{3,5},{5,7},{7,1},{8,10},{10,12},{12... | collective-permute-start | bytes 393224 | tf_op jit(solution)/shard_map/ppermute | solution.py:431
  46.0 3.3 %collective-permute-start.13 = (bf16[2,256,128]{2,1,0:T(8,128)(2,1)S(1)}, bf16[2,256,128]{2,1,0:T(8,128)(2,1)S(1)}, u32[]{:S(2)}, u32[]{:S(2)}) collective-permute-start(bf16[2,256,128]{2,1,0:T(8,128)(2,1)S(1)} %get-tuple-element.50), channel_id=1, source_target_pairs={{0,4},{2,6},{4,0},{6,2},{1,5},{3,7},{5,1},{7,3},{8,12},{10,14},{12... | collective-permute-start | bytes 393224 | tf_op jit(solution)/shard_map/ppermute | solution.py:431
  49.3 0.7 collective-permute-start.14
  50.7 0.9 collective-permute-done.12.refs_0_
  51.6 3.7 %collective-permute-done.13.refs_1_ = bf16[2,256,128]{2,1,0:T(8,128)(2,1)S(1)} collective-permute-done((bf16[2,256,128]{2,1,0:T(8,128)(2,1)S(1)}, bf16[2,256,128]{2,1,0:T(8,128)(2,1)S(1)}, u32[]{:S(2)}, u32[]{:S(2)}) %collective-permute-start.13) | collective-permute-done | bytes 131104 | tf_op jit(solution)/shard_map/ppermute | solution.py:431
  55.5 1.4 collective-permute-start.17
  56.9 2.1 %collective-permute-start.16 = (bf16[256,256]{1,0:T(8,128)(2,1)S(1)}, bf16[256,256]{1,0:T(8,128)(2,1)S(1)}, u32[]{:S(2)}, u32[]{:S(2)}) collective-permute-start(bf16[256,256]{1,0:T(8,128)(2,1)S(1)} %get-tuple-element.52.refs_0_), channel_id=1, source_target_pairs={{0,4},{2,6},{4,0},{6,2},{1,5},{3,7},{5,1},{7,3},{8,12},{10,14},{12... | collective-permute-start | bytes 393224 | tf_op jit(solution)/shard_map/ppermute | solution.py:431
  59.0 0.4 collective-permute-start.15
  59.4 6.3 %shard_map.85 = (bf16[4,2,256,128]{3,2,1,0:T(8,128)(2,1)S(1)}, bf16[4,256,768]{2,1,0:T(8,128)(2,1)S(1)}, bf16[4,2,256,384]{3,2,1,0:T(8,128)(2,1)S(1)}) custom-call(s32[2]{0:T(128)S(1)} %pad_add_fusion.where_ref, s32[2,8,6]{2,1,0:T(8,128)S(1)} %copy.11.ranks_ref, bf16[16,2,2,96,128]{4,3,2,1,0:T(8,128)(2,1)S(1)} %all-to-all-done.source_ref, ...), custom_call_target="tpu_custom_call" | custom-call | flops 1207959552 | bytes 8000000 | tf_op jit(solution)/shard_map/pallas_call | solution.py:157
  65.7 1.2 copy-done.3
  66.8 1.2 copy-done.5
  68.0 2.3 %collective-permute-start = (bf16[4,2,256,128]{3,2,1,0:T(8,128)(2,1)S(1)}, bf16[4,2,256,128]{3,2,1,0:T(8,128)(2,1)S(1)}, u32[]{:S(2)}, u32[]{:S(2)}) collective-permute-start(bf16[4,2,256,128]{3,2,1,0:T(8,128)(2,1)S(1)} %get-tuple-element.34), channel_id=1, source_target_pairs={{0,1},{1,0},{2,3},{3,2},{4,5},{5,4},{6,7},{7,6},{8,9},{9,8},{10,11... | collective-permute-start | bytes 1572872 | tf_op jit(solution)/shard_map/ppermute | solution.py:441
  70.3 0.5 collective-permute-start.21
  70.9 0.4 collective-permute-start.19
  71.3 3.6 %shard_map.93 = (bf16[4,256,384]{2,1,0:T(8,128)(2,1)S(1)}, bf16[6,2,256,512]{3,2,1,0:T(8,128)(2,1)S(1)}, bf16[4,2,256,384]{3,2,1,0:T(8,128)(2,1)S(1)}) custom-call(s32[2]{0:T(128)S(1)} %pad_add_fusion.where_ref, s32[2,8,6]{2,1,0:T(8,128)S(1)} %copy.11.ranks_ref, bf16[2,2,1536,512]{3,2,1,0:T(8,128)(2,1)} %right_ref.7, bf16[2,2,2048,384]{3,2,1,0:T(8,128)(2,1)} %left_ref.7, ...), custom_call_target="tpu_custom_call" | custom-call | flops 402653184 | bytes 4000000 | tf_op jit(solution)/shard_map/pallas_call | solution.py:239
  75.0 3.6 %shard_map.94 = bf16[16,2,96,128]{3,2,1,0:T(8,128)(2,1)} custom-call(s32[2]{0:T(128)S(1)} %pad_add_fusion.where_ref, s32[2,8,6]{2,1,0:T(8,128)S(1)} %copy.11.ranks_ref, bf16[4,256,384]{2,1,0:T(8,128)(2,1)S(1)} %get-tuple-element.53.near_ref, bf16[6,2,256,512]{3,2,1,0:T(8,128)(2,1)S(1)} %get-tuple-element.54.right_ref, ...), custom_call_target="tpu_custom_call" | custom-call | flops 1207959552 | bytes 8000000 | tf_op jit(solution)/shard_map/pallas_call | solution.py:302
  78.6 3.6 %all-to-all-start.2 = ((bf16[16,2,96,128]{3,2,1,0:T(8,128)(2,1)}), bf16[16,2,96,128]{3,2,1,0:T(8,128)(2,1)S(1)}, u32[]{:S(2)}, u32[]{:S(2)}) async-start(bf16[16,2,96,128]{3,2,1,0:T(8,128)(2,1)} %shard_map.94), calls=%async_computation.2 | async-start | bytes 1572864 | tf_op jit(solution)/shard_map/all_to_all | solution.py:434
  82.2 1.4 copy-done.4
  83.6 1.4 copy-done.6
  85.0 0.6 shard_map.86
  85.7 0.6 collective-permute-start.1
  86.2 0.8 collective-permute-start.2
  87.1 1.7 %collective-permute-start.3 = (bf16[2,256,128]{2,1,0:T(8,128)(2,1)S(1)}, bf16[2,256,128]{2,1,0:T(8,128)(2,1)S(1)}, u32[]{:S(2)}, u32[]{:S(2)}) collective-permute-start(bf16[2,256,128]{2,1,0:T(8,128)(2,1)S(1)} %get-tuple-element.39), channel_id=1, source_target_pairs={{0,6},{2,0},{4,2},{6,4},{1,7},{3,1},{5,3},{7,5},{8,14},{10,8},{12,... | collective-permute-start | bytes 393224 | tf_op jit(solution)/shard_map/ppermute | solution.py:431
  88.8 5.7 %collective-permute-done.1.refs_0_ = bf16[2,256,128]{2,1,0:T(8,128)(2,1)S(1)} collective-permute-done((bf16[2,256,128]{2,1,0:T(8,128)(2,1)S(1)}, bf16[2,256,128]{2,1,0:T(8,128)(2,1)S(1)}, u32[]{:S(2)}, u32[]{:S(2)}) %collective-permute-start.1) | collective-permute-done | bytes 131104 | tf_op jit(solution)/shard_map/ppermute | solution.py:431
  94.5 0.3 collective-permute-done.3.refs_2_
  95.0 1.2 collective-permute-start.6
  96.2 3.4 %collective-permute-start.5 = (bf16[256,256]{1,0:T(8,128)(2,1)S(1)}, bf16[256,256]{1,0:T(8,128)(2,1)S(1)}, u32[]{:S(2)}, u32[]{:S(2)}) collective-permute-start(bf16[256,256]{1,0:T(8,128)(2,1)S(1)} %get-tuple-element.40.refs_0_), channel_id=1, source_target_pairs={{0,4},{2,6},{4,0},{6,2},{1,5},{3,7},{5,1},{7,3},{8,12},{10,14},{12... | collective-permute-start | bytes 393224 | tf_op jit(solution)/shard_map/ppermute | solution.py:431
  99.5 1.1 collective-permute-start.7
  100.6 0.6 collective-permute-done.6.refs_3_
  101.2 1.7 %collective-permute-start.10 = (bf16[256,256]{1,0:T(8,128)(2,1)S(1)}, bf16[256,256]{1,0:T(8,128)(2,1)S(1)}, u32[]{:S(2)}, u32[]{:S(2)}) collective-permute-start(bf16[256,256]{1,0:T(8,128)(2,1)S(1)} %collective-permute-done.6.refs_3_), channel_id=1, source_target_pairs={{0,1},{1,0},{2,3},{3,2},{4,5},{5,4},{6,7},{7,6},{8,9},{9,8},{10,11... | collective-permute-start | bytes 393224 | tf_op jit(solution)/shard_map/ppermute | solution.py:452
  102.8 2.6 %collective-permute-done.5.refs_2_ = bf16[256,256]{1,0:T(8,128)(2,1)S(1)} collective-permute-done((bf16[256,256]{1,0:T(8,128)(2,1)S(1)}, bf16[256,256]{1,0:T(8,128)(2,1)S(1)}, u32[]{:S(2)}, u32[]{:S(2)}) %collective-permute-start.5) | collective-permute-done | bytes 131104 | tf_op jit(solution)/shard_map/ppermute | solution.py:431
  105.4 1.3 collective-permute-start.9
  106.8 3.6 %shard_map.88 = (bf16[4,256,384]{2,1,0:T(8,128)(2,1)S(1)}, bf16[6,2,256,512]{3,2,1,0:T(8,128)(2,1)S(1)}, bf16[4,2,256,384]{3,2,1,0:T(8,128)(2,1)S(1)}) custom-call(s32[2]{0:T(128)S(1)} %pad_add_fusion.where_ref, s32[2,8,6]{2,1,0:T(8,128)S(1)} %copy.11.ranks_ref, bf16[2,2,1536,512]{3,2,1,0:T(8,128)(2,1)} %right_ref.7, bf16[2,2,2048,384]{3,2,1,0:T(8,128)(2,1)} %left_ref.7, ...), custom_call_target="tpu_custom_call" | custom-call | flops 402653184 | bytes 4000000 | tf_op jit(solution)/shard_map/pallas_call | solution.py:239
  110.5 3.6 %shard_map.89 = bf16[16,2,96,128]{3,2,1,0:T(8,128)(2,1)} custom-call(s32[2]{0:T(128)S(1)} %pad_add_fusion.where_ref, s32[2,8,6]{2,1,0:T(8,128)S(1)} %copy.11.ranks_ref, bf16[4,256,384]{2,1,0:T(8,128)(2,1)S(1)} %get-tuple-element.41.near_ref, bf16[6,2,256,512]{3,2,1,0:T(8,128)(2,1)S(1)} %get-tuple-element.42.right_ref, ...), custom_call_target="tpu_custom_call" | custom-call | flops 1207959552 | bytes 8000000 | tf_op jit(solution)/shard_map/pallas_call | solution.py:302
  114.1 6.7 %all-to-all-start.1 = ((bf16[16,2,96,128]{3,2,1,0:T(8,128)(2,1)}), bf16[16,2,96,128]{3,2,1,0:T(8,128)(2,1)S(1)}, u32[]{:S(2)}, u32[]{:S(2)}) async-start(bf16[16,2,96,128]{3,2,1,0:T(8,128)(2,1)} %shard_map.89), calls=%async_computation.1 | async-start | bytes 1572864 | tf_op jit(solution)/shard_map/all_to_all | solution.py:434
  120.9 0.2 shard_map.95
  121.1 13.2 %all-to-all-done.1.partial_ref = bf16[16,2,96,128]{3,2,1,0:T(8,128)(2,1)S(1)} async-done(((bf16[16,2,96,128]{3,2,1,0:T(8,128)(2,1)}), bf16[16,2,96,128]{3,2,1,0:T(8,128)(2,1)S(1)}, u32[]{:S(2)}, u32[]{:S(2)}) %all-to-all-start.1) | async-done | bytes 786464 | tf_op jit(solution)/shard_map/all_to_all | solution.py:434
  134.2 0.2 shard_map.96
  134.5 15.5 %all_to_all.20.all_ref = f32[128,1,128]{2,1,0:T(1,128)S(1)} all-to-all(f32[128,1,128]{2,1,0:T(1,128)S(1)} %broadcast_in_dim.3), channel_id=1, replica_groups=mesh['trow_0'=4,'trow_1'=4,'tcol_0'=4,'tcol_1'=2] {'trow_0','trow_1','tc..., dimensions={0} | all-to-all | bytes 131072 | tf_op jit(solution)/shard_map/all_to_all | solution.py:434
  150.0 1.1 finish.1
  (36 shorter events, 0.7 us)
Async XLA Ops:
  0.6 0.9 copy-start
  2.9 7.6 %copy-start.7 = (s32[2,8,6]{1,0,2:T(2,128)S(1)}, s32[2,8,6]{1,0,2:T(2,128)}, u32[]{:S(2)}) copy-start(s32[2,8,6]{1,0,2:T(2,128)} %param.8) | copy-start | bytes 1156
  2.9 30.7 %all-to-all-start = ((bf16[16,2,2,96,128]{4,3,2,1,0:T(8,128)(2,1)}), bf16[16,2,2,96,128]{4,3,2,1,0:T(8,128)(2,1)S(1)}, u32[]{:S(2)}, u32[]{:S(2)}) async-start(bf16[16,2,2,96,128]{4,3,2,1,0:T(8,128)(2,1)} %prepare.1), calls=%async_computation | async-start | bytes 3145728 | tf_op jit(solution)/shard_map/all_to_all | solution.py:434
  39.7 4.0 %collective-permute-start.11 = (bf16[4,2,256,128]{3,2,1,0:T(8,128)(2,1)S(1)}, bf16[4,2,256,128]{3,2,1,0:T(8,128)(2,1)S(1)}, u32[]{:S(2)}, u32[]{:S(2)}) collective-permute-start(bf16[4,2,256,128]{3,2,1,0:T(8,128)(2,1)S(1)} %get-tuple-element.46), channel_id=1, source_target_pairs={{0,1},{1,0},{2,3},{3,2},{4,5},{5,4},{6,7},{7,6},{8,9},{9,8},{10,11... | collective-permute-start | bytes 1572872 | tf_op jit(solution)/shard_map/ppermute | solution.py:441
  43.7 11.6 %copy-start.2 = (f32[2,2,256,128]{3,2,1,0:T(8,128)S(1)}, f32[2,2,256,128]{3,2,1,0:T(8,128)}, u32[]{:S(2)}) copy-start(f32[2,2,256,128]{3,2,1,0:T(8,128)} %u_prev_ref.3) | copy-start | bytes 1572868
  44.3 7.3 %collective-permute-start.12 = (bf16[2,256,128]{2,1,0:T(8,128)(2,1)S(1)}, bf16[2,256,128]{2,1,0:T(8,128)(2,1)S(1)}, u32[]{:S(2)}, u32[]{:S(2)}) collective-permute-start(bf16[2,256,128]{2,1,0:T(8,128)(2,1)S(1)} %get-tuple-element.49), channel_id=1, source_target_pairs={{0,2},{2,4},{4,6},{6,0},{1,3},{3,5},{5,7},{7,1},{8,10},{10,12},{12... | collective-permute-start | bytes 393224 | tf_op jit(solution)/shard_map/ppermute | solution.py:431
  46.0 9.3 %collective-permute-start.13 = (bf16[2,256,128]{2,1,0:T(8,128)(2,1)S(1)}, bf16[2,256,128]{2,1,0:T(8,128)(2,1)S(1)}, u32[]{:S(2)}, u32[]{:S(2)}) collective-permute-start(bf16[2,256,128]{2,1,0:T(8,128)(2,1)S(1)} %get-tuple-element.50), channel_id=1, source_target_pairs={{0,4},{2,6},{4,0},{6,2},{1,5},{3,7},{5,1},{7,3},{8,12},{10,14},{12... | collective-permute-start | bytes 393224 | tf_op jit(solution)/shard_map/ppermute | solution.py:431
  49.3 6.0 %collective-permute-start.14 = (bf16[2,256,128]{2,1,0:T(8,128)(2,1)S(1)}, bf16[2,256,128]{2,1,0:T(8,128)(2,1)S(1)}, u32[]{:S(2)}, u32[]{:S(2)}) collective-permute-start(bf16[2,256,128]{2,1,0:T(8,128)(2,1)S(1)} %get-tuple-element.51), channel_id=1, source_target_pairs={{0,6},{2,0},{4,2},{6,4},{1,7},{3,1},{5,3},{7,5},{8,14},{10,8},{12,... | collective-permute-start | bytes 393224 | tf_op jit(solution)/shard_map/ppermute | solution.py:431
  55.5 14.8 %collective-permute-start.17 = (bf16[256,256]{1,0:T(8,128)(2,1)S(1)}, bf16[256,256]{1,0:T(8,128)(2,1)S(1)}, u32[]{:S(2)}, u32[]{:S(2)}) collective-permute-start(bf16[256,256]{1,0:T(8,128)(2,1)S(1)} %get-tuple-element.52.refs_0_), channel_id=1, source_target_pairs={{0,2},{2,4},{4,6},{6,0},{1,3},{3,5},{5,7},{7,1},{8,10},{10,12},{12... | collective-permute-start | bytes 393224 | tf_op jit(solution)/shard_map/ppermute | solution.py:431
  56.9 13.9 %collective-permute-start.16 = (bf16[256,256]{1,0:T(8,128)(2,1)S(1)}, bf16[256,256]{1,0:T(8,128)(2,1)S(1)}, u32[]{:S(2)}, u32[]{:S(2)}) collective-permute-start(bf16[256,256]{1,0:T(8,128)(2,1)S(1)} %get-tuple-element.52.refs_0_), channel_id=1, source_target_pairs={{0,4},{2,6},{4,0},{6,2},{1,5},{3,7},{5,1},{7,3},{8,12},{10,14},{12... | collective-permute-start | bytes 393224 | tf_op jit(solution)/shard_map/ppermute | solution.py:431
  59.0 11.9 %collective-permute-start.15 = (bf16[256,256]{1,0:T(8,128)(2,1)S(1)}, bf16[256,256]{1,0:T(8,128)(2,1)S(1)}, u32[]{:S(2)}, u32[]{:S(2)}) collective-permute-start(bf16[256,256]{1,0:T(8,128)(2,1)S(1)} %get-tuple-element.52.refs_0_), channel_id=1, source_target_pairs={{0,6},{2,0},{4,2},{6,4},{1,7},{3,1},{5,3},{7,5},{8,14},{10,8},{12,... | collective-permute-start | bytes 393224 | tf_op jit(solution)/shard_map/ppermute | solution.py:431
  65.7 1.2 copy-start.3
  66.8 1.2 copy-start.5
  68.0 14.2 %collective-permute-start = (bf16[4,2,256,128]{3,2,1,0:T(8,128)(2,1)S(1)}, bf16[4,2,256,128]{3,2,1,0:T(8,128)(2,1)S(1)}, u32[]{:S(2)}, u32[]{:S(2)}) collective-permute-start(bf16[4,2,256,128]{3,2,1,0:T(8,128)(2,1)S(1)} %get-tuple-element.34), channel_id=1, source_target_pairs={{0,1},{1,0},{2,3},{3,2},{4,5},{5,4},{6,7},{7,6},{8,9},{9,8},{10,11... | collective-permute-start | bytes 1572872 | tf_op jit(solution)/shard_map/ppermute | solution.py:441
  70.3 4.7 %collective-permute-start.18 = (bf16[256,256]{1,0:T(8,128)(2,1)S(1)}, bf16[256,256]{1,0:T(8,128)(2,1)S(1)}, u32[]{:S(2)}, u32[]{:S(2)}) collective-permute-start(bf16[256,256]{1,0:T(8,128)(2,1)S(1)} %get-tuple-element.52.refs_0_), channel_id=1, source_target_pairs={{0,1},{1,0},{2,3},{3,2},{4,5},{5,4},{6,7},{7,6},{8,9},{9,8},{10,11... | collective-permute-start | bytes 393224 | tf_op jit(solution)/shard_map/ppermute | solution.py:452
  70.3 4.7 %collective-permute-start.21 = (bf16[256,256]{1,0:T(8,128)(2,1)S(1)}, bf16[256,256]{1,0:T(8,128)(2,1)S(1)}, u32[]{:S(2)}, u32[]{:S(2)}) collective-permute-start(bf16[256,256]{1,0:T(8,128)(2,1)S(1)} %collective-permute-done.17.refs_3_), channel_id=1, source_target_pairs={{0,1},{1,0},{2,3},{3,2},{4,5},{5,4},{6,7},{7,6},{8,9},{9,8},{10,11... | collective-permute-start | bytes 393224 | tf_op jit(solution)/shard_map/ppermute | solution.py:452
  70.8 4.2 %collective-permute-start.20 = (bf16[256,256]{1,0:T(8,128)(2,1)S(1)}, bf16[256,256]{1,0:T(8,128)(2,1)S(1)}, u32[]{:S(2)}, u32[]{:S(2)}) collective-permute-start(bf16[256,256]{1,0:T(8,128)(2,1)S(1)} %collective-permute-done.16.refs_2_), channel_id=1, source_target_pairs={{0,1},{1,0},{2,3},{3,2},{4,5},{5,4},{6,7},{7,6},{8,9},{9,8},{10,11... | collective-permute-start | bytes 393224 | tf_op jit(solution)/shard_map/ppermute | solution.py:452
  70.9 4.1 %collective-permute-start.19 = (bf16[256,256]{1,0:T(8,128)(2,1)S(1)}, bf16[256,256]{1,0:T(8,128)(2,1)S(1)}, u32[]{:S(2)}, u32[]{:S(2)}) collective-permute-start(bf16[256,256]{1,0:T(8,128)(2,1)S(1)} %collective-permute-done.15.refs_1_), channel_id=1, source_target_pairs={{0,1},{1,0},{2,3},{3,2},{4,5},{5,4},{6,7},{7,6},{8,9},{9,8},{10,11... | collective-permute-start | bytes 393224 | tf_op jit(solution)/shard_map/ppermute | solution.py:452
  78.6 35.5 %all-to-all-start.2 = ((bf16[16,2,96,128]{3,2,1,0:T(8,128)(2,1)}), bf16[16,2,96,128]{3,2,1,0:T(8,128)(2,1)S(1)}, u32[]{:S(2)}, u32[]{:S(2)}) async-start(bf16[16,2,96,128]{3,2,1,0:T(8,128)(2,1)} %shard_map.94), calls=%async_computation.2 | async-start | bytes 1572864 | tf_op jit(solution)/shard_map/all_to_all | solution.py:434
  82.2 1.4 copy-start.4
  83.6 1.4 copy-start.6
  85.7 8.9 %collective-permute-start.1 = (bf16[2,256,128]{2,1,0:T(8,128)(2,1)S(1)}, bf16[2,256,128]{2,1,0:T(8,128)(2,1)S(1)}, u32[]{:S(2)}, u32[]{:S(2)}) collective-permute-start(bf16[2,256,128]{2,1,0:T(8,128)(2,1)S(1)} %get-tuple-element.37), channel_id=1, source_target_pairs={{0,2},{2,4},{4,6},{6,0},{1,3},{3,5},{5,7},{7,1},{8,10},{10,12},{12... | collective-permute-start | bytes 393224 | tf_op jit(solution)/shard_map/ppermute | solution.py:431
  86.2 8.3 %collective-permute-start.2 = (bf16[2,256,128]{2,1,0:T(8,128)(2,1)S(1)}, bf16[2,256,128]{2,1,0:T(8,128)(2,1)S(1)}, u32[]{:S(2)}, u32[]{:S(2)}) collective-permute-start(bf16[2,256,128]{2,1,0:T(8,128)(2,1)S(1)} %get-tuple-element.38), channel_id=1, source_target_pairs={{0,4},{2,6},{4,0},{6,2},{1,5},{3,7},{5,1},{7,3},{8,12},{10,14},{12... | collective-permute-start | bytes 393224 | tf_op jit(solution)/shard_map/ppermute | solution.py:431
  87.1 7.8 %collective-permute-start.3 = (bf16[2,256,128]{2,1,0:T(8,128)(2,1)S(1)}, bf16[2,256,128]{2,1,0:T(8,128)(2,1)S(1)}, u32[]{:S(2)}, u32[]{:S(2)}) collective-permute-start(bf16[2,256,128]{2,1,0:T(8,128)(2,1)S(1)} %get-tuple-element.39), channel_id=1, source_target_pairs={{0,6},{2,0},{4,2},{6,4},{1,7},{3,1},{5,3},{7,5},{8,14},{10,8},{12,... | collective-permute-start | bytes 393224 | tf_op jit(solution)/shard_map/ppermute | solution.py:431
  95.0 6.1 %collective-permute-start.6 = (bf16[256,256]{1,0:T(8,128)(2,1)S(1)}, bf16[256,256]{1,0:T(8,128)(2,1)S(1)}, u32[]{:S(2)}, u32[]{:S(2)}) collective-permute-start(bf16[256,256]{1,0:T(8,128)(2,1)S(1)} %get-tuple-element.40.refs_0_), channel_id=1, source_target_pairs={{0,2},{2,4},{4,6},{6,0},{1,3},{3,5},{5,7},{7,1},{8,10},{10,12},{12... | collective-permute-start | bytes 393224 | tf_op jit(solution)/shard_map/ppermute | solution.py:431
  96.2 9.3 %collective-permute-start.5 = (bf16[256,256]{1,0:T(8,128)(2,1)S(1)}, bf16[256,256]{1,0:T(8,128)(2,1)S(1)}, u32[]{:S(2)}, u32[]{:S(2)}) collective-permute-start(bf16[256,256]{1,0:T(8,128)(2,1)S(1)} %get-tuple-element.40.refs_0_), channel_id=1, source_target_pairs={{0,4},{2,6},{4,0},{6,2},{1,5},{3,7},{5,1},{7,3},{8,12},{10,14},{12... | collective-permute-start | bytes 393224 | tf_op jit(solution)/shard_map/ppermute | solution.py:431
  99.5 7.3 %collective-permute-start.4 = (bf16[256,256]{1,0:T(8,128)(2,1)S(1)}, bf16[256,256]{1,0:T(8,128)(2,1)S(1)}, u32[]{:S(2)}, u32[]{:S(2)}) collective-permute-start(bf16[256,256]{1,0:T(8,128)(2,1)S(1)} %get-tuple-element.40.refs_0_), channel_id=1, source_target_pairs={{0,6},{2,0},{4,2},{6,4},{1,7},{3,1},{5,3},{7,5},{8,14},{10,8},{12,... | collective-permute-start | bytes 393224 | tf_op jit(solution)/shard_map/ppermute | solution.py:431
  99.5 10.9 %collective-permute-start.7 = (bf16[256,256]{1,0:T(8,128)(2,1)S(1)}, bf16[256,256]{1,0:T(8,128)(2,1)S(1)}, u32[]{:S(2)}, u32[]{:S(2)}) collective-permute-start(bf16[256,256]{1,0:T(8,128)(2,1)S(1)} %get-tuple-element.40.refs_0_), channel_id=1, source_target_pairs={{0,1},{1,0},{2,3},{3,2},{4,5},{5,4},{6,7},{7,6},{8,9},{9,8},{10,11... | collective-permute-start | bytes 393224 | tf_op jit(solution)/shard_map/ppermute | solution.py:452
  101.2 9.3 %collective-permute-start.10 = (bf16[256,256]{1,0:T(8,128)(2,1)S(1)}, bf16[256,256]{1,0:T(8,128)(2,1)S(1)}, u32[]{:S(2)}, u32[]{:S(2)}) collective-permute-start(bf16[256,256]{1,0:T(8,128)(2,1)S(1)} %collective-permute-done.6.refs_3_), channel_id=1, source_target_pairs={{0,1},{1,0},{2,3},{3,2},{4,5},{5,4},{6,7},{7,6},{8,9},{9,8},{10,11... | collective-permute-start | bytes 393224 | tf_op jit(solution)/shard_map/ppermute | solution.py:452
  105.4 5.0 %collective-permute-start.9 = (bf16[256,256]{1,0:T(8,128)(2,1)S(1)}, bf16[256,256]{1,0:T(8,128)(2,1)S(1)}, u32[]{:S(2)}, u32[]{:S(2)}) collective-permute-start(bf16[256,256]{1,0:T(8,128)(2,1)S(1)} %collective-permute-done.5.refs_2_), channel_id=1, source_target_pairs={{0,1},{1,0},{2,3},{3,2},{4,5},{5,4},{6,7},{7,6},{8,9},{9,8},{10,11... | collective-permute-start | bytes 393224 | tf_op jit(solution)/shard_map/ppermute | solution.py:452
  106.8 3.7 %collective-permute-start.8 = (bf16[256,256]{1,0:T(8,128)(2,1)S(1)}, bf16[256,256]{1,0:T(8,128)(2,1)S(1)}, u32[]{:S(2)}, u32[]{:S(2)}) collective-permute-start(bf16[256,256]{1,0:T(8,128)(2,1)S(1)} %collective-permute-done.4.refs_1_), channel_id=1, source_target_pairs={{0,1},{1,0},{2,3},{3,2},{4,5},{5,4},{6,7},{7,6},{8,9},{9,8},{10,11... | collective-permute-start | bytes 393224 | tf_op jit(solution)/shard_map/ppermute | solution.py:452
  114.1 6.8 %copy-start.1 = (f32[2,2,96,128]{3,2,1,0:T(8,128)S(1)}, f32[2,2,96,128]{3,2,1,0:T(8,128)}, u32[]{:S(2)}) copy-start(f32[2,2,96,128]{3,2,1,0:T(8,128)} %v_ref.7) | copy-start | bytes 589828
  114.1 20.1 %all-to-all-start.1 = ((bf16[16,2,96,128]{3,2,1,0:T(8,128)(2,1)}), bf16[16,2,96,128]{3,2,1,0:T(8,128)(2,1)S(1)}, u32[]{:S(2)}, u32[]{:S(2)}) async-start(bf16[16,2,96,128]{3,2,1,0:T(8,128)(2,1)} %shard_map.89), calls=%async_computation.1 | async-start | bytes 1572864 | tf_op jit(solution)/shard_map/all_to_all | solution.py:434

commit v3 on v2

--- a/solution.py
+++ b/solution.py
@@ -58,46 +58,47 @@
     return jnp.concatenate([-block[half:], block[:half]], axis=0)
 
 
+def prepare_kernel(v_ref, *out_refs):
+    for f, ref in enumerate(out_refs):
+        value = v_ref[f].astype(BF)
+        for r in range(ref.shape[0]):
+            ref[r] = value
+
+
+def prepare(v, peers):
+    frequencies = v.shape[0]
+    return pl.pallas_call(
+        prepare_kernel,
+        out_shape=(jax.ShapeDtypeStruct((peers, *v.shape[1:]), BF),) * frequencies,
+        in_specs=[spec(VMEM)],
+        out_specs=(spec(VMEM),) * frequencies,
+        compiler_params=params(8),
+        cost_estimate=pl.CostEstimate(flops=v.size, bytes_accessed=v.size * 36, transcendentals=0),
+        name="prepare",
+    )(v)
+
+
 def run_all(copies):
     for copy in copies:
         copy.start()
     return copies
 
 
-def prepare_kernel(v_ref, *refs):
-    out, value, sem = refs
-    value[...] = v_ref[...].astype(BF)
-    peers = out.shape[0]
-    for copy in run_all([pltpu.make_async_copy(value, out.at[r], sem.at[r]) for r in range(peers)]):
+def wait_all(copies):
+    for copy in copies:
         copy.wait()
 
 
-def prepare(v, peers):
-    return pl.pallas_call(
-        prepare_kernel,
-        out_shape=jax.ShapeDtypeStruct((peers, *v.shape), BF),
-        in_specs=[spec(VMEM)],
-        out_specs=spec(HBM),
-        scratch_shapes=[pltpu.VMEM(v.shape, BF), pltpu.SemaphoreType.DMA((peers,))],
-        compiler_params=params(8),
-        cost_estimate=pl.CostEstimate(flops=v.size, bytes_accessed=v.size * 36, transcendentals=0),
-        name="prepare",
-    )(v)
-
-
-def tile_rows(index, tile):
-    return pl.ds(pl.multiple_of(index * tile, tile), tile)
-
-
 def tile_copies(factor_ref, f, indices, tile, out, sem):
-    return [
-        pltpu.make_async_copy(factor_ref.at[f, :, tile_rows(index, tile), :], out.at[n], sem.at[n])
-        for n, index in enumerate(indices)
-    ]
-
-
-def order_of(where_ref, half):
-    z, c = where_ref[0], where_ref[1]
+    copies = []
+    for n, index in enumerate(indices):
+        at = pl.ds(pl.multiple_of(index * tile, tile), tile)
+        copies.append(pltpu.make_async_copy(factor_ref.at[f, :, at, :], out.at[n], sem.at[n]))
+    return copies
+
+
+def sides(core_ref, half):
+    z, c = core_ref[0], core_ref[1]
     chips = [2 * lax.rem(z + d, half) for d in range(half)]
     return [chip + c for chip in chips], [chip + (1 - c) for chip in chips]
 
@@ -107,75 +108,105 @@
     return lax.dot_general(both, grouped, (((1,), (1,)), ((), ())), preferred_element_type=F32)
 
 
-def project_kernel(
-    f, dims, where_ref, ranks_ref, source_ref, right_ref, left_ref,
-    send_ref, kept_ref, kept_left_ref,
-    right_buf, left_buf, source_t, proj, grouped, right_sem, left_sem, kept_sem,
-):
+def masked(kept, real, imag):
+    return jnp.where(kept, real, 0.0).astype(BF), jnp.where(kept, imag, 0.0).astype(BF)
+
+
+def regroup_all(blocks, grouped, outer, inner, rank_full, nv):
+    wide = outer * rank_full
+    pair = 2 * rank_full
+    for o in range(0, outer, 2):
+        for i in range(0, inner, 2):
+            lanes = slice(i * rank_full, i * rank_full + pair)
+            even, odd = regroup(blocks[o, :, lanes], blocks[o + 1, :, lanes], rank_full)
+            at = o * rank_full
+            for n, block in enumerate((even, odd)):
+                grouped[i + n, :, at : at + pair] = block
+                grouped[i + n, :, wide + at : wide + at + pair] = turned(block, nv)
+
+
+def projected(f, dims, near, far, ranks_ref, source_ref, right, ready, left, left_ready, out_refs, scratch):
     tile, rank_full, rows, cols, nv, share, peers = dims
-    half = rows // 2
-    near, far = order_of(where_ref, half)
-    rights = run_all(tile_copies(right_ref, f, range(cols), tile, right_buf, right_sem))
-    lefts = run_all(tile_copies(left_ref, f, far, tile, left_buf, left_sem))
-    kept_lefts = run_all(tile_copies(left_ref, f, near, tile, kept_left_ref, kept_sem))
+    send_ref, kept_ref = out_refs
+    stored, proj, grouped = scratch
     for r in range(peers):
         for part in range(2):
-            source_t[part * nv : (part + 1) * nv, r * share : (r + 1) * share] = source_ref[r, f, part].T
+            stored[part, r * share : (r + 1) * share, :] = source_ref[r, part]
     for j in range(cols):
-        rights[j].wait()
-        stacked = source_t[:, j * tile : (j + 1) * tile]
-        real, imag = conjugated(stacked, right_buf[j, 0], right_buf[j, 1], nv)
+        at = slice(j * tile, (j + 1) * tile)
+        stacked = jnp.concatenate([stored[0, at].T, stored[1, at].T], axis=0)
+        ready(j)
+        real, imag = conjugated(stacked, right[j, 0], right[j, 1], nv)
         kept = rank_lanes(lambda i: ranks_ref[f, i, j], rows, rows * rank_full, rank_full)
-        proj[j, :nv] = jnp.where(kept, real, 0.0).astype(BF)
-        proj[j, nv:] = jnp.where(kept, imag, 0.0).astype(BF)
-    wide = cols * rank_full
-    pair = 2 * rank_full
-    for j in range(0, cols, 2):
-        for i in range(0, rows, 2):
-            lanes = slice(i * rank_full, i * rank_full + pair)
-            even, odd = regroup(proj[j, :, lanes], proj[j + 1, :, lanes], rank_full)
-            at = j * rank_full
-            grouped[i, :, at : at + pair] = even
-            grouped[i + 1, :, at : at + pair] = odd
-            grouped[i, :, wide + at : wide + at + pair] = turned(even, nv)
-            grouped[i + 1, :, wide + at : wide + at + pair] = turned(odd, nv)
-    for d in range(half):
-        lefts[d].wait()
-        out = expanded(left_buf[d], grouped[far[d]])
+        proj[j, :nv], proj[j, nv:] = masked(kept, real, imag)
+    regroup_all(proj, grouped, cols, rows, rank_full, nv)
+    for d in range(rows // 2):
+        left_ready(d)
+        out = expanded(left[d], grouped[far[d]])
         send_ref[d, 0] = out[:, :nv].astype(BF)
         send_ref[d, 1] = out[:, nv:].astype(BF)
         kept_ref[d] = grouped[near[d]]
-    for copy in kept_lefts:
-        copy.wait()
-
-
-def project(f, where, ranks, source, right, left, dims):
+
+
+def project_kernel(
+    f, dims, core_ref, ranks_ref, source_ref, right_ref, left_ref,
+    send_ref, kept_ref, near_left_ref,
+    right_buf, left_buf, stored, proj, grouped, right_sem, left_sem, near_sem,
+):
+    tile, rows, cols = dims[0], dims[2], dims[3]
+    near, far = sides(core_ref, rows // 2)
+    rights = run_all(tile_copies(right_ref, f, range(cols), tile, right_buf, right_sem))
+    lefts = tile_copies(left_ref, f, far, tile, left_buf, left_sem)
+    later = tile_copies(left_ref, f, near, tile, near_left_ref, near_sem)
+
+    def ready(j):
+        rights[j].wait()
+        if j == 0:
+            run_all(lefts)
+            run_all(later)
+
+    projected(
+        f, dims, near, far, ranks_ref, source_ref, right_buf, ready, left_buf,
+        lambda d: lefts[d].wait(), (send_ref, kept_ref), (stored, proj, grouped),
+    )
+    wait_all(later)
+
+
+def project_shapes(dims):
     tile, rank_full, rows, cols, nv, _, _ = dims
     half = rows // 2
-    flops = 12 * rows * cols * tile * rank_full * nv
-    left_tiles = (half, 2, tile, cols * rank_full)
+    shapes = {
+        "send": (half, 2, tile, nv),
+        "kept": (half, 2 * nv, 2 * cols * rank_full),
+        "left": (half, 2, tile, cols * rank_full),
+        "right": (cols, 2, tile, rows * rank_full),
+    }
+    scratch = [
+        pltpu.VMEM((2, cols * tile, nv), BF),
+        pltpu.VMEM((cols, 2 * nv, rows * rank_full), BF),
+        pltpu.VMEM((rows, 2 * nv, 2 * cols * rank_full), BF),
+    ]
+    return shapes, scratch, pl.CostEstimate(
+        flops=12 * rows * cols * tile * rank_full * nv, bytes_accessed=8_000_000, transcendentals=0
+    )
+
+
+def project(f, core, ranks, source, right, left, dims):
+    shapes, scratch, cost = project_shapes(dims)
+    half, cols = dims[2] // 2, dims[3]
+    outs = ("send", "kept", "left")
+    sem = pltpu.SemaphoreType.DMA
     return pl.pallas_call(
         functools.partial(project_kernel, f, dims),
-        out_shape=(
-            jax.ShapeDtypeStruct((half, 2, tile, nv), BF),
-            jax.ShapeDtypeStruct((half, 2 * nv, 2 * cols * rank_full), BF),
-            jax.ShapeDtypeStruct(left_tiles, BF),
-        ),
+        out_shape=tuple(jax.ShapeDtypeStruct(shapes[n], BF) for n in outs),
         in_specs=[spec(SMEM), spec(SMEM), spec(VMEM), spec(HBM), spec(HBM)],
-        out_specs=(spec(VMEM),) * 3,
-        scratch_shapes=[
-            pltpu.VMEM((cols, 2, tile, rows * rank_full), BF),
-            pltpu.VMEM(left_tiles, BF),
-            pltpu.VMEM((2 * nv, cols * tile), BF),
-            pltpu.VMEM((cols, 2 * nv, rows * rank_full), BF),
-            pltpu.VMEM((rows, 2 * nv, 2 * cols * rank_full), BF),
-            pltpu.SemaphoreType.DMA((cols,)),
-            pltpu.SemaphoreType.DMA((half,)),
-            pltpu.SemaphoreType.DMA((half,)),
-        ],
-        compiler_params=params(24),
-        cost_estimate=pl.CostEstimate(flops=flops, bytes_accessed=8_000_000, transcendentals=0),
-    )(where, ranks, source, in_hbm(right), in_hbm(left))
+        out_specs=(spec(VMEM),) * len(outs),
+        scratch_shapes=[pltpu.VMEM(shapes["right"], BF), pltpu.VMEM(shapes["left"], BF)]
+        + scratch
+        + [sem((cols,)), sem((half,)), sem((half,))],
+        compiler_params=params(20),
+        cost_estimate=cost,
+    )(core, ranks, source, in_hbm(right), in_hbm(left))
 
 
 def expand_kernel(dims, kept_ref, other_ref, left_ref, own_ref, *piece_refs):
@@ -211,28 +242,29 @@
     _, rank_full, _, cols, nv, _, _ = dims
     real, imag = conjugated(target, left[0], left[1], nv)
     kept = rank_lanes(lambda j: ranks_ref[f, index, j], cols, cols * rank_full, rank_full)
-    return jnp.where(kept, real, 0.0).astype(BF), jnp.where(kept, imag, 0.0).astype(BF)
-
-
-def near_kernel(f, dims, where_ref, ranks_ref, right_ref, left_ref, *refs):
+    return masked(kept, real, imag)
+
+
+def near_kernel(
+    f, dims, core_ref, ranks_ref, right_ref, left_ref, *refs,
+):
     tile, _, rows, cols, nv, _, _ = dims
     half = rows // 2
     targets = refs[:half]
-    back_ref, right_out, left_out, left_buf, left_sem, far_sem, right_sem = refs[half:]
-    near, far = order_of(where_ref, half)
+    back_ref, right_out, far_out, left_buf, left_sem, far_sem, right_sem = refs[half:]
+    near, far = sides(core_ref, half)
     lefts = run_all(tile_copies(left_ref, f, near, tile, left_buf, left_sem))
-    later = run_all(tile_copies(left_ref, f, far, tile, left_out, far_sem))
+    later = run_all(tile_copies(left_ref, f, far, tile, far_out, far_sem))
     later += run_all(tile_copies(right_ref, f, range(cols), tile, right_out, right_sem))
-    for d, target in enumerate(targets):
+    for d in range(half):
         lefts[d].wait()
-        real, imag = back_of(f, near[d], target[...], left_buf[d], ranks_ref, dims)
+        real, imag = back_of(f, near[d], targets[d][...], left_buf[d], ranks_ref, dims)
         back_ref[d, :nv] = real
         back_ref[d, nv:] = imag
-    for copy in later:
-        copy.wait()
-
-
-def near_back(f, where, ranks, right, left, targets, dims):
+    wait_all(later)
+
+
+def near_back(f, core, ranks, targets, right, left, dims):
     tile, rank_full, rows, cols, nv, _, _ = dims
     half = rows // 2
     left_tiles = (half, 2, tile, cols * rank_full)
@@ -251,35 +283,25 @@
             pltpu.SemaphoreType.DMA((half,)),
             pltpu.SemaphoreType.DMA((cols,)),
         ],
-        compiler_params=params(24),
+        compiler_params=params(16),
         cost_estimate=pl.CostEstimate(
-            flops=4 * rows * cols * tile * rank_full * nv, bytes_accessed=4_000_000, transcendentals=0
+            flops=4 * rows * cols * tile * rank_full * nv, bytes_accessed=8_000_000, transcendentals=0
         ),
-    )(where, ranks, in_hbm(right), in_hbm(left), *targets)
-
-
-def adjoint_kernel(f, dims, where_ref, ranks_ref, near_ref, right_ref, left_ref, *refs):
+    )(core, ranks, in_hbm(right), in_hbm(left), *targets)
+
+
+def adjoint_kernel(f, dims, core_ref, ranks_ref, near_ref, right_ref, far_left_ref, *refs):
     tile, rank_full, rows, cols, nv, share, _ = dims
     half = rows // 2
     targets = refs[:half]
     out_hbm, back, grouped, out_ref, out_sem = refs[half:]
-    near, far = order_of(where_ref, half)
+    near, far = sides(core_ref, half)
     for d in range(half):
         back[near[d]] = near_ref[d]
-        real, imag = back_of(f, far[d], targets[d][...], left_ref[d], ranks_ref, dims)
+        real, imag = back_of(f, far[d], targets[d][...], far_left_ref[d], ranks_ref, dims)
         back[far[d], :nv] = real
         back[far[d], nv:] = imag
-    wide = rows * rank_full
-    pair = 2 * rank_full
-    for i in range(0, rows, 2):
-        for j in range(0, cols, 2):
-            lanes = slice(j * rank_full, j * rank_full + pair)
-            even, odd = regroup(back[i, :, lanes], back[i + 1, :, lanes], rank_full)
-            at = i * rank_full
-            grouped[j, :, at : at + pair] = even
-            grouped[j + 1, :, at : at + pair] = odd
-            grouped[j, :, wide + at : wide + at + pair] = turned(even, nv)
-            grouped[j + 1, :, wide + at : wide + at + pair] = turned(odd, nv)
+    regroup_all(back, grouped, rows, cols, rank_full, nv)
     copies = []
     for j in range(cols):
         out = expanded(right_ref[j], grouped[j]).astype(BF)
@@ -287,18 +309,16 @@
         while row < tile:
             r, start = divmod(j * tile + row, share)
             count = min(share - start, tile - row)
-            out_ref[r, 0, start : start + count] = out[row : row + count, :nv]
-            out_ref[r, 1, start : start + count] = out[row : row + count, nv:]
+            for part in range(2):
+                out_ref[r, part, start : start + count] = out[row : row + count, part * nv : (part + 1) * nv]
             row += count
             if start + count == share:
                 copies += run_all([pltpu.make_async_copy(out_ref.at[r], out_hbm.at[r], out_sem.at[r])])
-    for copy in copies:
-        copy.wait()
-
-
-def adjoint(f, where, ranks, near, right, left, targets, dims):
+    wait_all(copies)
+
+
+def adjoint(f, core, ranks, near, right, far_left, targets, dims):
     tile, rank_full, rows, cols, nv, share, peers = dims
-    flops = 12 * rows * cols * tile * rank_full * nv
     return pl.pallas_call(
         functools.partial(adjoint_kernel, f, dims),
         out_shape=jax.ShapeDtypeStruct((peers, 2, share, nv), BF),
@@ -310,9 +330,11 @@
             pltpu.VMEM((peers, 2, share, nv), BF),
             pltpu.SemaphoreType.DMA((peers,)),
         ],
-        compiler_params=params(),
-        cost_estimate=pl.CostEstimate(flops=flops, bytes_accessed=8_000_000, transcendentals=0),
-    )(where, ranks, near, right, left, *targets)
+        compiler_params=params(16),
+        cost_estimate=pl.CostEstimate(
+            flops=12 * rows * cols * tile * rank_full * nv, bytes_accessed=8_000_000, transcendentals=0
+        ),
+    )(core, ranks, near, right, far_left, *targets)
 
 
 def folded(value):
@@ -424,21 +446,25 @@
     chips = lax.axis_size("tcol_0")
     devices = peers * lax.axis_size(TCOL)
     dims = (tile, rank_full, rows, cols, nv, v.shape[2], peers)
-    where = jnp.stack([lax.axis_index("tcol_0"), lax.axis_index("tcol_1")]).astype(jnp.int32)
-    swap = [(0, 1), (1, 0)]
+    core = jnp.stack([lax.axis_index("tcol_0"), lax.axis_index("tcol_1")]).astype(jnp.int32)
+
+    def exchange(value, axes):
+        return lax.all_to_all(value, axes, split_axis=0, concat_axis=0, tiled=True)
+
+    def swapped(value):
+        return lax.ppermute(value, "tcol_1", [(0, 1), (1, 0)])
 
     def along_z(value, step):
         return lax.ppermute(value, "tcol_0", [(i, (i + step) % chips) for i in range(chips)])
 
-    def exchange(value, axes):
-        return lax.all_to_all(value, axes, split_axis=0, concat_axis=0, tiled=True)
-
-    source = prepare(v, peers)
-    gathered = exchange(source, TROW)
+    sources = prepare(v, peers)
+    gathered = []
+    for f in range(frequencies):
+        gathered.append(exchange(sources[f], TROW))
     results = []
     for f in range(frequencies):
-        send, kept, kept_left = project(f, where, ranks, gathered, right, left, dims)
-        other = lax.ppermute(send, "tcol_1", swap)
+        send, kept, kept_left = project(f, core, ranks, gathered[f], right, left, dims)
+        other = swapped(send)
         own, *pieces = expand(kept, other, kept_left, dims)
         arrived = []
         for d, piece in enumerate(pieces):
@@ -449,9 +475,9 @@
             near.append(along_z(target, chips - d))
         far = []
         for d in range(chips):
-            far.append(lax.ppermute(near[d], "tcol_1", swap))
-        back, far_right, far_left = near_back(f, where, ranks, right, left, near, dims)
-        partial = adjoint(f, where, ranks, back, far_right, far_left, far, dims)
+            far.append(swapped(near[d]))
+        back, far_right, far_left = near_back(f, core, ranks, near, right, left, dims)
+        partial = adjoint(f, core, ranks, back, far_right, far_left, far, dims)
         results.append((res, square, exchange(partial, TROW)))
     (res0, square0, first), (res1, square1, second) = results
     w0, stats0 = sums(0, v, first, square0, ())

time: 152 us -> 146 us (0.961)
  waiting for transfers between devices: 51.5 us -> 38.3 us
  starting transfers between devices: 45.1 us -> 54.4 us
    all_to_all x3 -> x4, waiting for transfers between devices: 36.1 us -> 26.7 us  [exchange(): return lax.all_to_all(value, axes, split_axis=0, concat_axis=0, tiled=True)]
    all_to_all x3 -> x4, starting transfers between devices: 17.9 us -> 24.9 us  [exchange(): return lax.all_to_all(value, axes, split_axis=0, concat_axis=0, tiled=True)]
    ppermute x12, waiting for transfers between devices: 13.9 us -> 9.99 us  [along_z(): lax.ppermute(value, 'tcol_0', [(i, (i + step) % chips) for i in range(chi...]
    ppermute x10, starting transfers between devices: 9.85 us -> 12.5 us  [swapped(): return lax.ppermute(value, 'tcol_1', [(0, 1), (1, 0)])]
  transfers between devices with their start and end apart: 25 -> 26, of which waited for: 9 -> 7; matrix products, arithmetic and copies ran while one was open for 0% -> 0% of each run, Pallas kernels for 14% -> 19%
where the time goes in v3:
time: 146 us; the launch traced here: 145 us
  starting transfers between devices  54.4 us (37%)
  waiting for transfers between devices  38.3 us (26%)
  Pallas kernels  29.9 us (20%)
  blocking collectives  14.8 us (10%)
  local copies, waits for them, and re-layouts  6.19 us (4%)
  between operations  1.71 us (1%)
    all_to_all x4, waiting for transfers between devices, exchange(): return lax.all_to_all(value, axes, split_axis=0, concat_axis=0, tiled=True)  26.7 us
    all_to_all x4, starting transfers between devices, exchange(): return lax.all_to_all(value, axes, split_axis=0, concat_axis=0, tiled=True)  24.9 us
    ppermute x12, starting transfers between devices, along_z(): lax.ppermute(value, 'tcol_0', [(i, (i + step) % chips) for i in range(chi...  17 us
    all_to_all x1, blocking collectives, exchange(): return lax.all_to_all(value, axes, split_axis=0, concat_axis=0, tiled=True)  14.8 us
    ppermute x10, starting transfers between devices, swapped(): return lax.ppermute(value, 'tcol_1', [(0, 1), (1, 0)])  12.5 us
    pallas_call x2, Pallas kernels, project(): pl.pallas_call(functools.partial(project_kernel, f, dims), out_shape=tupl...  11.2 us
    ppermute x12, waiting for transfers between devices, along_z(): lax.ppermute(value, 'tcol_0', [(i, (i + step) % chips) for i in range(chi...  9.99 us
    pallas_call x2, Pallas kernels, near_back(): pl.pallas_call(functools.partial(near_kernel, f, dims), out_shape=(jax.Sh...  7.23 us
  transfers between devices with their start and end apart: 26, of which 7 were waited for; matrix products, arithmetic and copies ran while one was open for 0% of the time, Pallas kernels for 19%

profile of v3, /device:TPU:1, one launch (start us, length us, event | category | flops | bytes accessed | tf_op | source)
XLA Modules:
  0.0 145.4 jit_solution(352321163753029656)
XLA Ops:
  0.6 0.9 copy-done
  1.6 1.3 prepare.1
  2.8 7.6 %all-to-all-start.2 = ((bf16[16,2,96,128]{3,2,1,0:T(8,128)(2,1)}), bf16[16,2,96,128]{3,2,1,0:T(8,128)(2,1)S(1)}, u32[]{:S(2)}, u32[]{:S(2)}) async-start(bf16[16,2,96,128]{3,2,1,0:T(8,128)(2,1)} %get-tuple-element.48), calls=%async_computation.2 | async-start | bytes 1572864 | tf_op jit(solution)/shard_map/all_to_all | solution.py:452
  10.6 13.1 %all-to-all-done.2.source_ref = bf16[16,2,96,128]{3,2,1,0:T(8,128)(2,1)S(1)} async-done(((bf16[16,2,96,128]{3,2,1,0:T(8,128)(2,1)}), bf16[16,2,96,128]{3,2,1,0:T(8,128)(2,1)S(1)}, u32[]{:S(2)}, u32[]{:S(2)}) %all-to-all-start.2) | async-done | bytes 786464 | tf_op jit(solution)/shard_map/all_to_all | solution.py:452
  23.6 3.7 %all-to-all-start = ((bf16[16,2,96,128]{3,2,1,0:T(8,128)(2,1)}), bf16[16,2,96,128]{3,2,1,0:T(8,128)(2,1)S(1)}, u32[]{:S(2)}, u32[]{:S(2)}) async-start(bf16[16,2,96,128]{3,2,1,0:T(8,128)(2,1)} %get-tuple-element.35), calls=%async_computation | async-start | bytes 1572864 | tf_op jit(solution)/shard_map/all_to_all | solution.py:452
  27.3 5.6 %shard_map.90 = (bf16[4,2,256,128]{3,2,1,0:T(8,128)(2,1)S(1)}, bf16[4,256,768]{2,1,0:T(8,128)(2,1)S(1)}, bf16[4,2,256,384]{3,2,1,0:T(8,128)(2,1)S(1)}) custom-call(s32[2]{0:T(128)S(1)} %pad_add_fusion.core_ref, s32[2,8,6]{2,1,0:T(8,128)S(1)} %copy.11.ranks_ref, bf16[16,2,96,128]{3,2,1,0:T(8,128)(2,1)S(1)} %all-to-all-done.2.source_ref, ...), custom_call_target="tpu_custom_call" | custom-call | flops 1207959552 | bytes 8000000 | tf_op jit(solution)/shard_map/pallas_call | solution.py:199
  32.9 2.2 %collective-permute-start.11 = (bf16[4,2,256,128]{3,2,1,0:T(8,128)(2,1)S(1)}, bf16[4,2,256,128]{3,2,1,0:T(8,128)(2,1)S(1)}, u32[]{:S(2)}, u32[]{:S(2)}) collective-permute-start(bf16[4,2,256,128]{3,2,1,0:T(8,128)(2,1)S(1)} %get-tuple-element.50), channel_id=1, source_target_pairs={{0,1},{1,0},{2,3},{3,2},{4,5},{5,4},{6,7},{7,6},{8,9},{9,8},{10,11... | collective-permute-start | bytes 1572872 | tf_op jit(solution)/shard_map/ppermute | solution.py:455
  35.2 1.5 %collective-permute-done.11.other_ref = bf16[4,2,256,128]{3,2,1,0:T(8,128)(2,1)S(1)} collective-permute-done((bf16[4,2,256,128]{3,2,1,0:T(8,128)(2,1)S(1)}, bf16[4,2,256,128]{3,2,1,0:T(8,128)(2,1)S(1)}, u32[]{:S(2)}, u32[]{:S(2)}) %collective-permute-start.11) | collective-permute-done | bytes 524320 | tf_op jit(solution)/shard_map/ppermute | solution.py:455
  36.7 0.6 shard_map.91
  37.3 1.7 %collective-permute-start.12 = (bf16[2,256,128]{2,1,0:T(8,128)(2,1)S(1)}, bf16[2,256,128]{2,1,0:T(8,128)(2,1)S(1)}, u32[]{:S(2)}, u32[]{:S(2)}) collective-permute-start(bf16[2,256,128]{2,1,0:T(8,128)(2,1)S(1)} %get-tuple-element.53), channel_id=1, source_target_pairs={{0,2},{2,4},{4,6},{6,0},{1,3},{3,5},{5,7},{7,1},{8,10},{10,12},{12... | collective-permute-start | bytes 393224 | tf_op jit(solution)/shard_map/ppermute | solution.py:458
  39.0 3.3 %collective-permute-start.13 = (bf16[2,256,128]{2,1,0:T(8,128)(2,1)S(1)}, bf16[2,256,128]{2,1,0:T(8,128)(2,1)S(1)}, u32[]{:S(2)}, u32[]{:S(2)}) collective-permute-start(bf16[2,256,128]{2,1,0:T(8,128)(2,1)S(1)} %get-tuple-element.54), channel_id=1, source_target_pairs={{0,4},{2,6},{4,0},{6,2},{1,5},{3,7},{5,1},{7,3},{8,12},{10,14},{12... | collective-permute-start | bytes 393224 | tf_op jit(solution)/shard_map/ppermute | solution.py:458
  42.3 0.7 collective-permute-start.14
  43.7 0.9 collective-permute-done.12.refs_0_
  44.7 3.7 %collective-permute-done.13.refs_1_ = bf16[2,256,128]{2,1,0:T(8,128)(2,1)S(1)} collective-permute-done((bf16[2,256,128]{2,1,0:T(8,128)(2,1)S(1)}, bf16[2,256,128]{2,1,0:T(8,128)(2,1)S(1)}, u32[]{:S(2)}, u32[]{:S(2)}) %collective-permute-start.13) | collective-permute-done | bytes 131104 | tf_op jit(solution)/shard_map/ppermute | solution.py:458
  48.5 2.3 %collective-permute-start.15 = (bf16[256,256]{1,0:T(8,128)(2,1)S(1)}, bf16[256,256]{1,0:T(8,128)(2,1)S(1)}, u32[]{:S(2)}, u32[]{:S(2)}) collective-permute-start(bf16[256,256]{1,0:T(8,128)(2,1)S(1)} %get-tuple-element.56.refs_0_), channel_id=1, source_target_pairs={{0,6},{2,0},{4,2},{6,4},{1,7},{3,1},{5,3},{7,5},{8,14},{10,8},{12,... | collective-permute-start | bytes 393224 | tf_op jit(solution)/shard_map/ppermute | solution.py:458
  50.8 0.9 collective-permute-start.16
  51.7 5.6 %shard_map.85 = (bf16[4,2,256,128]{3,2,1,0:T(8,128)(2,1)S(1)}, bf16[4,256,768]{2,1,0:T(8,128)(2,1)S(1)}, bf16[4,2,256,384]{3,2,1,0:T(8,128)(2,1)S(1)}) custom-call(s32[2]{0:T(128)S(1)} %pad_add_fusion.core_ref, s32[2,8,6]{2,1,0:T(8,128)S(1)} %copy.11.ranks_ref, bf16[16,2,96,128]{3,2,1,0:T(8,128)(2,1)S(1)} %all-to-all-done.source_ref, ...), custom_call_target="tpu_custom_call" | custom-call | flops 1207959552 | bytes 8000000 | tf_op jit(solution)/shard_map/pallas_call | solution.py:199
  57.3 1.2 copy-done.3
  58.5 1.2 copy-done.5
  59.7 1.8 %collective-permute-start = (bf16[4,2,256,128]{3,2,1,0:T(8,128)(2,1)S(1)}, bf16[4,2,256,128]{3,2,1,0:T(8,128)(2,1)S(1)}, u32[]{:S(2)}, u32[]{:S(2)}) collective-permute-start(bf16[4,2,256,128]{3,2,1,0:T(8,128)(2,1)S(1)} %get-tuple-element.37), channel_id=1, source_target_pairs={{0,1},{1,0},{2,3},{3,2},{4,5},{5,4},{6,7},{7,6},{8,9},{9,8},{10,11... | collective-permute-start | bytes 1572872 | tf_op jit(solution)/shard_map/ppermute | solution.py:455
  61.4 0.5 collective-permute-start.19
  62.0 0.4 collective-permute-start.21
  62.4 3.6 %shard_map.93 = (bf16[4,256,384]{2,1,0:T(8,128)(2,1)S(1)}, bf16[6,2,256,512]{3,2,1,0:T(8,128)(2,1)S(1)}, bf16[4,2,256,384]{3,2,1,0:T(8,128)(2,1)S(1)}) custom-call(s32[2]{0:T(128)S(1)} %pad_add_fusion.core_ref, s32[2,8,6]{2,1,0:T(8,128)S(1)} %copy.11.ranks_ref, bf16[2,2,1536,512]{3,2,1,0:T(8,128)(2,1)} %right_ref.7, bf16[2,2,2048,384]{3,2,1,0:T(8,128)(2,1)} %left_ref.7, ...), custom_call_target="tpu_custom_call" | custom-call | flops 402653184 | bytes 8000000 | tf_op jit(solution)/shard_map/pallas_call | solution.py:271
  66.1 3.6 %shard_map.94 = bf16[16,2,96,128]{3,2,1,0:T(8,128)(2,1)} custom-call(s32[2]{0:T(128)S(1)} %pad_add_fusion.core_ref, s32[2,8,6]{2,1,0:T(8,128)S(1)} %copy.11.ranks_ref, bf16[4,256,384]{2,1,0:T(8,128)(2,1)S(1)} %get-tuple-element.57.near_ref, bf16[6,2,256,512]{3,2,1,0:T(8,128)(2,1)S(1)} %get-tuple-element.58.right_ref, ...), custom_call_target="tpu_custom_call" | custom-call | flops 1207959552 | bytes 8000000 | tf_op jit(solution)/shard_map/pallas_call | solution.py:322
  69.7 6.9 %all-to-all-start.3 = ((bf16[16,2,96,128]{3,2,1,0:T(8,128)(2,1)}), bf16[16,2,96,128]{3,2,1,0:T(8,128)(2,1)S(1)}, u32[]{:S(2)}, u32[]{:S(2)}) async-start(bf16[16,2,96,128]{3,2,1,0:T(8,128)(2,1)} %shard_map.94), calls=%async_computation.3 | async-start | bytes 1572864 | tf_op jit(solution)/shard_map/all_to_all | solution.py:452
  76.6 1.4 copy-done.4
  78.0 1.4 copy-done.6
  79.4 0.6 shard_map.86
  80.0 1.8 %collective-permute-start.1 = (bf16[2,256,128]{2,1,0:T(8,128)(2,1)S(1)}, bf16[2,256,128]{2,1,0:T(8,128)(2,1)S(1)}, u32[]{:S(2)}, u32[]{:S(2)}) collective-permute-start(bf16[2,256,128]{2,1,0:T(8,128)(2,1)S(1)} %get-tuple-element.40), channel_id=1, source_target_pairs={{0,2},{2,4},{4,6},{6,0},{1,3},{3,5},{5,7},{7,1},{8,10},{10,12},{12... | collective-permute-start | bytes 393224 | tf_op jit(solution)/shard_map/ppermute | solution.py:458
  81.8 2.1 %collective-permute-start.2 = (bf16[2,256,128]{2,1,0:T(8,128)(2,1)S(1)}, bf16[2,256,128]{2,1,0:T(8,128)(2,1)S(1)}, u32[]{:S(2)}, u32[]{:S(2)}) collective-permute-start(bf16[2,256,128]{2,1,0:T(8,128)(2,1)S(1)} %get-tuple-element.41), channel_id=1, source_target_pairs={{0,4},{2,6},{4,0},{6,2},{1,5},{3,7},{5,1},{7,3},{8,12},{10,14},{12... | collective-permute-start | bytes 393224 | tf_op jit(solution)/shard_map/ppermute | solution.py:458
  83.9 0.5 collective-permute-start.3
  84.4 1.4 collective-permute-done.1.refs_0_
  85.8 3.9 %collective-permute-done.2.refs_1_ = bf16[2,256,128]{2,1,0:T(8,128)(2,1)S(1)} collective-permute-done((bf16[2,256,128]{2,1,0:T(8,128)(2,1)S(1)}, bf16[2,256,128]{2,1,0:T(8,128)(2,1)S(1)}, u32[]{:S(2)}, u32[]{:S(2)}) %collective-permute-start.2) | collective-permute-done | bytes 131104 | tf_op jit(solution)/shard_map/ppermute | solution.py:458
  89.9 1.8 %collective-permute-start.6 = (bf16[256,256]{1,0:T(8,128)(2,1)S(1)}, bf16[256,256]{1,0:T(8,128)(2,1)S(1)}, u32[]{:S(2)}, u32[]{:S(2)}) collective-permute-start(bf16[256,256]{1,0:T(8,128)(2,1)S(1)} %get-tuple-element.43.refs_0_), channel_id=1, source_target_pairs={{0,2},{2,4},{4,6},{6,0},{1,3},{3,5},{5,7},{7,1},{8,10},{10,12},{12... | collective-permute-start | bytes 393224 | tf_op jit(solution)/shard_map/ppermute | solution.py:458
  91.7 1.0 collective-permute-start.4
  92.6 0.9 collective-permute-start.5
  93.6 1.8 %collective-permute-start.7 = (bf16[256,256]{1,0:T(8,128)(2,1)S(1)}, bf16[256,256]{1,0:T(8,128)(2,1)S(1)}, u32[]{:S(2)}, u32[]{:S(2)}) collective-permute-start(bf16[256,256]{1,0:T(8,128)(2,1)S(1)} %get-tuple-element.43.refs_0_), channel_id=1, source_target_pairs={{0,1},{1,0},{2,3},{3,2},{4,5},{5,4},{6,7},{7,6},{8,9},{9,8},{10,11... | collective-permute-start | bytes 393224 | tf_op jit(solution)/shard_map/ppermute | solution.py:455
  95.4 2.4 %collective-permute-start.10 = (bf16[256,256]{1,0:T(8,128)(2,1)S(1)}, bf16[256,256]{1,0:T(8,128)(2,1)S(1)}, u32[]{:S(2)}, u32[]{:S(2)}) collective-permute-start(bf16[256,256]{1,0:T(8,128)(2,1)S(1)} %collective-permute-done.6.refs_3_), channel_id=1, source_target_pairs={{0,1},{1,0},{2,3},{3,2},{4,5},{5,4},{6,7},{7,6},{8,9},{9,8},{10,11... | collective-permute-start | bytes 393224 | tf_op jit(solution)/shard_map/ppermute | solution.py:455
  97.8 1.1 collective-permute-start.8
  99.0 2.1 %collective-permute-start.9 = (bf16[256,256]{1,0:T(8,128)(2,1)S(1)}, bf16[256,256]{1,0:T(8,128)(2,1)S(1)}, u32[]{:S(2)}, u32[]{:S(2)}) collective-permute-start(bf16[256,256]{1,0:T(8,128)(2,1)S(1)} %collective-permute-done.5.refs_2_), channel_id=1, source_target_pairs={{0,1},{1,0},{2,3},{3,2},{4,5},{5,4},{6,7},{7,6},{8,9},{9,8},{10,11... | collective-permute-start | bytes 393224 | tf_op jit(solution)/shard_map/ppermute | solution.py:455
  101.1 3.6 %shard_map.88 = (bf16[4,256,384]{2,1,0:T(8,128)(2,1)S(1)}, bf16[6,2,256,512]{3,2,1,0:T(8,128)(2,1)S(1)}, bf16[4,2,256,384]{3,2,1,0:T(8,128)(2,1)S(1)}) custom-call(s32[2]{0:T(128)S(1)} %pad_add_fusion.core_ref, s32[2,8,6]{2,1,0:T(8,128)S(1)} %copy.11.ranks_ref, bf16[2,2,1536,512]{3,2,1,0:T(8,128)(2,1)} %right_ref.7, bf16[2,2,2048,384]{3,2,1,0:T(8,128)(2,1)} %left_ref.7, ...), custom_call_target="tpu_custom_call" | custom-call | flops 402653184 | bytes 8000000 | tf_op jit(solution)/shard_map/pallas_call | solution.py:271
  104.7 3.6 %shard_map.89 = bf16[16,2,96,128]{3,2,1,0:T(8,128)(2,1)} custom-call(s32[2]{0:T(128)S(1)} %pad_add_fusion.core_ref, s32[2,8,6]{2,1,0:T(8,128)S(1)} %copy.11.ranks_ref, bf16[4,256,384]{2,1,0:T(8,128)(2,1)S(1)} %get-tuple-element.44.near_ref, bf16[6,2,256,512]{3,2,1,0:T(8,128)(2,1)S(1)} %get-tuple-element.45.right_ref, ...), custom_call_target="tpu_custom_call" | custom-call | flops 1207959552 | bytes 8000000 | tf_op jit(solution)/shard_map/pallas_call | solution.py:322
  108.4 6.8 %all-to-all-start.1 = ((bf16[16,2,96,128]{3,2,1,0:T(8,128)(2,1)}), bf16[16,2,96,128]{3,2,1,0:T(8,128)(2,1)S(1)}, u32[]{:S(2)}, u32[]{:S(2)}) async-start(bf16[16,2,96,128]{3,2,1,0:T(8,128)(2,1)} %shard_map.89), calls=%async_computation.1 | async-start | bytes 1572864 | tf_op jit(solution)/shard_map/all_to_all | solution.py:452
  115.2 0.2 shard_map.95
  115.4 13.6 %all-to-all-done.1.partial_ref = bf16[16,2,96,128]{3,2,1,0:T(8,128)(2,1)S(1)} async-done(((bf16[16,2,96,128]{3,2,1,0:T(8,128)(2,1)}), bf16[16,2,96,128]{3,2,1,0:T(8,128)(2,1)S(1)}, u32[]{:S(2)}, u32[]{:S(2)}) %all-to-all-start.1) | async-done | bytes 786464 | tf_op jit(solution)/shard_map/all_to_all | solution.py:452
  129.1 0.2 shard_map.96
  129.3 14.8 %all_to_all.25.all_ref = f32[128,1,128]{2,1,0:T(1,128)S(1)} all-to-all(f32[128,1,128]{2,1,0:T(1,128)S(1)} %broadcast_in_dim.3), channel_id=1, replica_groups=mesh['trow_0'=4,'trow_1'=4,'tcol_0'=4,'tcol_1'=2] {'trow_0','trow_1','tc..., dimensions={0} | all-to-all | bytes 131072 | tf_op jit(solution)/shard_map/all_to_all | solution.py:452
  144.1 1.1 finish.1
  (38 shorter events, 0.7 us)
Async XLA Ops:
  0.6 0.9 copy-start
  1.6 8.8 %copy-start.7 = (s32[2,8,6]{1,0,2:T(2,128)S(1)}, s32[2,8,6]{1,0,2:T(2,128)}, u32[]{:S(2)}) copy-start(s32[2,8,6]{1,0,2:T(2,128)} %param.8) | copy-start | bytes 1156
  2.8 20.8 %all-to-all-start.2 = ((bf16[16,2,96,128]{3,2,1,0:T(8,128)(2,1)}), bf16[16,2,96,128]{3,2,1,0:T(8,128)(2,1)S(1)}, u32[]{:S(2)}, u32[]{:S(2)}) async-start(bf16[16,2,96,128]{3,2,1,0:T(8,128)(2,1)} %get-tuple-element.48), calls=%async_computation.2 | async-start | bytes 1572864 | tf_op jit(solution)/shard_map/all_to_all | solution.py:452
  23.6 28.1 %all-to-all-start = ((bf16[16,2,96,128]{3,2,1,0:T(8,128)(2,1)}), bf16[16,2,96,128]{3,2,1,0:T(8,128)(2,1)S(1)}, u32[]{:S(2)}, u32[]{:S(2)}) async-start(bf16[16,2,96,128]{3,2,1,0:T(8,128)(2,1)} %get-tuple-element.35), calls=%async_computation | async-start | bytes 1572864 | tf_op jit(solution)/shard_map/all_to_all | solution.py:452
  32.9 3.8 %collective-permute-start.11 = (bf16[4,2,256,128]{3,2,1,0:T(8,128)(2,1)S(1)}, bf16[4,2,256,128]{3,2,1,0:T(8,128)(2,1)S(1)}, u32[]{:S(2)}, u32[]{:S(2)}) collective-permute-start(bf16[4,2,256,128]{3,2,1,0:T(8,128)(2,1)S(1)} %get-tuple-element.50), channel_id=1, source_target_pairs={{0,1},{1,0},{2,3},{3,2},{4,5},{5,4},{6,7},{7,6},{8,9},{9,8},{10,11... | collective-permute-start | bytes 1572872 | tf_op jit(solution)/shard_map/ppermute | solution.py:455
  36.7 11.7 %copy-start.2 = (f32[2,2,256,128]{3,2,1,0:T(8,128)S(1)}, f32[2,2,256,128]{3,2,1,0:T(8,128)}, u32[]{:S(2)}) copy-start(f32[2,2,256,128]{3,2,1,0:T(8,128)} %u_prev_ref.3) | copy-start | bytes 1572868
  37.3 7.3 %collective-permute-start.12 = (bf16[2,256,128]{2,1,0:T(8,128)(2,1)S(1)}, bf16[2,256,128]{2,1,0:T(8,128)(2,1)S(1)}, u32[]{:S(2)}, u32[]{:S(2)}) collective-permute-start(bf16[2,256,128]{2,1,0:T(8,128)(2,1)S(1)} %get-tuple-element.53), channel_id=1, source_target_pairs={{0,2},{2,4},{4,6},{6,0},{1,3},{3,5},{5,7},{7,1},{8,10},{10,12},{12... | collective-permute-start | bytes 393224 | tf_op jit(solution)/shard_map/ppermute | solution.py:458
  39.0 9.3 %collective-permute-start.13 = (bf16[2,256,128]{2,1,0:T(8,128)(2,1)S(1)}, bf16[2,256,128]{2,1,0:T(8,128)(2,1)S(1)}, u32[]{:S(2)}, u32[]{:S(2)}) collective-permute-start(bf16[2,256,128]{2,1,0:T(8,128)(2,1)S(1)} %get-tuple-element.54), channel_id=1, source_target_pairs={{0,4},{2,6},{4,0},{6,2},{1,5},{3,7},{5,1},{7,3},{8,12},{10,14},{12... | collective-permute-start | bytes 393224 | tf_op jit(solution)/shard_map/ppermute | solution.py:458
  42.3 6.0 %collective-permute-start.14 = (bf16[2,256,128]{2,1,0:T(8,128)(2,1)S(1)}, bf16[2,256,128]{2,1,0:T(8,128)(2,1)S(1)}, u32[]{:S(2)}, u32[]{:S(2)}) collective-permute-start(bf16[2,256,128]{2,1,0:T(8,128)(2,1)S(1)} %get-tuple-element.55), channel_id=1, source_target_pairs={{0,6},{2,0},{4,2},{6,4},{1,7},{3,1},{5,3},{7,5},{8,14},{10,8},{12,... | collective-permute-start | bytes 393224 | tf_op jit(solution)/shard_map/ppermute | solution.py:458
  48.5 12.9 %collective-permute-start.15 = (bf16[256,256]{1,0:T(8,128)(2,1)S(1)}, bf16[256,256]{1,0:T(8,128)(2,1)S(1)}, u32[]{:S(2)}, u32[]{:S(2)}) collective-permute-start(bf16[256,256]{1,0:T(8,128)(2,1)S(1)} %get-tuple-element.56.refs_0_), channel_id=1, source_target_pairs={{0,6},{2,0},{4,2},{6,4},{1,7},{3,1},{5,3},{7,5},{8,14},{10,8},{12,... | collective-permute-start | bytes 393224 | tf_op jit(solution)/shard_map/ppermute | solution.py:458
  50.8 11.1 %collective-permute-start.16 = (bf16[256,256]{1,0:T(8,128)(2,1)S(1)}, bf16[256,256]{1,0:T(8,128)(2,1)S(1)}, u32[]{:S(2)}, u32[]{:S(2)}) collective-permute-start(bf16[256,256]{1,0:T(8,128)(2,1)S(1)} %get-tuple-element.56.refs_0_), channel_id=1, source_target_pairs={{0,4},{2,6},{4,0},{6,2},{1,5},{3,7},{5,1},{7,3},{8,12},{10,14},{12... | collective-permute-start | bytes 393224 | tf_op jit(solution)/shard_map/ppermute | solution.py:458
  51.7 10.3 %collective-permute-start.17 = (bf16[256,256]{1,0:T(8,128)(2,1)S(1)}, bf16[256,256]{1,0:T(8,128)(2,1)S(1)}, u32[]{:S(2)}, u32[]{:S(2)}) collective-permute-start(bf16[256,256]{1,0:T(8,128)(2,1)S(1)} %get-tuple-element.56.refs_0_), channel_id=1, source_target_pairs={{0,2},{2,4},{4,6},{6,0},{1,3},{3,5},{5,7},{7,1},{8,10},{10,12},{12... | collective-permute-start | bytes 393224 | tf_op jit(solution)/shard_map/ppermute | solution.py:458
  57.3 1.2 copy-start.3
  58.5 1.2 copy-start.5
  59.7 16.9 %collective-permute-start = (bf16[4,2,256,128]{3,2,1,0:T(8,128)(2,1)S(1)}, bf16[4,2,256,128]{3,2,1,0:T(8,128)(2,1)S(1)}, u32[]{:S(2)}, u32[]{:S(2)}) collective-permute-start(bf16[4,2,256,128]{3,2,1,0:T(8,128)(2,1)S(1)} %get-tuple-element.37), channel_id=1, source_target_pairs={{0,1},{1,0},{2,3},{3,2},{4,5},{5,4},{6,7},{7,6},{8,9},{9,8},{10,11... | collective-permute-start | bytes 1572872 | tf_op jit(solution)/shard_map/ppermute | solution.py:455
  61.4 4.7 %collective-permute-start.18 = (bf16[256,256]{1,0:T(8,128)(2,1)S(1)}, bf16[256,256]{1,0:T(8,128)(2,1)S(1)}, u32[]{:S(2)}, u32[]{:S(2)}) collective-permute-start(bf16[256,256]{1,0:T(8,128)(2,1)S(1)} %get-tuple-element.56.refs_0_), channel_id=1, source_target_pairs={{0,1},{1,0},{2,3},{3,2},{4,5},{5,4},{6,7},{7,6},{8,9},{9,8},{10,11... | collective-permute-start | bytes 393224 | tf_op jit(solution)/shard_map/ppermute | solution.py:455
  61.4 4.7 %collective-permute-start.19 = (bf16[256,256]{1,0:T(8,128)(2,1)S(1)}, bf16[256,256]{1,0:T(8,128)(2,1)S(1)}, u32[]{:S(2)}, u32[]{:S(2)}) collective-permute-start(bf16[256,256]{1,0:T(8,128)(2,1)S(1)} %collective-permute-done.15.refs_1_), channel_id=1, source_target_pairs={{0,1},{1,0},{2,3},{3,2},{4,5},{5,4},{6,7},{7,6},{8,9},{9,8},{10,11... | collective-permute-start | bytes 393224 | tf_op jit(solution)/shard_map/ppermute | solution.py:455
  61.9 4.2 %collective-permute-start.20 = (bf16[256,256]{1,0:T(8,128)(2,1)S(1)}, bf16[256,256]{1,0:T(8,128)(2,1)S(1)}, u32[]{:S(2)}, u32[]{:S(2)}) collective-permute-start(bf16[256,256]{1,0:T(8,128)(2,1)S(1)} %collective-permute-done.16.refs_2_), channel_id=1, source_target_pairs={{0,1},{1,0},{2,3},{3,2},{4,5},{5,4},{6,7},{7,6},{8,9},{9,8},{10,11... | collective-permute-start | bytes 393224 | tf_op jit(solution)/shard_map/ppermute | solution.py:455
  62.0 4.1 %collective-permute-start.21 = (bf16[256,256]{1,0:T(8,128)(2,1)S(1)}, bf16[256,256]{1,0:T(8,128)(2,1)S(1)}, u32[]{:S(2)}, u32[]{:S(2)}) collective-permute-start(bf16[256,256]{1,0:T(8,128)(2,1)S(1)} %collective-permute-done.17.refs_3_), channel_id=1, source_target_pairs={{0,1},{1,0},{2,3},{3,2},{4,5},{5,4},{6,7},{7,6},{8,9},{9,8},{10,11... | collective-permute-start | bytes 393224 | tf_op jit(solution)/shard_map/ppermute | solution.py:455
  69.7 38.7 %all-to-all-start.3 = ((bf16[16,2,96,128]{3,2,1,0:T(8,128)(2,1)}), bf16[16,2,96,128]{3,2,1,0:T(8,128)(2,1)S(1)}, u32[]{:S(2)}, u32[]{:S(2)}) async-start(bf16[16,2,96,128]{3,2,1,0:T(8,128)(2,1)} %shard_map.94), calls=%async_computation.3 | async-start | bytes 1572864 | tf_op jit(solution)/shard_map/all_to_all | solution.py:452
  76.6 1.4 copy-start.4
  78.0 1.4 copy-start.6
  80.0 5.8 %collective-permute-start.1 = (bf16[2,256,128]{2,1,0:T(8,128)(2,1)S(1)}, bf16[2,256,128]{2,1,0:T(8,128)(2,1)S(1)}, u32[]{:S(2)}, u32[]{:S(2)}) collective-permute-start(bf16[2,256,128]{2,1,0:T(8,128)(2,1)S(1)} %get-tuple-element.40), channel_id=1, source_target_pairs={{0,2},{2,4},{4,6},{6,0},{1,3},{3,5},{5,7},{7,1},{8,10},{10,12},{12... | collective-permute-start | bytes 393224 | tf_op jit(solution)/shard_map/ppermute | solution.py:458
  81.8 7.9 %collective-permute-start.2 = (bf16[2,256,128]{2,1,0:T(8,128)(2,1)S(1)}, bf16[2,256,128]{2,1,0:T(8,128)(2,1)S(1)}, u32[]{:S(2)}, u32[]{:S(2)}) collective-permute-start(bf16[2,256,128]{2,1,0:T(8,128)(2,1)S(1)} %get-tuple-element.41), channel_id=1, source_target_pairs={{0,4},{2,6},{4,0},{6,2},{1,5},{3,7},{5,1},{7,3},{8,12},{10,14},{12... | collective-permute-start | bytes 393224 | tf_op jit(solution)/shard_map/ppermute | solution.py:458
  83.9 5.9 %collective-permute-start.3 = (bf16[2,256,128]{2,1,0:T(8,128)(2,1)S(1)}, bf16[2,256,128]{2,1,0:T(8,128)(2,1)S(1)}, u32[]{:S(2)}, u32[]{:S(2)}) collective-permute-start(bf16[2,256,128]{2,1,0:T(8,128)(2,1)S(1)} %get-tuple-element.42), channel_id=1, source_target_pairs={{0,6},{2,0},{4,2},{6,4},{1,7},{3,1},{5,3},{7,5},{8,14},{10,8},{12,... | collective-permute-start | bytes 393224 | tf_op jit(solution)/shard_map/ppermute | solution.py:458
  89.9 5.5 %collective-permute-start.6 = (bf16[256,256]{1,0:T(8,128)(2,1)S(1)}, bf16[256,256]{1,0:T(8,128)(2,1)S(1)}, u32[]{:S(2)}, u32[]{:S(2)}) collective-permute-start(bf16[256,256]{1,0:T(8,128)(2,1)S(1)} %get-tuple-element.43.refs_0_), channel_id=1, source_target_pairs={{0,2},{2,4},{4,6},{6,0},{1,3},{3,5},{5,7},{7,1},{8,10},{10,12},{12... | collective-permute-start | bytes 393224 | tf_op jit(solution)/shard_map/ppermute | solution.py:458
  91.7 6.2 %collective-permute-start.4 = (bf16[256,256]{1,0:T(8,128)(2,1)S(1)}, bf16[256,256]{1,0:T(8,128)(2,1)S(1)}, u32[]{:S(2)}, u32[]{:S(2)}) collective-permute-start(bf16[256,256]{1,0:T(8,128)(2,1)S(1)} %get-tuple-element.43.refs_0_), channel_id=1, source_target_pairs={{0,6},{2,0},{4,2},{6,4},{1,7},{3,1},{5,3},{7,5},{8,14},{10,8},{12,... | collective-permute-start | bytes 393224 | tf_op jit(solution)/shard_map/ppermute | solution.py:458
  92.6 6.3 %collective-permute-start.5 = (bf16[256,256]{1,0:T(8,128)(2,1)S(1)}, bf16[256,256]{1,0:T(8,128)(2,1)S(1)}, u32[]{:S(2)}, u32[]{:S(2)}) collective-permute-start(bf16[256,256]{1,0:T(8,128)(2,1)S(1)} %get-tuple-element.43.refs_0_), channel_id=1, source_target_pairs={{0,4},{2,6},{4,0},{6,2},{1,5},{3,7},{5,1},{7,3},{8,12},{10,14},{12... | collective-permute-start | bytes 393224 | tf_op jit(solution)/shard_map/ppermute | solution.py:458
  93.6 11.1 %collective-permute-start.7 = (bf16[256,256]{1,0:T(8,128)(2,1)S(1)}, bf16[256,256]{1,0:T(8,128)(2,1)S(1)}, u32[]{:S(2)}, u32[]{:S(2)}) collective-permute-start(bf16[256,256]{1,0:T(8,128)(2,1)S(1)} %get-tuple-element.43.refs_0_), channel_id=1, source_target_pairs={{0,1},{1,0},{2,3},{3,2},{4,5},{5,4},{6,7},{7,6},{8,9},{9,8},{10,11... | collective-permute-start | bytes 393224 | tf_op jit(solution)/shard_map/ppermute | solution.py:455
  95.4 9.3 %collective-permute-start.10 = (bf16[256,256]{1,0:T(8,128)(2,1)S(1)}, bf16[256,256]{1,0:T(8,128)(2,1)S(1)}, u32[]{:S(2)}, u32[]{:S(2)}) collective-permute-start(bf16[256,256]{1,0:T(8,128)(2,1)S(1)} %collective-permute-done.6.refs_3_), channel_id=1, source_target_pairs={{0,1},{1,0},{2,3},{3,2},{4,5},{5,4},{6,7},{7,6},{8,9},{9,8},{10,11... | collective-permute-start | bytes 393224 | tf_op jit(solution)/shard_map/ppermute | solution.py:455
  97.8 6.9 %collective-permute-start.8 = (bf16[256,256]{1,0:T(8,128)(2,1)S(1)}, bf16[256,256]{1,0:T(8,128)(2,1)S(1)}, u32[]{:S(2)}, u32[]{:S(2)}) collective-permute-start(bf16[256,256]{1,0:T(8,128)(2,1)S(1)} %collective-permute-done.4.refs_1_), channel_id=1, source_target_pairs={{0,1},{1,0},{2,3},{3,2},{4,5},{5,4},{6,7},{7,6},{8,9},{9,8},{10,11... | collective-permute-start | bytes 393224 | tf_op jit(solution)/shard_map/ppermute | solution.py:455
  99.0 5.8 %collective-permute-start.9 = (bf16[256,256]{1,0:T(8,128)(2,1)S(1)}, bf16[256,256]{1,0:T(8,128)(2,1)S(1)}, u32[]{:S(2)}, u32[]{:S(2)}) collective-permute-start(bf16[256,256]{1,0:T(8,128)(2,1)S(1)} %collective-permute-done.5.refs_2_), channel_id=1, source_target_pairs={{0,1},{1,0},{2,3},{3,2},{4,5},{5,4},{6,7},{7,6},{8,9},{9,8},{10,11... | collective-permute-start | bytes 393224 | tf_op jit(solution)/shard_map/ppermute | solution.py:455
  108.4 6.8 %copy-start.1 = (f32[2,2,96,128]{3,2,1,0:T(8,128)S(1)}, f32[2,2,96,128]{3,2,1,0:T(8,128)}, u32[]{:S(2)}) copy-start(f32[2,2,96,128]{3,2,1,0:T(8,128)} %v_ref.7) | copy-start | bytes 589828
  108.4 20.7 %all-to-all-start.1 = ((bf16[16,2,96,128]{3,2,1,0:T(8,128)(2,1)}), bf16[16,2,96,128]{3,2,1,0:T(8,128)(2,1)S(1)}, u32[]{:S(2)}, u32[]{:S(2)}) async-start(bf16[16,2,96,128]{3,2,1,0:T(8,128)(2,1)} %shard_map.89), calls=%async_computation.1 | async-start | bytes 1572864 | tf_op jit(solution)/shard_map/all_to_all | solution.py:452

commit v4 on v3

v4 whole, which is shorter than its diff:
```python
import functools

import jax
import jax.numpy as jnp
from jax import lax
from jax.experimental import pallas as pl
from jax.experimental.pallas import tpu as pltpu
from jax.sharding import Mesh
from jax.sharding import PartitionSpec as P


TROW = ("trow_0", "trow_1")
TCOL = ("tcol_0", "tcol_1")
TROW_TCOL = ("trow_0", "trow_1", "tcol_0", "tcol_1")
TCOL_TROW = ("tcol_0", "tcol_1", "trow_0", "trow_1")

epsilon = 1e-06
BF = jnp.bfloat16
F32 = jnp.float32
VMEM = pltpu.MemorySpace.VMEM
SMEM = pltpu.MemorySpace.SMEM
HBM = pltpu.MemorySpace.HBM


def spec(space):
    return pl.BlockSpec(memory_space=space)


def in_hbm(value):
    return pltpu.with_memory_space_constraint(value, HBM)


def params(mib=16):
    return pltpu.CompilerParams(vmem_limit_bytes=mib * 1024 * 1024)


def rank_lanes(ranks_of, count, width, rank_full):
    lane = lax.broadcasted_iota(jnp.int32, (8, width), 1)
    limit = jnp.full((8, width), ranks_of(0), jnp.int32)
    for tile in range(1, count):
        limit = jnp.where(lane >= tile * rank_full, ranks_of(tile) + tile * rank_full, limit)
    return (lane < limit)[:1]


def conjugated(stacked, real, imag, half):
    a = jnp.dot(stacked, real, preferred_element_type=F32)
    b = jnp.dot(stacked, imag, preferred_element_type=F32)
    return a[:half] + b[half:], a[half:] - b[:half]


def regroup(first, second, rank_full):
    even = jnp.concatenate([first[:, :rank_full], second[:, :rank_full]], axis=1)
    odd = jnp.concatenate([first[:, rank_full:], second[:, rank_full:]], axis=1)
    return even, odd


def turned(block, half):
    return jnp.concatenate([-block[half:], block[:half]], axis=0)


def prepare_kernel(v_ref, *out_refs):
    for f, ref in enumerate(out_refs):
        ref[...] = v_ref[f].astype(BF)


def prepare(v):
    frequencies = v.shape[0]
    return pl.pallas_call(
        prepare_kernel,
        out_shape=(jax.ShapeDtypeStruct(v.shape[1:], BF),) * frequencies,
        in_specs=[spec(VMEM)],
        out_specs=(spec(VMEM),) * frequencies,
        compiler_params=params(4),
        cost_estimate=pl.CostEstimate(flops=v.size, bytes_accessed=v.size * 6, transcendentals=0),
        name="prepare",
    )(v)


def pack_kernel(axis, *refs):
    parts, out_ref = refs[:-1], refs[-1]
    me = lax.axis_index(axis)
    for d, ref in enumerate(parts):
        out_ref[lax.rem(me + d, len(parts))] = ref[...]


def pack(axis, parts):
    return pl.pallas_call(
        functools.partial(pack_kernel, axis),
        out_shape=jax.ShapeDtypeStruct((len(parts), *parts[0].shape), BF),
        in_specs=[spec(VMEM)] * len(parts),
        out_specs=spec(VMEM),
        compiler_params=params(4),
        cost_estimate=pl.CostEstimate(flops=parts[0].size, bytes_accessed=parts[0].size * 16, transcendentals=0),
    )(*parts)


def load_kernel(*refs):
    factor_ref, outs, sem = refs[-4], refs[-3:-1], refs[-1]
    wait_all(run_all([pltpu.make_async_copy(factor_ref.at[f], out, sem.at[f]) for f, out in enumerate(outs)]))


def load(factor, after=()):
    shape = jax.ShapeDtypeStruct(factor.shape[1:], BF)
    return pl.pallas_call(
        load_kernel,
        out_shape=(shape,) * 2,
        in_specs=[spec(SMEM)] * len(after) + [spec(HBM)],
        out_specs=(spec(VMEM),) * 2,
        scratch_shapes=[pltpu.SemaphoreType.DMA((2,))],
        compiler_params=params(2),
        cost_estimate=pl.CostEstimate(flops=1000000, bytes_accessed=factor.size * 4, transcendentals=0),
    )(*after, in_hbm(factor))


def run_all(copies):
    for copy in copies:
        copy.start()
    return copies


def wait_all(copies):
    for copy in copies:
        copy.wait()


def sides(half):
    z, c = lax.axis_index("tcol_0"), lax.axis_index("tcol_1")
    chips = [2 * lax.rem(z + d, half) for d in range(half)]
    return [chip + c for chip in chips], [chip + (1 - c) for chip in chips]


def tile_of(factor_ref, index, tile):
    at = pl.ds(pl.multiple_of(index * tile, tile), tile)
    return factor_ref[0, at, :], factor_ref[1, at, :]


def expanded(factor, grouped):
    both = jnp.concatenate(factor, axis=1)
    return lax.dot_general(both, grouped, (((1,), (1,)), ((), ())), preferred_element_type=F32)


def masked(kept, real, imag):
    return jnp.where(kept, real, 0.0).astype(BF), jnp.where(kept, imag, 0.0).astype(BF)


def regroup_all(blocks, grouped, outer, inner, rank_full, nv):
    wide = outer * rank_full
    pair = 2 * rank_full
    for o in range(0, outer, 2):
        for i in range(0, inner, 2):
            lanes = slice(i * rank_full, i * rank_full + pair)
            even, odd = regroup(blocks[o, :, lanes], blocks[o + 1, :, lanes], rank_full)
            at = o * rank_full
            for n, block in enumerate((even, odd)):
                grouped[i + n, :, at : at + pair] = block
                grouped[i + n, :, wide + at : wide + at + pair] = turned(block, nv)


def project_kernel(f, dims, axes, ranks_ref, packed_ref, *refs):
    tile, rank_full, rows, cols, nv, share, _ = dims
    arrived, (right_ref, left_ref, send_ref, kept_ref, stored, proj, grouped) = refs[:-7], refs[-7:]
    near, far = sides(rows // 2)
    side = 1 + len(arrived)
    me = lax.axis_index(axes[1])
    for e, ref in enumerate((packed_ref, *arrived)):
        other = lax.rem(me + e, side)
        for n in range(side):
            r = n * side + other if axes[1] == TROW[1] else other * side + n
            at = pl.ds(pl.multiple_of(r * share, share), share)
            for part in range(2):
                stored[part, at, :] = ref[n, part]
    for j in range(cols):
        at = slice(j * tile, (j + 1) * tile)
        stacked = jnp.concatenate([stored[0, at].T, stored[1, at].T], axis=0)
        real, imag = conjugated(stacked, right_ref[0, at, :], right_ref[1, at, :], nv)
        kept = rank_lanes(lambda i: ranks_ref[j, f, i], rows, rows * rank_full, rank_full)
        proj[j, :nv], proj[j, nv:] = masked(kept, real, imag)
    regroup_all(proj, grouped, cols, rows, rank_full, nv)
    for d in range(rows // 2):
        out = expanded(tile_of(left_ref, far[d], tile), grouped[far[d]])
        send_ref[d, 0] = out[:, :nv]
        send_ref[d, 1] = out[:, nv:]
        kept_ref[d] = grouped[near[d]]


def project(f, ranks, axes, packed, arrived, right, left, dims):
    tile, rank_full, rows, cols, nv, _, _ = dims
    half = rows // 2
    return pl.pallas_call(
        functools.partial(project_kernel, f, dims, axes),
        out_shape=(
            jax.ShapeDtypeStruct((half, 2, tile, nv), F32),
            jax.ShapeDtypeStruct((half, 2 * nv, 2 * cols * rank_full), BF),
        ),
        in_specs=[spec(SMEM)] + [spec(VMEM)] * (3 + len(arrived)),
        out_specs=(spec(VMEM),) * 2,
        scratch_shapes=[
            pltpu.VMEM((2, cols * tile, nv), BF),
            pltpu.VMEM((cols, 2 * nv, rows * rank_full), BF),
            pltpu.VMEM((rows, 2 * nv, 2 * cols * rank_full), BF),
        ],
        compiler_params=params(14),
        cost_estimate=pl.CostEstimate(
            flops=12 * rows * cols * tile * rank_full * nv, bytes_accessed=8_000_000, transcendentals=0
        ),
    )(ranks, packed, *arrived, right, left)


def expand_kernel(dims, kept_ref, other_ref, left_ref, own_ref, *piece_refs):
    tile, nv, half = dims[0], dims[4], dims[2] // 2
    near, _ = sides(half)
    for d in list(range(1, half)) + [0]:
        out = expanded(tile_of(left_ref, near[d], tile), kept_ref[d])
        for part in range(2):
            total = out[:, part * nv : (part + 1) * nv] + other_ref[d, part]
            if d == 0:
                own_ref[part] = total
            else:
                piece_refs[d - 1][part] = total.astype(BF)


def expand(kept, other, left, dims):
    tile, rank_full, rows, cols, nv, _, _ = dims
    half = rows // 2
    piece = (2, tile, nv)
    return pl.pallas_call(
        functools.partial(expand_kernel, dims),
        out_shape=(jax.ShapeDtypeStruct(piece, F32),)
        + (jax.ShapeDtypeStruct(piece, BF),) * (half - 1),
        in_specs=[spec(VMEM)] * 3,
        out_specs=(spec(VMEM),) * half,
        compiler_params=params(),
        cost_estimate=pl.CostEstimate(
            flops=4 * rows * cols * tile * rank_full * nv, bytes_accessed=4_000_000, transcendentals=0
        ),
    )(kept, other, left)


def back_of(f, index, target, left_ref, ranks_ref, dims):
    tile, rank_full, _, cols, nv, _, _ = dims
    real, imag = conjugated(target, *tile_of(left_ref, index, tile), nv)
    kept = rank_lanes(lambda j: ranks_ref[j, f, index], cols, cols * rank_full, rank_full)
    whole = [jnp.where(kept, value, 0.0) for value in (real, imag)]
    lead = [value.astype(BF) for value in whole]
    rest = [(value - top.astype(F32)).astype(BF) for value, top in zip(whole, lead)]
    return lead, rest


def near_kernel(f, dims, ranks_ref, left_ref, *refs):
    nv, half = dims[4], dims[2] // 2
    targets, back_ref = refs[:-1], refs[-1]
    near, _ = sides(half)
    for d in range(half):
        for term, parts in enumerate(back_of(f, near[d], targets[d][...], left_ref, ranks_ref, dims)):
            back_ref[term, d, :nv], back_ref[term, d, nv:] = parts


def near_back(f, ranks, targets, left, dims):
    tile, rank_full, rows, cols, nv, _, _ = dims
    half = rows // 2
    return pl.pallas_call(
        functools.partial(near_kernel, f, dims),
        out_shape=jax.ShapeDtypeStruct((2, half, 2 * nv, cols * rank_full), BF),
        in_specs=[spec(SMEM), spec(VMEM)] + [spec(VMEM)] * half,
        out_specs=spec(VMEM),
        compiler_params=params(8),
        cost_estimate=pl.CostEstimate(
            flops=4 * rows * cols * tile * rank_full * nv, bytes_accessed=4_000_000, transcendentals=0
        ),
    )(ranks, left, *targets)


def place(axes, along_first, along_second, side):
    if axes[0] == TROW[0]:
        return along_first * side + along_second
    return along_second * side + along_first


def adjoint_kernel(f, dims, axes, side, ranks_ref, near_ref, right_ref, left_ref, *refs):
    tile, rank_full, rows, cols, nv, share, _ = dims
    half = rows // 2
    targets, piece_refs, (back, grouped, out_ref) = refs[:half], refs[half:-3], refs[-3:]
    near, far = sides(half)
    for d in range(half):
        for term, parts in enumerate(back_of(f, far[d], targets[d][...], left_ref, ranks_ref, dims)):
            back[term, near[d]] = near_ref[term, d]
            back[term, far[d], :nv], back[term, far[d], nv:] = parts
    for term in range(2):
        regroup_all(back.at[term], grouped.at[term], rows, cols, rank_full, nv)
    for j in range(cols):
        factor = tile_of(right_ref, j, tile)
        out = (expanded(factor, grouped[0, j]) + expanded(factor, grouped[1, j])).astype(BF)
        row = 0
        while row < tile:
            r, start = divmod(j * tile + row, share)
            count = min(share - start, tile - row)
            for part in range(2):
                piece = out[row : row + count, part * nv : (part + 1) * nv]
                out_ref[r, part, start : start + count] = piece
            row += count
    me = lax.axis_index(axes[0])
    for d, ref in enumerate(piece_refs):
        for n in range(side):
            ref[n] = out_ref[place(axes, lax.rem(me + d, side), n, side)]


def adjoint(f, ranks, axes, near, right, left, targets, dims):
    tile, rank_full, rows, cols, nv, share, peers = dims
    side = lax.axis_size(axes[0])
    return pl.pallas_call(
        functools.partial(adjoint_kernel, f, dims, axes, side),
        out_shape=(jax.ShapeDtypeStruct((peers // side, 2, share, nv), BF),) * side,
        in_specs=[spec(SMEM)] + [spec(VMEM)] * (3 + len(targets)),
        out_specs=(spec(VMEM),) * side,
        scratch_shapes=[
            pltpu.VMEM((2, rows, 2 * nv, cols * rank_full), BF),
            pltpu.VMEM((2, cols, 2 * nv, 2 * rows * rank_full), BF),
            pltpu.VMEM((peers, 2, share, nv), BF),
        ],
        compiler_params=params(18),
        cost_estimate=pl.CostEstimate(
            flops=12 * rows * cols * tile * rank_full * nv, bytes_accessed=8_000_000, transcendentals=0
        ),
    )(ranks, near, right, left, *targets)


def merge_kernel(axis, *refs):
    half = len(refs) // 2
    parts, own_ref, piece_refs = refs[:half], refs[half], refs[half + 1 :]
    me = lax.axis_index(axis)
    for e in range(half):
        n = lax.rem(me + e, half)
        total = parts[0][n].astype(F32)
        for ref in parts[1:]:
            total = total + ref[n].astype(F32)
        if e == 0:
            own_ref[...] = total
        else:
            piece_refs[e - 1][...] = total


def merge(axis, parts):
    piece = parts[0].shape[1:]
    count = len(parts)
    return pl.pallas_call(
        functools.partial(merge_kernel, axis),
        out_shape=(jax.ShapeDtypeStruct(piece, F32),) * count,
        in_specs=[spec(VMEM)] * count,
        out_specs=(spec(VMEM),) * count,
        compiler_params=params(8),
        cost_estimate=pl.CostEstimate(flops=parts[0].size * 8, bytes_accessed=parts[0].size * 12, transcendentals=0),
    )(*parts)


def folded(value):
    return jnp.sum(value.reshape(-1, 8, value.shape[-1]), axis=0)


def residual_kernel(f, alpha_ref, u_prev_ref, own_ref, *refs):
    pieces, (res_ref, target_ref, square_ref) = refs[:-3], refs[-3:]
    total = own_ref[...] - alpha_ref[0] * u_prev_ref[f]
    for ref in pieces:
        total = total + ref[...].astype(F32)
    res_ref[...] = total
    nv = total.shape[-1]
    for part in range(2):
        target_ref[part * nv : (part + 1) * nv] = total[part].T.astype(BF)
    square_ref[...] = folded(total * total)


def residual(f, alpha_prev, u_prev, own, pieces):
    _, tile, nv = own.shape
    return pl.pallas_call(
        functools.partial(residual_kernel, f),
        out_shape=(
            jax.ShapeDtypeStruct(own.shape, F32),
            jax.ShapeDtypeStruct((2 * nv, tile), BF),
            jax.ShapeDtypeStruct((8, nv), F32),
        ),
        in_specs=[spec(SMEM)] + [spec(VMEM)] * (2 + len(pieces)),
        out_specs=(spec(VMEM),) * 3,
        compiler_params=params(),
        cost_estimate=pl.CostEstimate(flops=own.size * 8, bytes_accessed=own.size * 16, transcendentals=0),
    )(alpha_prev, u_prev, own, *pieces)


def nothing_kernel(out_ref):
    out_ref[...] = jnp.zeros_like(out_ref)


def nothing(nv):
    return pl.pallas_call(
        nothing_kernel,
        out_shape=jax.ShapeDtypeStruct((1, nv), F32),
        out_specs=spec(VMEM),
        compiler_params=params(1),
        cost_estimate=pl.CostEstimate(flops=nv, bytes_accessed=nv * 4, transcendentals=0),
        name="nothing",
    )()


def lane_sums(stats):
    nv = stats[0].shape[-1]
    lane = lax.broadcasted_iota(jnp.int32, (1, nv), 1)
    row = jnp.zeros((1, nv), F32)
    for n, value in enumerate(stats):
        total = jnp.sum(jnp.sum(value, axis=0, keepdims=True), axis=1, keepdims=True)
        row = jnp.where(lane == n, total, row)
    return row


def sums_kernel(f, v_ref, square_ref, own_ref, *refs):
    arrived, (before_ref, w_ref, stats_ref) = refs[:-3], refs[-3:]
    total = own_ref[...]
    for ref in arrived:
        total = total + ref[...]
    w_ref[...] = total
    v = v_ref[f]
    row = lane_sums([folded(total * total), folded(total * v), folded(v * v), square_ref[...]])
    stats_ref[...] = row + before_ref[...]


def sums(f, v, square, own, arrived, before):
    nv = v.shape[-1]
    return pl.pallas_call(
        functools.partial(sums_kernel, f),
        out_shape=(jax.ShapeDtypeStruct(v.shape[1:], F32), jax.ShapeDtypeStruct((1, nv), F32)),
        in_specs=[spec(VMEM)] * (4 + len(arrived)),
        out_specs=(spec(VMEM),) * 2,
        compiler_params=params(8),
        cost_estimate=pl.CostEstimate(flops=own.size * 8, bytes_accessed=own.size * 12, transcendentals=0),
    )(v, square, own, *arrived, before)


def finish_kernel(count_u, count_v, all_ref, v_ref, w0_ref, w1_ref, res0_ref, res1_ref, u_ref, next_ref, scale_ref):
    nv = v_ref.shape[-1]
    everyone = jnp.sum(all_ref[...], axis=0)
    ww, wv, vv, uu = [everyone[:, n : n + 1] for n in range(4)]
    beta = jnp.sqrt(uu / count_u + epsilon)
    inverse = 1.0 / beta
    square = ww * inverse * inverse - 2.0 * wv + vv * beta * beta
    alpha = jnp.sqrt(jnp.maximum(square, 0.0) / count_v + epsilon)
    spread = [jnp.broadcast_to(x, (1, nv)) for x in (beta, inverse, 1.0 / alpha)]
    b, ib, ia = spread
    u_ref[0] = res0_ref[...] * ib
    u_ref[1] = res1_ref[...] * ib
    for f, w_ref in enumerate((w0_ref, w1_ref)):
        next_ref[f] = (w_ref[...] * ib - v_ref[f] * b) * ia
    scale_ref[0] = beta[0, 0]
    scale_ref[1] = alpha[0, 0]


def finish(everyone, v, w0, w1, res0, res1, devices):
    count_u = float(2 * res0.size * devices)
    count_v = float(v.size * devices)
    return pl.pallas_call(
        functools.partial(finish_kernel, count_u, count_v),
        out_shape=(
            jax.ShapeDtypeStruct((2, *res0.shape), F32),
            jax.ShapeDtypeStruct(v.shape, F32),
            jax.ShapeDtypeStruct((2,), F32),
        ),
        in_specs=[spec(VMEM)] * 6,
        out_specs=(spec(VMEM), spec(VMEM), spec(SMEM)),
        compiler_params=params(),
        cost_estimate=pl.CostEstimate(flops=v.size * 16, bytes_accessed=v.size * 16, transcendentals=0),
        name="finish",
    )(everyone, v, w0, w1, res0, res1)


def body(left, right, ranks, v, u_prev, alpha_prev):
    frequencies, rows, cols = ranks.shape
    tile = left.shape[2] // rows
    rank_full = left.shape[3] // cols
    nv = v.shape[3]
    ranks = jnp.transpose(ranks, (2, 0, 1))
    peers = lax.axis_size(TROW)
    chips = lax.axis_size("tcol_0")
    devices = peers * lax.axis_size(TCOL)
    dims = (tile, rank_full, rows, cols, nv, v.shape[2], peers)

    def exchange(value, axes):
        return lax.all_to_all(value, axes, split_axis=0, concat_axis=0, tiled=True)

    def swapped(value):
        return lax.ppermute(value, "tcol_1", [(0, 1), (1, 0)])

    def along(value, axis, step):
        size = lax.axis_size(axis)
        return lax.ppermute(value, axis, [(i, (i + step) % size) for i in range(size)])

    def from_others(value, axis):
        size = lax.axis_size(axis)
        arrived = []
        for d in range(1, size):
            arrived.append(along(value, axis, size - d))
        return arrived

    sources = prepare(v)
    ways = [(TROW[1], TROW[0]), (TROW[0], TROW[1])]
    stage = [[sources[f], *from_others(sources[f], ways[f][0])] for f in range(frequencies)]
    rights = load(right, (ranks, alpha_prev))
    lefts = load(left)
    packed = [pack(ways[f][0], stage[f]) for f in range(frequencies)]
    arrivals = [from_others(packed[f], ways[f][1]) for f in range(frequencies)]
    squares, residuals, merged = [], [], []
    for f in range(frequencies):
        send, kept = project(f, ranks, ways[f], packed[f], arrivals[f], rights[f], lefts[f], dims)
        other = swapped(send)
        own, *pieces = expand(kept, other, lefts[f], dims)
        arrived = []
        for d, piece in enumerate(pieces):
            arrived.append(along(piece, "tcol_0", d + 1))
        res, target, square = residual(f, alpha_prev, u_prev, own, arrived)
        near = [target, *from_others(target, "tcol_0")]
        far = []
        for d in range(chips):
            far.append(swapped(near[d]))
        back = near_back(f, ranks, near, lefts[f], dims)
        way = ways[0]
        mine, *others = adjoint(f, ranks, way, back, rights[f], lefts[f], far, dims)
        parts = [mine]
        for d, piece in enumerate(others):
            parts.append(along(piece, way[0], d + 1))
        mine, *others = merge(way[1], parts)
        parts = []
        for d, piece in enumerate(others):
            parts.append(along(piece, way[1], d + 1))
        merged.append((mine, parts))
        residuals.append(res)
        squares.append(square)
    ws, stats = [], nothing(nv)
    for f in range(frequencies):
        w, stats = sums(f, v, squares[f], *merged[f], stats)
        ws.append(w)
    everyone = exchange(jnp.broadcast_to(stats, (devices, *stats.shape)), TROW_TCOL)
    return finish(everyone, v, *ws, *residuals, devices)


def solution(mesh):
    finer = Mesh(mesh.devices.reshape(4, 4, 4, 2), ("trow_0", "trow_1", "tcol_0", "tcol_1"))
    placed = (
        P(None, None, TROW, TCOL),
        P(None, None, TCOL, TROW),
        P(None, TROW, TCOL),
        P(None, None, TCOL_TROW, None),
        P(None, None, TROW_TCOL, None),
        P(),
    )
    return jax.shard_map(
        body,
        mesh=finer,
        in_specs=placed,
        out_specs=(P(None, None, TROW_TCOL, None), P(None, None, TCOL_TROW, None), P()),
        check_vma=False,
    )
```

time: 146 us -> 133 us (0.911)
  waiting for transfers between devices: 38.3 us -> 22.4 us
  starting transfers between devices: 54.4 us -> 62.9 us
  local copies, waits for them, and re-layouts: 6.19 us -> 0.98 us
  blocking collectives: 14.8 us -> 19.4 us
  Pallas kernels: 29.9 us -> 25.5 us
    ppermute x12 -> x36, starting transfers between devices: 17 us -> 49.1 us  [along(): lax.ppermute(value, axis, [(i, (i + step) % size) for i in range(size)])]
    all_to_all x4 -> x0, waiting for transfers between devices: 26.7 us -> none  [exchange(): return lax.all_to_all(value, axes, split_axis=0, concat_axis=0, tiled=True)]
    all_to_all x4 -> x0, starting transfers between devices: 24.9 us -> none  [exchange(): return lax.all_to_all(value, axes, split_axis=0, concat_axis=0, tiled=True)]
    ppermute x12 -> x36, waiting for transfers between devices: 9.99 us -> 22.4 us  [along(): lax.ppermute(value, axis, [(i, (i + step) % size) for i in range(size)])]
    unnamed x17 -> x8, local copies, waits for them, and re-layouts: 6.15 us -> 0.94 us
    all_to_all x1, blocking collectives: 14.8 us -> 19.4 us  [exchange(): return lax.all_to_all(value, axes, split_axis=0, concat_axis=0, tiled=True)]
    pallas_call x7 -> x14, Pallas kernels: 26.9 us -> 22.5 us  [the longest x2 7.73 us: adjoint(): pl.pallas_call(functools.partial(adjoint_kernel, f, dims, axes, side), ou...]
    ppermute x10, waiting for transfers between devices: 1.56 us -> 0.03 us  [swapped(): return lax.ppermute(value, 'tcol_1', [(0, 1), (1, 0)])]
  transfers between devices with their start and end apart: 26 -> 46, of which waited for: 7 -> 13; matrix products, arithmetic and copies ran while one was open for 0% -> 0% of each run, Pallas kernels for 19% -> 18%
where the time goes in v4:
time: 133 us
  starting transfers between devices  62.9 us (47%)
  Pallas kernels  25.5 us (19%)
  waiting for transfers between devices  22.4 us (17%)
  blocking collectives  19.4 us (15%)
  between operations  1.69 us (1%)
    ppermute x36, starting transfers between devices, along(): lax.ppermute(value, axis, [(i, (i + step) % size) for i in range(size)])  49.1 us
    ppermute x36, waiting for transfers between devices, along(): lax.ppermute(value, axis, [(i, (i + step) % size) for i in range(size)])  22.4 us
    all_to_all x1, blocking collectives, exchange(): return lax.all_to_all(value, axes, split_axis=0, concat_axis=0, tiled=True)  19.4 us
    ppermute x10, starting transfers between devices, swapped(): return lax.ppermute(value, 'tcol_1', [(0, 1), (1, 0)])  13.9 us
    pallas_call x2, Pallas kernels, adjoint(): pl.pallas_call(functools.partial(adjoint_kernel, f, dims, axes, side), ou...  7.73 us
    pallas_call x2, Pallas kernels, load(): pl.pallas_call(load_kernel, out_shape=(shape,) * 2, in_specs=[spec(SMEM)]...  6.36 us
    pallas_call x2, Pallas kernels, project(): pl.pallas_call(functools.partial(project_kernel, f, dims, axes), out_shap...  5.45 us
    pallas_call x2, Pallas kernels, near_back(): pl.pallas_call(functools.partial(near_kernel, f, dims), out_shape=jax.Sha...  2.73 us
  transfers between devices with their start and end apart: 46, of which 13 were waited for; matrix products, arithmetic and copies ran while one was open for 0% of the time, Pallas kernels for 18%

profile of v4, /device:TPU:1, one launch (start us, length us, event | category | flops | bytes accessed | tf_op | source)
XLA Modules:
  0.0 132.9 jit_solution(2074630002738604324)
XLA Ops:
  0.6 0.9 copy-done
  1.6 3.6 %collective-permute-start = (bf16[2,96,128]{2,1,0:T(8,128)(2,1)S(1)}, bf16[2,96,128]{2,1,0:T(8,128)(2,1)S(1)}, u32[]{:S(2)}, u32[]{:S(2)}) collective-permute-start(bf16[2,96,128]{2,1,0:T(8,128)(2,1)S(1)} %get-tuple-element.47.refs_0_), channel_id=1, source_target_pairs={{0,96},{32,0},{64,32},{96,64},{1,97},{33,1},{65,33},{97,65},{2,98}... | collective-permute-start | bytes 147464 | tf_op jit(solution)/shard_map/ppermute | solution.py:490
  6.4 3.3 %collective-permute-done.1.refs_2_ = bf16[2,96,128]{2,1,0:T(8,128)(2,1)S(1)} collective-permute-done((bf16[2,96,128]{2,1,0:T(8,128)(2,1)S(1)}, bf16[2,96,128]{2,1,0:T(8,128)(2,1)S(1)}, u32[]{:S(2)}, u32[]{:S(2)}) %collective-permute-start.1) | collective-permute-done | bytes 49184 | tf_op jit(solution)/shard_map/ppermute | solution.py:490
  10.2 2.5 %collective-permute-start.3 = (bf16[4,2,96,128]{3,2,1,0:T(8,128)(2,1)S(1)}, bf16[4,2,96,128]{3,2,1,0:T(8,128)(2,1)S(1)}, u32[]{:S(2)}, u32[]{:S(2)}) collective-permute-start(bf16[4,2,96,128]{3,2,1,0:T(8,128)(2,1)S(1)} %shard_map.85.packed_ref), channel_id=1, source_target_pairs={{0,24},{8,0},{16,8},{24,16},{1,25},{9,1},{17,9},{25,17},{2,26},{10... | collective-permute-start | bytes 589832 | tf_op jit(solution)/shard_map/ppermute | solution.py:490
  13.9 2.1 %collective-permute-start.23 = (bf16[2,96,128]{2,1,0:T(8,128)(2,1)S(1)}, bf16[2,96,128]{2,1,0:T(8,128)(2,1)S(1)}, u32[]{:S(2)}, u32[]{:S(2)}) collective-permute-start(bf16[2,96,128]{2,1,0:T(8,128)(2,1)S(1)} %get-tuple-element.66.refs_0_), channel_id=1, source_target_pairs={{0,24},{8,0},{16,8},{24,16},{1,25},{9,1},{17,9},{25,17},{2,26},{10... | collective-permute-start | bytes 147464 | tf_op jit(solution)/shard_map/ppermute | solution.py:490
  15.9 1.2 collective-permute-start.24
  17.2 2.8 %collective-permute-done.23.refs_1_ = bf16[2,96,128]{2,1,0:T(8,128)(2,1)S(1)} collective-permute-done((bf16[2,96,128]{2,1,0:T(8,128)(2,1)S(1)}, bf16[2,96,128]{2,1,0:T(8,128)(2,1)S(1)}, u32[]{:S(2)}, u32[]{:S(2)}) %collective-permute-start.23) | collective-permute-done | bytes 49184 | tf_op jit(solution)/shard_map/ppermute | solution.py:490
  20.2 3.5 %collective-permute-done.24.refs_2_ = bf16[2,96,128]{2,1,0:T(8,128)(2,1)S(1)} collective-permute-done((bf16[2,96,128]{2,1,0:T(8,128)(2,1)S(1)}, bf16[2,96,128]{2,1,0:T(8,128)(2,1)S(1)}, u32[]{:S(2)}, u32[]{:S(2)}) %collective-permute-start.24) | collective-permute-done | bytes 49184 | tf_op jit(solution)/shard_map/ppermute | solution.py:490
  23.7 3.0 %collective-permute-done.25.refs_3_ = bf16[2,96,128]{2,1,0:T(8,128)(2,1)S(1)} collective-permute-done((bf16[2,96,128]{2,1,0:T(8,128)(2,1)S(1)}, bf16[2,96,128]{2,1,0:T(8,128)(2,1)S(1)}, u32[]{:S(2)}, u32[]{:S(2)}) %collective-permute-start.25) | collective-permute-done | bytes 49184 | tf_op jit(solution)/shard_map/ppermute | solution.py:490
  27.4 1.0 collective-permute-start.27
  29.9 2.9 %shard_map.87 = (bf16[2,2048,384]{2,1,0:T(8,128)(2,1)S(1)}, bf16[2,2048,384]{2,1,0:T(8,128)(2,1)S(1)}) custom-call(bf16[2,2,2048,384]{3,2,1,0:T(8,128)(2,1)} %refs_0_.1), custom_call_target="tpu_custom_call" | custom-call | flops 1000000 | bytes 12582912 | tf_op jit(solution)/shard_map/pallas_call | solution.py:104
  32.8 3.5 %shard_map.86 = (bf16[2,1536,512]{2,1,0:T(8,128)(2,1)S(1)}, bf16[2,1536,512]{2,1,0:T(8,128)(2,1)S(1)}) custom-call(s32[6,2,8]{2,1,0:T(2,128)S(1)} %bitcast.2, f32[1]{0:T(128)S(6)} %copy.9.refs_1_.alpha_ref, bf16[2,2,1536,512]{3,2,1,0:T(8,128)(2,1)} %refs_2_.1), custom_call_target="tpu_custom_call" | custom-call | flops 1000000 | bytes 12582912 | tf_op jit(solution)/shard_map/pallas_call | solution.py:104
  36.3 2.7 %shard_map.88 = (f32[4,2,256,128]{3,2,1,0:T(8,128)S(1)}, bf16[4,256,768]{2,1,0:T(8,128)(2,1)S(1)}) custom-call(s32[6,2,8]{2,1,0:T(2,128)S(1)} %bitcast.3, bf16[4,2,96,128]{3,2,1,0:T(8,128)(2,1)S(1)} %shard_map.85.packed_ref, bf16[4,2,96,128]{3,2,1,0:T(8,128)(2,1)S(1)} %collective-permute-done.3.refs_0_, ...), custom_call_target="tpu_custom_call" | custom-call | flops 1207959552 | bytes 8000000 | tf_op jit(solution)/shard_map/pallas_call | solution.py:189
  39.0 4.1 %collective-permute-start.6 = (f32[4,2,256,128]{3,2,1,0:T(8,128)S(1)}, f32[4,2,256,128]{3,2,1,0:T(8,128)S(1)}, u32[]{:S(2)}, u32[]{:S(2)}) collective-permute-start(f32[4,2,256,128]{3,2,1,0:T(8,128)S(1)} %get-tuple-element.51), channel_id=1, source_target_pairs={{0,1},{1,0},{2,3},{3,2},{4,5},{5,4},{6,7},{7,6},{8,9},{9,8},{10,11... | collective-permute-start | bytes 3145736 | tf_op jit(solution)/shard_map/ppermute | solution.py:486
  43.2 2.7 %shard_map.95 = (f32[4,2,256,128]{3,2,1,0:T(8,128)S(1)}, bf16[4,256,768]{2,1,0:T(8,128)(2,1)S(1)}) custom-call(s32[6,2,8]{2,1,0:T(2,128)S(1)} %bitcast.4, bf16[4,2,96,128]{3,2,1,0:T(8,128)(2,1)S(1)} %shard_map.94.packed_ref, bf16[4,2,96,128]{3,2,1,0:T(8,128)(2,1)S(1)} %collective-permute-done.26.refs_0_, ...), custom_call_target="tpu_custom_call" | custom-call | flops 1207959552 | bytes 8000000 | tf_op jit(solution)/shard_map/pallas_call | solution.py:189
  46.7 1.7 %collective-permute-start.7 = (bf16[2,256,128]{2,1,0:T(8,128)(2,1)S(1)}, bf16[2,256,128]{2,1,0:T(8,128)(2,1)S(1)}, u32[]{:S(2)}, u32[]{:S(2)}) collective-permute-start(bf16[2,256,128]{2,1,0:T(8,128)(2,1)S(1)} %get-tuple-element.53), channel_id=1, source_target_pairs={{0,2},{2,4},{4,6},{6,0},{1,3},{3,5},{5,7},{7,1},{8,10},{10,12},{12... | collective-permute-start | bytes 393224 | tf_op jit(solution)/shard_map/ppermute | solution.py:490
  48.4 3.3 %collective-permute-start.8 = (bf16[2,256,128]{2,1,0:T(8,128)(2,1)S(1)}, bf16[2,256,128]{2,1,0:T(8,128)(2,1)S(1)}, u32[]{:S(2)}, u32[]{:S(2)}) collective-permute-start(bf16[2,256,128]{2,1,0:T(8,128)(2,1)S(1)} %get-tuple-element.54), channel_id=1, source_target_pairs={{0,4},{2,6},{4,0},{6,2},{1,5},{3,7},{5,1},{7,3},{8,12},{10,14},{12... | collective-permute-start | bytes 393224 | tf_op jit(solution)/shard_map/ppermute | solution.py:490
  53.1 0.8 collective-permute-start.30
  54.3 2.0 %collective-permute-start.32 = (bf16[2,256,128]{2,1,0:T(8,128)(2,1)S(1)}, bf16[2,256,128]{2,1,0:T(8,128)(2,1)S(1)}, u32[]{:S(2)}, u32[]{:S(2)}) collective-permute-start(bf16[2,256,128]{2,1,0:T(8,128)(2,1)S(1)} %get-tuple-element.74), channel_id=1, source_target_pairs={{0,6},{2,0},{4,2},{6,4},{1,7},{3,1},{5,3},{7,5},{8,14},{10,8},{12,... | collective-permute-start | bytes 393224 | tf_op jit(solution)/shard_map/ppermute | solution.py:490
  56.4 1.2 collective-permute-done.8.refs_1_
  57.8 2.4 %collective-permute-start.10 = (bf16[256,256]{1,0:T(8,128)(2,1)S(1)}, bf16[256,256]{1,0:T(8,128)(2,1)S(1)}, u32[]{:S(2)}, u32[]{:S(2)}) collective-permute-start(bf16[256,256]{1,0:T(8,128)(2,1)S(1)} %get-tuple-element.57.refs_0_), channel_id=1, source_target_pairs={{0,6},{2,0},{4,2},{6,4},{1,7},{3,1},{5,3},{7,5},{8,14},{10,8},{12,... | collective-permute-start | bytes 393224 | tf_op jit(solution)/shard_map/ppermute | solution.py:490
  60.1 1.2 collective-permute-start.11
  61.4 1.8 %collective-permute-done.31.refs_1_ = bf16[2,256,128]{2,1,0:T(8,128)(2,1)S(1)} collective-permute-done((bf16[2,256,128]{2,1,0:T(8,128)(2,1)S(1)}, bf16[2,256,128]{2,1,0:T(8,128)(2,1)S(1)}, u32[]{:S(2)}, u32[]{:S(2)}) %collective-permute-start.31) | collective-permute-done | bytes 131104 | tf_op jit(solution)/shard_map/ppermute | solution.py:490
  63.4 2.5 %collective-permute-start.33 = (bf16[256,256]{1,0:T(8,128)(2,1)S(1)}, bf16[256,256]{1,0:T(8,128)(2,1)S(1)}, u32[]{:S(2)}, u32[]{:S(2)}) collective-permute-start(bf16[256,256]{1,0:T(8,128)(2,1)S(1)} %get-tuple-element.76.refs_0_), channel_id=1, source_target_pairs={{0,6},{2,0},{4,2},{6,4},{1,7},{3,1},{5,3},{7,5},{8,14},{10,8},{12,... | collective-permute-start | bytes 393224 | tf_op jit(solution)/shard_map/ppermute | solution.py:490
  66.7 1.9 %collective-permute-start.12 = (bf16[256,256]{1,0:T(8,128)(2,1)S(1)}, bf16[256,256]{1,0:T(8,128)(2,1)S(1)}, u32[]{:S(2)}, u32[]{:S(2)}) collective-permute-start(bf16[256,256]{1,0:T(8,128)(2,1)S(1)} %get-tuple-element.57.refs_0_), channel_id=1, source_target_pairs={{0,2},{2,4},{4,6},{6,0},{1,3},{3,5},{5,7},{7,1},{8,10},{10,12},{12... | collective-permute-start | bytes 393224 | tf_op jit(solution)/shard_map/ppermute | solution.py:490
  68.6 2.3 %collective-permute-start.36 = (bf16[256,256]{1,0:T(8,128)(2,1)S(1)}, bf16[256,256]{1,0:T(8,128)(2,1)S(1)}, u32[]{:S(2)}, u32[]{:S(2)}) collective-permute-start(bf16[256,256]{1,0:T(8,128)(2,1)S(1)} %get-tuple-element.76.refs_0_), channel_id=1, source_target_pairs={{0,1},{1,0},{2,3},{3,2},{4,5},{5,4},{6,7},{7,6},{8,9},{9,8},{10,11... | collective-permute-start | bytes 393224 | tf_op jit(solution)/shard_map/ppermute | solution.py:486
  70.8 3.1 %collective-permute-start.37 = (bf16[256,256]{1,0:T(8,128)(2,1)S(1)}, bf16[256,256]{1,0:T(8,128)(2,1)S(1)}, u32[]{:S(2)}, u32[]{:S(2)}) collective-permute-start(bf16[256,256]{1,0:T(8,128)(2,1)S(1)} %collective-permute-done.33.refs_1_), channel_id=1, source_target_pairs={{0,1},{1,0},{2,3},{3,2},{4,5},{5,4},{6,7},{7,6},{8,9},{9,8},{10,11... | collective-permute-start | bytes 393224 | tf_op jit(solution)/shard_map/ppermute | solution.py:486
  73.9 1.3 collective-permute-start.38
  75.2 1.9 %collective-permute-start.39 = (bf16[256,256]{1,0:T(8,128)(2,1)S(1)}, bf16[256,256]{1,0:T(8,128)(2,1)S(1)}, u32[]{:S(2)}, u32[]{:S(2)}) collective-permute-start(bf16[256,256]{1,0:T(8,128)(2,1)S(1)} %collective-permute-done.35.refs_3_), channel_id=1, source_target_pairs={{0,1},{1,0},{2,3},{3,2},{4,5},{5,4},{6,7},{7,6},{8,9},{9,8},{10,11... | collective-permute-start | bytes 393224 | tf_op jit(solution)/shard_map/ppermute | solution.py:486
  77.1 1.4 %shard_map.98.near_ref = bf16[2,4,256,384]{3,2,1,0:T(8,128)(2,1)S(1)} custom-call(s32[6,2,8]{2,1,0:T(2,128)S(1)} %bitcast.5, bf16[2,2048,384]{2,1,0:T(8,128)(2,1)S(1)} %get-tuple-element.68.refs_4_.left_ref, bf16[256,256]{1,0:T(8,128)(2,1)S(1)} %get-tuple-element.76.refs_0_, bf16[256,256]{1,0:T(8,128)(2,1)S(1)} %collective-permute-done.33.refs_1_, ...), custom_call_target="tpu_custom_call" | custom-call | flops 402653184 | bytes 4000000 | tf_op jit(solution)/shard_map/pallas_call | solution.py:261
  79.6 3.9 %shard_map.99 = (bf16[4,2,96,128]{3,2,1,0:T(8,128)(2,1)S(1)}, bf16[4,2,96,128]{3,2,1,0:T(8,128)(2,1)S(1)}, bf16[4,2,96,128]{3,2,1,0:T(8,128)(2,1)S(1)}, bf16[4,2,96,128]{3,2,1,0:T(8,128)(2,1)S(1)}) custom-call(s32[6,2,8]{2,1,0:T(2,128)S(1)} %bitcast.6, bf16[2,4,256,384]{3,2,1,0:T(8,128)(2,1)S(1)} %shard_map.98.near_ref, ...), custom_call_target="tpu_custom_call" | custom-call | flops 1207959552 | bytes 8000000 | tf_op jit(solution)/shard_map/pallas_call | solution.py:310
  83.5 1.4 %shard_map.91.near_ref = bf16[2,4,256,384]{3,2,1,0:T(8,128)(2,1)S(1)} custom-call(s32[6,2,8]{2,1,0:T(2,128)S(1)} %bitcast.7, bf16[2,2048,384]{2,1,0:T(8,128)(2,1)S(1)} %get-tuple-element.49.refs_4_.left_ref, bf16[256,256]{1,0:T(8,128)(2,1)S(1)} %get-tuple-element.57.refs_0_, bf16[256,256]{1,0:T(8,128)(2,1)S(1)} %collective-permute-done.10.refs_1_, ...), custom_call_target="tpu_custom_call" | custom-call | flops 402653184 | bytes 4000000 | tf_op jit(solution)/shard_map/pallas_call | solution.py:261
  84.9 3.0 %collective-permute-start.41 = (bf16[4,2,96,128]{3,2,1,0:T(8,128)(2,1)S(1)}, bf16[4,2,96,128]{3,2,1,0:T(8,128)(2,1)S(1)}, u32[]{:S(2)}, u32[]{:S(2)}) collective-permute-start(bf16[4,2,96,128]{3,2,1,0:T(8,128)(2,1)S(1)} %get-tuple-element.79), channel_id=1, source_target_pairs={{0,16},{8,24},{16,0},{24,8},{1,17},{9,25},{17,1},{25,9},{2,18},{10... | collective-permute-start | bytes 589832 | tf_op jit(solution)/shard_map/ppermute | solution.py:490
  88.0 3.9 %shard_map.92 = (bf16[4,2,96,128]{3,2,1,0:T(8,128)(2,1)S(1)}, bf16[4,2,96,128]{3,2,1,0:T(8,128)(2,1)S(1)}, bf16[4,2,96,128]{3,2,1,0:T(8,128)(2,1)S(1)}, bf16[4,2,96,128]{3,2,1,0:T(8,128)(2,1)S(1)}) custom-call(s32[6,2,8]{2,1,0:T(2,128)S(1)} %bitcast.8, bf16[2,4,256,384]{3,2,1,0:T(8,128)(2,1)S(1)} %shard_map.91.near_ref, ...), custom_call_target="tpu_custom_call" | custom-call | flops 1207959552 | bytes 8000000 | tf_op jit(solution)/shard_map/pallas_call | solution.py:310
  91.9 1.5 %collective-permute-start.17 = (bf16[4,2,96,128]{3,2,1,0:T(8,128)(2,1)S(1)}, bf16[4,2,96,128]{3,2,1,0:T(8,128)(2,1)S(1)}, u32[]{:S(2)}, u32[]{:S(2)}) collective-permute-start(bf16[4,2,96,128]{3,2,1,0:T(8,128)(2,1)S(1)} %get-tuple-element.59), channel_id=1, source_target_pairs={{0,8},{8,16},{16,24},{24,0},{1,9},{9,17},{17,25},{25,1},{2,10},{10... | collective-permute-start | bytes 589832 | tf_op jit(solution)/shard_map/ppermute | solution.py:490
  94.1 2.0 %collective-permute-start.19 = (bf16[4,2,96,128]{3,2,1,0:T(8,128)(2,1)S(1)}, bf16[4,2,96,128]{3,2,1,0:T(8,128)(2,1)S(1)}, u32[]{:S(2)}, u32[]{:S(2)}) collective-permute-start(bf16[4,2,96,128]{3,2,1,0:T(8,128)(2,1)S(1)} %get-tuple-element.61), channel_id=1, source_target_pairs={{0,24},{8,0},{16,8},{24,16},{1,25},{9,1},{17,9},{25,17},{2,26},{10... | collective-permute-start | bytes 589832 | tf_op jit(solution)/shard_map/ppermute | solution.py:490
  96.1 1.2 collective-permute-done.42.refs_3_
  97.4 0.9 collective-permute-start.43
  98.3 1.9 %collective-permute-start.44 = (f32[2,96,128]{2,1,0:T(8,128)S(1)}, f32[2,96,128]{2,1,0:T(8,128)S(1)}, u32[]{:S(2)}, u32[]{:S(2)}) collective-permute-start(f32[2,96,128]{2,1,0:T(8,128)S(1)} %get-tuple-element.83), channel_id=1, source_target_pairs={{0,64},{32,96},{64,0},{96,32},{1,65},{33,97},{65,1},{97,33},{2,66}... | collective-permute-start | bytes 294920 | tf_op jit(solution)/shard_map/ppermute | solution.py:490
  100.3 1.9 %collective-permute-start.45 = (f32[2,96,128]{2,1,0:T(8,128)S(1)}, f32[2,96,128]{2,1,0:T(8,128)S(1)}, u32[]{:S(2)}, u32[]{:S(2)}) collective-permute-start(f32[2,96,128]{2,1,0:T(8,128)S(1)} %get-tuple-element.84), channel_id=1, source_target_pairs={{0,96},{32,0},{64,32},{96,64},{1,97},{33,1},{65,33},{97,65},{2,98}... | collective-permute-start | bytes 294920 | tf_op jit(solution)/shard_map/ppermute | solution.py:490
  102.2 1.6 %collective-permute-done.18.refs_2_ = bf16[4,2,96,128]{3,2,1,0:T(8,128)(2,1)S(1)} collective-permute-done((bf16[4,2,96,128]{3,2,1,0:T(8,128)(2,1)S(1)}, bf16[4,2,96,128]{3,2,1,0:T(8,128)(2,1)S(1)}, u32[]{:S(2)}, u32[]{:S(2)}) %collective-permute-start.18) | collective-permute-done | bytes 196640 | tf_op jit(solution)/shard_map/ppermute | solution.py:490
  103.8 1.5 %collective-permute-done.19.refs_3_ = bf16[4,2,96,128]{3,2,1,0:T(8,128)(2,1)S(1)} collective-permute-done((bf16[4,2,96,128]{3,2,1,0:T(8,128)(2,1)S(1)}, bf16[4,2,96,128]{3,2,1,0:T(8,128)(2,1)S(1)}, u32[]{:S(2)}, u32[]{:S(2)}) %collective-permute-start.19) | collective-permute-done | bytes 196640 | tf_op jit(solution)/shard_map/ppermute | solution.py:490
  105.4 0.9 collective-permute-start.20
  106.3 2.0 %collective-permute-start.21 = (f32[2,96,128]{2,1,0:T(8,128)S(1)}, f32[2,96,128]{2,1,0:T(8,128)S(1)}, u32[]{:S(2)}, u32[]{:S(2)}) collective-permute-start(f32[2,96,128]{2,1,0:T(8,128)S(1)} %get-tuple-element.64), channel_id=1, source_target_pairs={{0,64},{32,96},{64,0},{96,32},{1,65},{33,97},{65,1},{97,33},{2,66}... | collective-permute-start | bytes 294920 | tf_op jit(solution)/shard_map/ppermute | solution.py:490
  108.3 1.9 %collective-permute-start.22 = (f32[2,96,128]{2,1,0:T(8,128)S(1)}, f32[2,96,128]{2,1,0:T(8,128)S(1)}, u32[]{:S(2)}, u32[]{:S(2)}) collective-permute-start(f32[2,96,128]{2,1,0:T(8,128)S(1)} %get-tuple-element.65), channel_id=1, source_target_pairs={{0,96},{32,0},{64,32},{96,64},{1,97},{33,1},{65,33},{97,65},{2,98}... | collective-permute-start | bytes 294920 | tf_op jit(solution)/shard_map/ppermute | solution.py:490
  110.3 1.1 collective-permute-done.21.refs_1_
  112.2 19.4 %all_to_all.5.all_ref = f32[128,1,128]{2,1,0:T(1,128)S(1)} all-to-all(f32[128,1,128]{2,1,0:T(1,128)S(1)} %broadcast_in_dim.3), channel_id=1, replica_groups=mesh['trow_0'=4,'trow_1'=4,'tcol_0'=4,'tcol_1'=2] {'trow_0','trow_1','tc..., dimensions={0} | all-to-all | bytes 131072 | tf_op jit(solution)/shard_map/all_to_all | solution.py:483
  131.6 1.1 finish.1
  (75 shorter events, 11.3 us)
Async XLA Ops:
  1.6 4.8 %collective-permute-start = (bf16[2,96,128]{2,1,0:T(8,128)(2,1)S(1)}, bf16[2,96,128]{2,1,0:T(8,128)(2,1)S(1)}, u32[]{:S(2)}, u32[]{:S(2)}) collective-permute-start(bf16[2,96,128]{2,1,0:T(8,128)(2,1)S(1)} %get-tuple-element.47.refs_0_), channel_id=1, source_target_pairs={{0,96},{32,0},{64,32},{96,64},{1,97},{33,1},{65,33},{97,65},{2,98}... | collective-permute-start | bytes 147464 | tf_op jit(solution)/shard_map/ppermute | solution.py:490
  5.2 4.5 %collective-permute-start.1 = (bf16[2,96,128]{2,1,0:T(8,128)(2,1)S(1)}, bf16[2,96,128]{2,1,0:T(8,128)(2,1)S(1)}, u32[]{:S(2)}, u32[]{:S(2)}) collective-permute-start(bf16[2,96,128]{2,1,0:T(8,128)(2,1)S(1)} %get-tuple-element.47.refs_0_), channel_id=1, source_target_pairs={{0,64},{32,96},{64,0},{96,32},{1,65},{33,97},{65,1},{97,33},{2,66}... | collective-permute-start | bytes 147464 | tf_op jit(solution)/shard_map/ppermute | solution.py:490
  5.5 4.6 %collective-permute-start.2 = (bf16[2,96,128]{2,1,0:T(8,128)(2,1)S(1)}, bf16[2,96,128]{2,1,0:T(8,128)(2,1)S(1)}, u32[]{:S(2)}, u32[]{:S(2)}) collective-permute-start(bf16[2,96,128]{2,1,0:T(8,128)(2,1)S(1)} %get-tuple-element.47.refs_0_), channel_id=1, source_target_pairs={{0,32},{32,64},{64,96},{96,0},{1,33},{33,65},{65,97},{97,1},{2,34}... | collective-permute-start | bytes 147464 | tf_op jit(solution)/shard_map/ppermute | solution.py:490
  10.2 18.2 %collective-permute-start.3 = (bf16[4,2,96,128]{3,2,1,0:T(8,128)(2,1)S(1)}, bf16[4,2,96,128]{3,2,1,0:T(8,128)(2,1)S(1)}, u32[]{:S(2)}, u32[]{:S(2)}) collective-permute-start(bf16[4,2,96,128]{3,2,1,0:T(8,128)(2,1)S(1)} %shard_map.85.packed_ref), channel_id=1, source_target_pairs={{0,24},{8,0},{16,8},{24,16},{1,25},{9,1},{17,9},{25,17},{2,26},{10... | collective-permute-start | bytes 589832 | tf_op jit(solution)/shard_map/ppermute | solution.py:490
  12.7 23.5 %collective-permute-start.4 = (bf16[4,2,96,128]{3,2,1,0:T(8,128)(2,1)S(1)}, bf16[4,2,96,128]{3,2,1,0:T(8,128)(2,1)S(1)}, u32[]{:S(2)}, u32[]{:S(2)}) collective-permute-start(bf16[4,2,96,128]{3,2,1,0:T(8,128)(2,1)S(1)} %shard_map.85.packed_ref), channel_id=1, source_target_pairs={{0,16},{8,24},{16,0},{24,8},{1,17},{9,25},{17,1},{25,9},{2,18},{10... | collective-permute-start | bytes 589832 | tf_op jit(solution)/shard_map/ppermute | solution.py:490
  13.3 23.0 %collective-permute-start.5 = (bf16[4,2,96,128]{3,2,1,0:T(8,128)(2,1)S(1)}, bf16[4,2,96,128]{3,2,1,0:T(8,128)(2,1)S(1)}, u32[]{:S(2)}, u32[]{:S(2)}) collective-permute-start(bf16[4,2,96,128]{3,2,1,0:T(8,128)(2,1)S(1)} %shard_map.85.packed_ref), channel_id=1, source_target_pairs={{0,8},{8,16},{16,24},{24,0},{1,9},{9,17},{17,25},{25,1},{2,10},{10... | collective-permute-start | bytes 589832 | tf_op jit(solution)/shard_map/ppermute | solution.py:490
  13.9 6.1 %collective-permute-start.23 = (bf16[2,96,128]{2,1,0:T(8,128)(2,1)S(1)}, bf16[2,96,128]{2,1,0:T(8,128)(2,1)S(1)}, u32[]{:S(2)}, u32[]{:S(2)}) collective-permute-start(bf16[2,96,128]{2,1,0:T(8,128)(2,1)S(1)} %get-tuple-element.66.refs_0_), channel_id=1, source_target_pairs={{0,24},{8,0},{16,8},{24,16},{1,25},{9,1},{17,9},{25,17},{2,26},{10... | collective-permute-start | bytes 147464 | tf_op jit(solution)/shard_map/ppermute | solution.py:490
  15.9 7.7 %collective-permute-start.24 = (bf16[2,96,128]{2,1,0:T(8,128)(2,1)S(1)}, bf16[2,96,128]{2,1,0:T(8,128)(2,1)S(1)}, u32[]{:S(2)}, u32[]{:S(2)}) collective-permute-start(bf16[2,96,128]{2,1,0:T(8,128)(2,1)S(1)} %get-tuple-element.66.refs_0_), channel_id=1, source_target_pairs={{0,16},{8,24},{16,0},{24,8},{1,17},{9,25},{17,1},{25,9},{2,18},{10... | collective-permute-start | bytes 147464 | tf_op jit(solution)/shard_map/ppermute | solution.py:490
  20.0 6.8 %collective-permute-start.25 = (bf16[2,96,128]{2,1,0:T(8,128)(2,1)S(1)}, bf16[2,96,128]{2,1,0:T(8,128)(2,1)S(1)}, u32[]{:S(2)}, u32[]{:S(2)}) collective-permute-start(bf16[2,96,128]{2,1,0:T(8,128)(2,1)S(1)} %get-tuple-element.66.refs_0_), channel_id=1, source_target_pairs={{0,8},{8,16},{16,24},{24,0},{1,9},{9,17},{17,25},{25,1},{2,10},{10... | collective-permute-start | bytes 147464 | tf_op jit(solution)/shard_map/ppermute | solution.py:490
  26.7 16.4 %collective-permute-start.26 = (bf16[4,2,96,128]{3,2,1,0:T(8,128)(2,1)S(1)}, bf16[4,2,96,128]{3,2,1,0:T(8,128)(2,1)S(1)}, u32[]{:S(2)}, u32[]{:S(2)}) collective-permute-start(bf16[4,2,96,128]{3,2,1,0:T(8,128)(2,1)S(1)} %shard_map.94.packed_ref), channel_id=1, source_target_pairs={{0,96},{32,0},{64,32},{96,64},{1,97},{33,1},{65,33},{97,65},{2,98}... | collective-permute-start | bytes 589832 | tf_op jit(solution)/shard_map/ppermute | solution.py:490
  27.4 15.8 %collective-permute-start.27 = (bf16[4,2,96,128]{3,2,1,0:T(8,128)(2,1)S(1)}, bf16[4,2,96,128]{3,2,1,0:T(8,128)(2,1)S(1)}, u32[]{:S(2)}, u32[]{:S(2)}) collective-permute-start(bf16[4,2,96,128]{3,2,1,0:T(8,128)(2,1)S(1)} %shard_map.94.packed_ref), channel_id=1, source_target_pairs={{0,64},{32,96},{64,0},{96,32},{1,65},{33,97},{65,1},{97,33},{2,66}... | collective-permute-start | bytes 589832 | tf_op jit(solution)/shard_map/ppermute | solution.py:490
  28.4 14.7 %collective-permute-start.28 = (bf16[4,2,96,128]{3,2,1,0:T(8,128)(2,1)S(1)}, bf16[4,2,96,128]{3,2,1,0:T(8,128)(2,1)S(1)}, u32[]{:S(2)}, u32[]{:S(2)}) collective-permute-start(bf16[4,2,96,128]{3,2,1,0:T(8,128)(2,1)S(1)} %shard_map.94.packed_ref), channel_id=1, source_target_pairs={{0,32},{32,64},{64,96},{96,0},{1,33},{33,65},{65,97},{97,1},{2,34}... | collective-permute-start | bytes 589832 | tf_op jit(solution)/shard_map/ppermute | solution.py:490
  39.0 7.0 %collective-permute-start.6 = (f32[4,2,256,128]{3,2,1,0:T(8,128)S(1)}, f32[4,2,256,128]{3,2,1,0:T(8,128)S(1)}, u32[]{:S(2)}, u32[]{:S(2)}) collective-permute-start(f32[4,2,256,128]{3,2,1,0:T(8,128)S(1)} %get-tuple-element.51), channel_id=1, source_target_pairs={{0,1},{1,0},{2,3},{3,2},{4,5},{5,4},{6,7},{7,6},{8,9},{9,8},{10,11... | collective-permute-start | bytes 3145736 | tf_op jit(solution)/shard_map/ppermute | solution.py:486
  45.9 6.5 %collective-permute-start.29 = (f32[4,2,256,128]{3,2,1,0:T(8,128)S(1)}, f32[4,2,256,128]{3,2,1,0:T(8,128)S(1)}, u32[]{:S(2)}, u32[]{:S(2)}) collective-permute-start(f32[4,2,256,128]{3,2,1,0:T(8,128)S(1)} %get-tuple-element.70), channel_id=1, source_target_pairs={{0,1},{1,0},{2,3},{3,2},{4,5},{5,4},{6,7},{7,6},{8,9},{9,8},{10,11... | collective-permute-start | bytes 3145736 | tf_op jit(solution)/shard_map/ppermute | solution.py:486
  46.7 10.9 %copy-start.2 = (f32[2,2,256,128]{3,2,1,0:T(8,128)S(1)}, f32[2,2,256,128]{3,2,1,0:T(8,128)}, u32[]{:S(2)}) copy-start(f32[2,2,256,128]{3,2,1,0:T(8,128)} %u_prev_ref.3) | copy-start | bytes 1572868
  46.7 7.6 %collective-permute-start.7 = (bf16[2,256,128]{2,1,0:T(8,128)(2,1)S(1)}, bf16[2,256,128]{2,1,0:T(8,128)(2,1)S(1)}, u32[]{:S(2)}, u32[]{:S(2)}) collective-permute-start(bf16[2,256,128]{2,1,0:T(8,128)(2,1)S(1)} %get-tuple-element.53), channel_id=1, source_target_pairs={{0,2},{2,4},{4,6},{6,0},{1,3},{3,5},{5,7},{7,1},{8,10},{10,12},{12... | collective-permute-start | bytes 393224 | tf_op jit(solution)/shard_map/ppermute | solution.py:490
  48.4 9.2 %collective-permute-start.8 = (bf16[2,256,128]{2,1,0:T(8,128)(2,1)S(1)}, bf16[2,256,128]{2,1,0:T(8,128)(2,1)S(1)}, u32[]{:S(2)}, u32[]{:S(2)}) collective-permute-start(bf16[2,256,128]{2,1,0:T(8,128)(2,1)S(1)} %get-tuple-element.54), channel_id=1, source_target_pairs={{0,4},{2,6},{4,0},{6,2},{1,5},{3,7},{5,1},{7,3},{8,12},{10,14},{12... | collective-permute-start | bytes 393224 | tf_op jit(solution)/shard_map/ppermute | solution.py:490
  51.7 5.9 %collective-permute-start.9 = (bf16[2,256,128]{2,1,0:T(8,128)(2,1)S(1)}, bf16[2,256,128]{2,1,0:T(8,128)(2,1)S(1)}, u32[]{:S(2)}, u32[]{:S(2)}) collective-permute-start(bf16[2,256,128]{2,1,0:T(8,128)(2,1)S(1)} %get-tuple-element.55), channel_id=1, source_target_pairs={{0,6},{2,0},{4,2},{6,4},{1,7},{3,1},{5,3},{7,5},{8,14},{10,8},{12,... | collective-permute-start | bytes 393224 | tf_op jit(solution)/shard_map/ppermute | solution.py:490
  53.1 8.3 %collective-permute-start.30 = (bf16[2,256,128]{2,1,0:T(8,128)(2,1)S(1)}, bf16[2,256,128]{2,1,0:T(8,128)(2,1)S(1)}, u32[]{:S(2)}, u32[]{:S(2)}) collective-permute-start(bf16[2,256,128]{2,1,0:T(8,128)(2,1)S(1)} %get-tuple-element.72), channel_id=1, source_target_pairs={{0,2},{2,4},{4,6},{6,0},{1,3},{3,5},{5,7},{7,1},{8,10},{10,12},{12... | collective-permute-start | bytes 393224 | tf_op jit(solution)/shard_map/ppermute | solution.py:490
  53.9 9.4 %collective-permute-start.31 = (bf16[2,256,128]{2,1,0:T(8,128)(2,1)S(1)}, bf16[2,256,128]{2,1,0:T(8,128)(2,1)S(1)}, u32[]{:S(2)}, u32[]{:S(2)}) collective-permute-start(bf16[2,256,128]{2,1,0:T(8,128)(2,1)S(1)} %get-tuple-element.73), channel_id=1, source_target_pairs={{0,4},{2,6},{4,0},{6,2},{1,5},{3,7},{5,1},{7,3},{8,12},{10,14},{12... | collective-permute-start | bytes 393224 | tf_op jit(solution)/shard_map/ppermute | solution.py:490
  54.3 8.9 %collective-permute-start.32 = (bf16[2,256,128]{2,1,0:T(8,128)(2,1)S(1)}, bf16[2,256,128]{2,1,0:T(8,128)(2,1)S(1)}, u32[]{:S(2)}, u32[]{:S(2)}) collective-permute-start(bf16[2,256,128]{2,1,0:T(8,128)(2,1)S(1)} %get-tuple-element.74), channel_id=1, source_target_pairs={{0,6},{2,0},{4,2},{6,4},{1,7},{3,1},{5,3},{7,5},{8,14},{10,8},{12,... | collective-permute-start | bytes 393224 | tf_op jit(solution)/shard_map/ppermute | solution.py:490
  57.8 8.9 %collective-permute-start.10 = (bf16[256,256]{1,0:T(8,128)(2,1)S(1)}, bf16[256,256]{1,0:T(8,128)(2,1)S(1)}, u32[]{:S(2)}, u32[]{:S(2)}) collective-permute-start(bf16[256,256]{1,0:T(8,128)(2,1)S(1)} %get-tuple-element.57.refs_0_), channel_id=1, source_target_pairs={{0,6},{2,0},{4,2},{6,4},{1,7},{3,1},{5,3},{7,5},{8,14},{10,8},{12,... | collective-permute-start | bytes 393224 | tf_op jit(solution)/shard_map/ppermute | solution.py:490
  60.1 8.4 %collective-permute-start.11 = (bf16[256,256]{1,0:T(8,128)(2,1)S(1)}, bf16[256,256]{1,0:T(8,128)(2,1)S(1)}, u32[]{:S(2)}, u32[]{:S(2)}) collective-permute-start(bf16[256,256]{1,0:T(8,128)(2,1)S(1)} %get-tuple-element.57.refs_0_), channel_id=1, source_target_pairs={{0,4},{2,6},{4,0},{6,2},{1,5},{3,7},{5,1},{7,3},{8,12},{10,14},{12... | collective-permute-start | bytes 393224 | tf_op jit(solution)/shard_map/ppermute | solution.py:490
  63.4 7.4 %collective-permute-start.33 = (bf16[256,256]{1,0:T(8,128)(2,1)S(1)}, bf16[256,256]{1,0:T(8,128)(2,1)S(1)}, u32[]{:S(2)}, u32[]{:S(2)}) collective-permute-start(bf16[256,256]{1,0:T(8,128)(2,1)S(1)} %get-tuple-element.76.refs_0_), channel_id=1, source_target_pairs={{0,6},{2,0},{4,2},{6,4},{1,7},{3,1},{5,3},{7,5},{8,14},{10,8},{12,... | collective-permute-start | bytes 393224 | tf_op jit(solution)/shard_map/ppermute | solution.py:490
  65.9 8.0 %collective-permute-start.34 = (bf16[256,256]{1,0:T(8,128)(2,1)S(1)}, bf16[256,256]{1,0:T(8,128)(2,1)S(1)}, u32[]{:S(2)}, u32[]{:S(2)}) collective-permute-start(bf16[256,256]{1,0:T(8,128)(2,1)S(1)} %get-tuple-element.76.refs_0_), channel_id=1, source_target_pairs={{0,4},{2,6},{4,0},{6,2},{1,5},{3,7},{5,1},{7,3},{8,12},{10,14},{12... | collective-permute-start | bytes 393224 | tf_op jit(solution)/shard_map/ppermute | solution.py:490
  66.7 8.6 %collective-permute-start.35 = (bf16[256,256]{1,0:T(8,128)(2,1)S(1)}, bf16[256,256]{1,0:T(8,128)(2,1)S(1)}, u32[]{:S(2)}, u32[]{:S(2)}) collective-permute-start(bf16[256,256]{1,0:T(8,128)(2,1)S(1)} %get-tuple-element.76.refs_0_), channel_id=1, source_target_pairs={{0,2},{2,4},{4,6},{6,0},{1,3},{3,5},{5,7},{7,1},{8,10},{10,12},{12... | collective-permute-start | bytes 393224 | tf_op jit(solution)/shard_map/ppermute | solution.py:490
  66.7 11.8 %collective-permute-start.12 = (bf16[256,256]{1,0:T(8,128)(2,1)S(1)}, bf16[256,256]{1,0:T(8,128)(2,1)S(1)}, u32[]{:S(2)}, u32[]{:S(2)}) collective-permute-start(bf16[256,256]{1,0:T(8,128)(2,1)S(1)} %get-tuple-element.57.refs_0_), channel_id=1, source_target_pairs={{0,2},{2,4},{4,6},{6,0},{1,3},{3,5},{5,7},{7,1},{8,10},{10,12},{12... | collective-permute-start | bytes 393224 | tf_op jit(solution)/shard_map/ppermute | solution.py:490
  68.6 10.4 %collective-permute-start.36 = (bf16[256,256]{1,0:T(8,128)(2,1)S(1)}, bf16[256,256]{1,0:T(8,128)(2,1)S(1)}, u32[]{:S(2)}, u32[]{:S(2)}) collective-permute-start(bf16[256,256]{1,0:T(8,128)(2,1)S(1)} %get-tuple-element.76.refs_0_), channel_id=1, source_target_pairs={{0,1},{1,0},{2,3},{3,2},{4,5},{5,4},{6,7},{7,6},{8,9},{9,8},{10,11... | collective-permute-start | bytes 393224 | tf_op jit(solution)/shard_map/ppermute | solution.py:486
  70.8 8.2 %collective-permute-start.37 = (bf16[256,256]{1,0:T(8,128)(2,1)S(1)}, bf16[256,256]{1,0:T(8,128)(2,1)S(1)}, u32[]{:S(2)}, u32[]{:S(2)}) collective-permute-start(bf16[256,256]{1,0:T(8,128)(2,1)S(1)} %collective-permute-done.33.refs_1_), channel_id=1, source_target_pairs={{0,1},{1,0},{2,3},{3,2},{4,5},{5,4},{6,7},{7,6},{8,9},{9,8},{10,11... | collective-permute-start | bytes 393224 | tf_op jit(solution)/shard_map/ppermute | solution.py:486
  73.9 5.5 %collective-permute-start.38 = (bf16[256,256]{1,0:T(8,128)(2,1)S(1)}, bf16[256,256]{1,0:T(8,128)(2,1)S(1)}, u32[]{:S(2)}, u32[]{:S(2)}) collective-permute-start(bf16[256,256]{1,0:T(8,128)(2,1)S(1)} %collective-permute-done.34.refs_2_), channel_id=1, source_target_pairs={{0,1},{1,0},{2,3},{3,2},{4,5},{5,4},{6,7},{7,6},{8,9},{9,8},{10,11... | collective-permute-start | bytes 393224 | tf_op jit(solution)/shard_map/ppermute | solution.py:486
  75.2 4.4 %collective-permute-start.39 = (bf16[256,256]{1,0:T(8,128)(2,1)S(1)}, bf16[256,256]{1,0:T(8,128)(2,1)S(1)}, u32[]{:S(2)}, u32[]{:S(2)}) collective-permute-start(bf16[256,256]{1,0:T(8,128)(2,1)S(1)} %collective-permute-done.35.refs_3_), channel_id=1, source_target_pairs={{0,1},{1,0},{2,3},{3,2},{4,5},{5,4},{6,7},{7,6},{8,9},{9,8},{10,11... | collective-permute-start | bytes 393224 | tf_op jit(solution)/shard_map/ppermute | solution.py:486
  78.5 6.4 %collective-permute-start.13 = (bf16[256,256]{1,0:T(8,128)(2,1)S(1)}, bf16[256,256]{1,0:T(8,128)(2,1)S(1)}, u32[]{:S(2)}, u32[]{:S(2)}) collective-permute-start(bf16[256,256]{1,0:T(8,128)(2,1)S(1)} %get-tuple-element.57.refs_0_), channel_id=1, source_target_pairs={{0,1},{1,0},{2,3},{3,2},{4,5},{5,4},{6,7},{7,6},{8,9},{9,8},{10,11... | collective-permute-start | bytes 393224 | tf_op jit(solution)/shard_map/ppermute | solution.py:486
  79.0 9.0 %collective-permute-start.14 = (bf16[256,256]{1,0:T(8,128)(2,1)S(1)}, bf16[256,256]{1,0:T(8,128)(2,1)S(1)}, u32[]{:S(2)}, u32[]{:S(2)}) collective-permute-start(bf16[256,256]{1,0:T(8,128)(2,1)S(1)} %collective-permute-done.10.refs_1_), channel_id=1, source_target_pairs={{0,1},{1,0},{2,3},{3,2},{4,5},{5,4},{6,7},{7,6},{8,9},{9,8},{10,11... | collective-permute-start | bytes 393224 | tf_op jit(solution)/shard_map/ppermute | solution.py:486
  79.1 8.9 %collective-permute-start.15 = (bf16[256,256]{1,0:T(8,128)(2,1)S(1)}, bf16[256,256]{1,0:T(8,128)(2,1)S(1)}, u32[]{:S(2)}, u32[]{:S(2)}) collective-permute-start(bf16[256,256]{1,0:T(8,128)(2,1)S(1)} %collective-permute-done.11.refs_2_), channel_id=1, source_target_pairs={{0,1},{1,0},{2,3},{3,2},{4,5},{5,4},{6,7},{7,6},{8,9},{9,8},{10,11... | collective-permute-start | bytes 393224 | tf_op jit(solution)/shard_map/ppermute | solution.py:486
  79.5 8.5 %collective-permute-start.16 = (bf16[256,256]{1,0:T(8,128)(2,1)S(1)}, bf16[256,256]{1,0:T(8,128)(2,1)S(1)}, u32[]{:S(2)}, u32[]{:S(2)}) collective-permute-start(bf16[256,256]{1,0:T(8,128)(2,1)S(1)} %collective-permute-done.12.refs_3_), channel_id=1, source_target_pairs={{0,1},{1,0},{2,3},{3,2},{4,5},{5,4},{6,7},{7,6},{8,9},{9,8},{10,11... | collective-permute-start | bytes 393224 | tf_op jit(solution)/shard_map/ppermute | solution.py:486
  83.5 10.6 %collective-permute-start.40 = (bf16[4,2,96,128]{3,2,1,0:T(8,128)(2,1)S(1)}, bf16[4,2,96,128]{3,2,1,0:T(8,128)(2,1)S(1)}, u32[]{:S(2)}, u32[]{:S(2)}) collective-permute-start(bf16[4,2,96,128]{3,2,1,0:T(8,128)(2,1)S(1)} %get-tuple-element.78), channel_id=1, source_target_pairs={{0,8},{8,16},{16,24},{24,0},{1,9},{9,17},{17,25},{25,1},{2,10},{10... | collective-permute-start | bytes 589832 | tf_op jit(solution)/shard_map/ppermute | solution.py:490
  84.9 11.1 %collective-permute-start.41 = (bf16[4,2,96,128]{3,2,1,0:T(8,128)(2,1)S(1)}, bf16[4,2,96,128]{3,2,1,0:T(8,128)(2,1)S(1)}, u32[]{:S(2)}, u32[]{:S(2)}) collective-permute-start(bf16[4,2,96,128]{3,2,1,0:T(8,128)(2,1)S(1)} %get-tuple-element.79), channel_id=1, source_target_pairs={{0,16},{8,24},{16,0},{24,8},{1,17},{9,25},{17,1},{25,9},{2,18},{10... | collective-permute-start | bytes 589832 | tf_op jit(solution)/shard_map/ppermute | solution.py:490
  87.9 22.2 %copy-start.1 = (f32[2,2,96,128]{3,2,1,0:T(8,128)S(1)}, f32[2,2,96,128]{3,2,1,0:T(8,128)}, u32[]{:S(2)}) copy-start(f32[2,2,96,128]{3,2,1,0:T(8,128)} %v_ref.7) | copy-start | bytes 589828
  88.0 9.3 %collective-permute-start.42 = (bf16[4,2,96,128]{3,2,1,0:T(8,128)(2,1)S(1)}, bf16[4,2,96,128]{3,2,1,0:T(8,128)(2,1)S(1)}, u32[]{:S(2)}, u32[]{:S(2)}) collective-permute-start(bf16[4,2,96,128]{3,2,1,0:T(8,128)(2,1)S(1)} %get-tuple-element.80), channel_id=1, source_target_pairs={{0,24},{8,0},{16,8},{24,16},{1,25},{9,1},{17,9},{25,17},{2,26},{10... | collective-permute-start | bytes 589832 | tf_op jit(solution)/shard_map/ppermute | solution.py:490
  91.9 8.4 %collective-permute-start.17 = (bf16[4,2,96,128]{3,2,1,0:T(8,128)(2,1)S(1)}, bf16[4,2,96,128]{3,2,1,0:T(8,128)(2,1)S(1)}, u32[]{:S(2)}, u32[]{:S(2)}) collective-permute-start(bf16[4,2,96,128]{3,2,1,0:T(8,128)(2,1)S(1)} %get-tuple-element.59), channel_id=1, source_target_pairs={{0,8},{8,16},{16,24},{24,0},{1,9},{9,17},{17,25},{25,1},{2,10},{10... | collective-permute-start | bytes 589832 | tf_op jit(solution)/shard_map/ppermute | solution.py:490
  93.4 10.4 %collective-permute-start.18 = (bf16[4,2,96,128]{3,2,1,0:T(8,128)(2,1)S(1)}, bf16[4,2,96,128]{3,2,1,0:T(8,128)(2,1)S(1)}, u32[]{:S(2)}, u32[]{:S(2)}) collective-permute-start(bf16[4,2,96,128]{3,2,1,0:T(8,128)(2,1)S(1)} %get-tuple-element.60), channel_id=1, source_target_pairs={{0,16},{8,24},{16,0},{24,8},{1,17},{9,25},{17,1},{25,9},{2,18},{10... | collective-permute-start | bytes 589832 | tf_op jit(solution)/shard_map/ppermute | solution.py:490
  94.1 11.2 %collective-permute-start.19 = (bf16[4,2,96,128]{3,2,1,0:T(8,128)(2,1)S(1)}, bf16[4,2,96,128]{3,2,1,0:T(8,128)(2,1)S(1)}, u32[]{:S(2)}, u32[]{:S(2)}) collective-permute-start(bf16[4,2,96,128]{3,2,1,0:T(8,128)(2,1)S(1)} %get-tuple-element.61), channel_id=1, source_target_pairs={{0,24},{8,0},{16,8},{24,16},{1,25},{9,1},{17,9},{25,17},{2,26},{10... | collective-permute-start | bytes 589832 | tf_op jit(solution)/shard_map/ppermute | solution.py:490
  97.4 10.9 %collective-permute-start.43 = (f32[2,96,128]{2,1,0:T(8,128)S(1)}, f32[2,96,128]{2,1,0:T(8,128)S(1)}, u32[]{:S(2)}, u32[]{:S(2)}) collective-permute-start(f32[2,96,128]{2,1,0:T(8,128)S(1)} %get-tuple-element.82), channel_id=1, source_target_pairs={{0,32},{32,64},{64,96},{96,0},{1,33},{33,65},{65,97},{97,1},{2,34}... | collective-permute-start | bytes 294920 | tf_op jit(solution)/shard_map/ppermute | solution.py:490
  98.3 11.9 %collective-permute-start.44 = (f32[2,96,128]{2,1,0:T(8,128)S(1)}, f32[2,96,128]{2,1,0:T(8,128)S(1)}, u32[]{:S(2)}, u32[]{:S(2)}) collective-permute-start(f32[2,96,128]{2,1,0:T(8,128)S(1)} %get-tuple-element.83), channel_id=1, source_target_pairs={{0,64},{32,96},{64,0},{96,32},{1,65},{33,97},{65,1},{97,33},{2,66}... | collective-permute-start | bytes 294920 | tf_op jit(solution)/shard_map/ppermute | solution.py:490
  100.3 9.9 %collective-permute-start.45 = (f32[2,96,128]{2,1,0:T(8,128)S(1)}, f32[2,96,128]{2,1,0:T(8,128)S(1)}, u32[]{:S(2)}, u32[]{:S(2)}) collective-permute-start(f32[2,96,128]{2,1,0:T(8,128)S(1)} %get-tuple-element.84), channel_id=1, source_target_pairs={{0,96},{32,0},{64,32},{96,64},{1,97},{33,1},{65,33},{97,65},{2,98}... | collective-permute-start | bytes 294920 | tf_op jit(solution)/shard_map/ppermute | solution.py:490
  105.4 4.9 %collective-permute-start.20 = (f32[2,96,128]{2,1,0:T(8,128)S(1)}, f32[2,96,128]{2,1,0:T(8,128)S(1)}, u32[]{:S(2)}, u32[]{:S(2)}) collective-permute-start(f32[2,96,128]{2,1,0:T(8,128)S(1)} %get-tuple-element.63), channel_id=1, source_target_pairs={{0,32},{32,64},{64,96},{96,0},{1,33},{33,65},{65,97},{97,1},{2,34}... | collective-permute-start | bytes 294920 | tf_op jit(solution)/shard_map/ppermute | solution.py:490
  106.3 5.2 %collective-permute-start.21 = (f32[2,96,128]{2,1,0:T(8,128)S(1)}, f32[2,96,128]{2,1,0:T(8,128)S(1)}, u32[]{:S(2)}, u32[]{:S(2)}) collective-permute-start(f32[2,96,128]{2,1,0:T(8,128)S(1)} %get-tuple-element.64), channel_id=1, source_target_pairs={{0,64},{32,96},{64,0},{96,32},{1,65},{33,97},{65,1},{97,33},{2,66}... | collective-permute-start | bytes 294920 | tf_op jit(solution)/shard_map/ppermute | solution.py:490
  108.3 3.8 %collective-permute-start.22 = (f32[2,96,128]{2,1,0:T(8,128)S(1)}, f32[2,96,128]{2,1,0:T(8,128)S(1)}, u32[]{:S(2)}, u32[]{:S(2)}) collective-permute-start(f32[2,96,128]{2,1,0:T(8,128)S(1)} %get-tuple-element.65), channel_id=1, source_target_pairs={{0,96},{32,0},{64,32},{96,64},{1,97},{33,1},{65,33},{97,65},{2,98}... | collective-permute-start | bytes 294920 | tf_op jit(solution)/shard_map/ppermute | solution.py:490
  (2 other events, 3.8 us)
